TPU v7x, 8 devices: a whole 2x2x1 slice. The times are simulated.
8 devices in a mesh: dp: 2 (over z, y), tp: 4 (over x, core).
Axes of the slice: x: 2, y: 2, z: 1, core: 2. Of those that a mesh axis runs over, the one named last changes fastest.
Arguments:
- residual: float32 [512, 2560], P('dp'), parts along dimension 0
- norm_w: bfloat16 [2, 2560], replicated
- w_in: bfloat16 [2, 2560, 2, 5120], P(None, None, None, 'tp')
- conv_w: bfloat16 [2, 4, 5120], P(None, None, 'tp')
- conv_b: bfloat16 [2, 5120], P(None, 'tp')
- w_x: bfloat16 [2, 5120, 192], P(None, 'tp')
- w_dt: bfloat16 [2, 160, 5120], P(None, None, 'tp')
- b_dt: float32 [2, 5120], P(None, 'tp')
- a_log: float32 [2, 16, 5120], P(None, None, 'tp')
- d_skip: float32 [2, 5120], P(None, 'tp')
- w_out: bfloat16 [2, 5120, 2560], P(None, 'tp')
- conv_state: bfloat16 [2, 512, 3, 5120], P(None, 'dp', None, 'tp'), parts along dimension 1
- ssm_state: float32 [2, 512, 16, 5120], P(None, 'dp', None, 'tp'), parts along dimension 1
Outputs:
- output 1: float32 [512, 2560], P('dp'), parts along dimension 0
- output 2: bfloat16 [2, 512, 3, 5120], P(None, 'dp', None, 'tp'), parts along dimension 1
- output 3: float32 [2, 512, 16, 5120], P(None, 'dp', None, 'tp'), parts along dimension 1
There are 2 independent parts. A program takes and returns all parts, laid end to end along the dimension named above; an argument that names none is the same for every part.
All inputs are finite; a program needn't handle non-finite values.
Results may differ from a plain program's by a relative error of at most 0.0173252.
Values are sent between devices in bfloat16 or wider.
A program may use at most 1 GiB of HBM per device.

v0:
```python
import jax
import jax.numpy as jnp
from jax import lax
from jax.sharding import PartitionSpec as P


def rms_norm(vector, epsilon):
    return vector * lax.rsqrt(jnp.mean(vector * vector, axis=-1, keepdims=True) + epsilon)


def solution(mesh):
    def device_step(residual, norm_w, w_in, conv_w, conv_b, w_x, w_dt, b_dt, a_log, d_skip, w_out, conv_state, ssm_state):
        rank_dim = w_dt.shape[1]
        state_dim = a_log.shape[1]
        conv_list = []
        ssm_list = []
        for layer_idx in range(norm_w.shape[0]):
            hidden = (rms_norm(residual, 1e-5) * norm_w[layer_idx].astype(jnp.float32)).astype(jnp.bfloat16)
            xz_val = jnp.einsum('bd,dwe->bwe', hidden, w_in[layer_idx], preferred_element_type=jnp.float32).astype(jnp.bfloat16)
            window = jnp.concatenate([conv_state[layer_idx], xz_val[:, 0:1, :]], axis=1)
            conv_pre = jnp.sum(window.astype(jnp.float32) * conv_w[layer_idx].astype(jnp.float32), axis=1) + conv_b[layer_idx].astype(jnp.float32)
            x_conv = jax.nn.silu(conv_pre).astype(jnp.bfloat16)
            proj_part = jnp.dot(x_conv, w_x[layer_idx], preferred_element_type=jnp.float32).astype(jnp.bfloat16)
            proj_sum = lax.psum(proj_part, 'tp').astype(jnp.float32)
            dt_low = rms_norm(proj_sum[:, :rank_dim], 1e-6).astype(jnp.bfloat16)
            b_vec = rms_norm(proj_sum[:, rank_dim:rank_dim + state_dim], 1e-6)
            c_vec = rms_norm(proj_sum[:, rank_dim + state_dim:], 1e-6)
            dt_val = jax.nn.softplus(jnp.dot(dt_low, w_dt[layer_idx], preferred_element_type=jnp.float32) + b_dt[layer_idx])
            x_float = x_conv.astype(jnp.float32)
            decay_fac = jnp.exp(dt_val[:, None, :] * -jnp.exp(a_log[layer_idx]))
            new_ssm = decay_fac * ssm_state[layer_idx] + (dt_val * x_float)[:, None, :] * b_vec[:, :, None]
            y_val = jnp.sum(new_ssm * c_vec[:, :, None], axis=1) + d_skip[layer_idx] * x_float
            gated_y = (y_val * jax.nn.silu(xz_val[:, 1, :].astype(jnp.float32))).astype(jnp.bfloat16)
            out_part = jnp.dot(gated_y, w_out[layer_idx], preferred_element_type=jnp.float32).astype(jnp.bfloat16)
            residual = residual + lax.psum(out_part, 'tp').astype(jnp.float32)
            conv_list.append(window[:, 1:, :])
            ssm_list.append(new_ssm)
        return residual, jnp.stack(conv_list), jnp.stack(ssm_list)

    cache_spec = P(None, 'dp', None, 'tp')
    in_specs = (P('dp', None), P(None, None), P(None, None, None, 'tp'), P(None, None, 'tp'), P(None, 'tp'), P(None, 'tp', None), P(None, None, 'tp'), P(None, 'tp'), P(None, None, 'tp'), P(None, 'tp'), P(None, 'tp', None), cache_spec, cache_spec)
    out_specs = (P('dp', None), cache_spec, cache_spec)
    return jax.shard_map(device_step, mesh=mesh, in_specs=in_specs, out_specs=out_specs, check_vma=False)
```

profile of v0, /device:TPU:0, one launch (start us, length us, event | category | flops | bytes accessed | tf_op | source)
XLA Modules:
  0.0 276.6 jit_solution(158282934577210316)
XLA Ops:
  7.2 0.0 all-reduce.5.cloned.1.call-start
  7.2 2.0 multiply_reduce_fusion.3
  9.3 0.7 convert_reduce_fusion.1
  10.0 3.7 %slice_bitcast_fusion = (bf16[256,3,1280]{2,0,1:T(8,128)(2,1)}, bf16[256,3,1280]{2,0,1:T(8,128)(2,1)S(1)}) fusion(bf16[2,256,3,1280]{3,1,2,0:T(8,128)(2,1)} %param.24), kind=kLoop, calls=%fused_computation.48 | loop fusion | bytes 7864320 | tf_op jit(solution)/shard_map/squeeze | solution.py:20
  13.6 21.6 %fusion.64 = (bf16[1,2560,2,1280]{3,2,1,0:T(2,128)(2,1)S(1)}, bf16[1,2560,2,1280]{3,2,1,0:T(2,128)(2,1)}) fusion(bf16[2,2560,2,1280]{3,2,1,0:T(2,128)(2,1)} %param.15), kind=kLoop, calls=%fused_computation.132 | loop fusion | bytes 52428800 | tf_op jit(solution)/shard_map/slice | solution.py:19
  35.2 3.6 %fusion.20 = bf16[256,2,1280]{2,0,1:T(8,128)(2,1)S(1)} fusion(bf16[1,2560,2,1280]{3,2,1,0:T(2,128)(2,1)S(1)} %get-tuple-element.17, f32[256,2560]{1,0:T(8,128)S(1)} %copy-done, f32[2560]{0:T(1024)S(1)} %get-tuple-element.11, f32[256]{0:T(256)S(1)} %add_rsqrt_fusion.7), kind=kOutput, calls=%fused_computation.32 | convolution fusion | flops 3358064640 | bytes 17050624 | tf_op jit(solution)/shard_map/bd,dwe->bwe/dot_general | solution.py:19
  38.9 0.5 multiply_reduce_fusion.1
  39.4 0.4 copy-done.20
  39.9 1.1 copy-done.5
  41.0 0.4 multiply_convert_fusion.5
  41.4 0.9 copy-done.15
  42.3 1.0 convolution_convert_fusion.1
  43.3 0.0 all-reduce.7.cloned.1.call-start
  43.4 0.6 slice_reduce_fusion.1
  44.0 1.6 negate_bitcast_fusion
  45.6 0.6 slice_reduce_fusion
  46.2 26.1 %all-reduce.5.cloned.1.call-done = bf16[256,192]{0,1:T(8,128)(2,1)} async-done(((bf16[256,192]{0,1:T(8,128)(2,1)}), bf16[256,192]{0,1:T(8,128)(2,1)}) %all-reduce.5.cloned.1.call-update) | async-done | bytes 98320 | tf_op jit(solution)/shard_map/psum | solution.py:24
  72.4 0.9 convert_element_type.133
  73.4 0.6 copy-done.12
  73.9 0.1 copy.17
  74.0 0.8 copy.18
  74.8 2.3 convert_multiply_fusion.3
  77.2 17.1 %fusion.5 = f32[256,1280]{1,0:T(8,128)S(1)} fusion(f32[2,256,16,1280]{3,2,1,0:T(8,128)} %param.25, f32[256,16]{1,0:T(8,128)S(1)} %copy-done.17, f32[256,16]{1,0:T(8,128)S(1)} %copy.17, f32[256,1280]{1,0:T(8,128)S(1)} %get-tuple-element.29, f32[16,1280]{1,0:T(8,128)S(1)} %copy-done.13, f32[256,1280]{1,0:T(8,128)S(1)} %get-tuple-element.30), kind=kLoop, calls=%fused_computation.8 | loop fusion | flops 31129600 | bytes 25018368 | tf_op jit(solution)/shard_map/reduce_sum | solution.py:32
  94.4 6.3 %fusion.14 = bf16[256,2560]{1,0:T(8,128)(2,1)} fusion(bf16[2,1280,2560]{2,1,0:T(8,128)(2,1)} %param.23, f32[256,1280]{1,0:T(8,128)S(1)} %fusion.5, f32[256,1280]{1,0:T(8,128)S(1)} %copy-done.6, bf16[256,2,1280]{2,0,1:T(8,128)(2,1)S(1)} %copy-done.21, f32[1280]{0:T(1024)S(1)} %copy-done.24, f32[1280]{0:T(1024)S(1)} %copy-done.32), kind=kOutput, calls=%fused_computation.26 | convolution fusion | flops 1683619840 | bytes 11157504 | tf_op jit(solution)/shard_map/dot_general | solution.py:34
  100.7 0.2 all-reduce.9.cloned.1.call-start
  100.9 2.8 %fusion.25 = bf16[1,256,3,1280]{3,1,2,0:T(8,128)(2,1)} fusion(bf16[256,3,1280]{2,0,1:T(8,128)(2,1)} %copy-done.2, bf16[256,1,1280]{2,0,1:T(8,128)(2,1)S(1)} %slice.150), kind=kLoop, calls=%fused_computation.47 | loop fusion | flops 983040 | bytes 4587520 | tf_op jit(solution)/shard_map/stack | solution.py:38
  103.7 30.9 %all-reduce.7.cloned.1.call-done = bf16[256,2560]{1,0:T(8,128)(2,1)} async-done(((bf16[256,2560]{1,0:T(8,128)(2,1)}), bf16[256,2560]{1,0:T(8,128)(2,1)}) %all-reduce.7.cloned.1.call-update) | async-done | bytes 1310736 | tf_op jit(solution)/shard_map/psum | solution.py:35
  134.6 1.8 multiply_reduce_fusion.2
  136.5 8.5 %fusion.21 = bf16[256,2,1280]{2,0,1:T(8,128)(2,1)S(1)} fusion(bf16[1,2560,2,1280]{3,2,1,0:T(2,128)(2,1)} %get-tuple-element.18, f32[2560]{0:T(1024)S(1)} %copy-done.27, f32[256]{0:T(256)S(1)} %add_rsqrt_fusion.3, f32[256,2560]{1,0:T(8,128)S(1)} %copy-done, bf16[256,2560]{1,0:T(8,128)(2,1)S(1)} %copy-done.7), kind=kOutput, calls=%fused_computation.33 | convolution fusion | flops 3359375360 | bytes 18361344 | tf_op jit(solution)/shard_map/bd,dwe->bwe/dot_general | solution.py:19
  145.0 1.6 fusion.23
  146.7 0.5 multiply_reduce_fusion
  147.2 1.0 copy-done.3
  148.3 0.4 multiply_convert_fusion.3
  148.7 0.2 copy-done.34
  148.9 1.0 convolution_convert_fusion
  150.0 0.0 all-reduce.11.cloned.1.call-start
  150.0 4.4 %pad_maximum_fusion.1 = bf16[2,256,3,1280]{3,1,2,0:T(8,128)(2,1)} fusion(bf16[1,256,3,1280]{3,1,2,0:T(8,128)(2,1)} %fusion.23, bf16[1,256,3,1280]{3,1,2,0:T(8,128)(2,1)} %fusion.25), kind=kLoop, calls=%fused_computation.23 | loop fusion | flops 1966080 | bytes 7864320 | tf_op jit(solution)/shard_map/stack | solution.py:38
  154.4 21.7 %all-reduce.9.cloned.1.call-done = bf16[256,192]{0,1:T(8,128)(2,1)} async-done(((bf16[256,192]{0,1:T(8,128)(2,1)}), bf16[256,192]{0,1:T(8,128)(2,1)}) %all-reduce.9.cloned.1.call-update) | async-done | bytes 98320 | tf_op jit(solution)/shard_map/psum | solution.py:24
  176.1 0.9 convert_element_type.148
  177.2 0.1 copy.20
  177.3 0.1 copy.21
  177.4 2.4 convert_multiply_fusion.2
  179.8 30.1 %multiply_add_fusion.1 = (f32[1,256,16,1280]{3,2,1,0:T(8,128)}, f32[1,256,16,1280]{3,2,1,0:T(8,128)}) fusion(f32[2,256,16,1280]{3,2,1,0:T(8,128)} %param.25, f32[256,16]{1,0:T(8,128)S(1)} %copy.17, f32[256,1280]{1,0:T(8,128)S(1)} %copy-done.9, f32[16,1280]{1,0:T(8,128)S(1)} %copy-done.14, f32[256,1280]{1,0:T(8,128)S(1)} %copy-done.11, ...), kind=kLoop, calls=%fused_computation.10 | loop fusion | flops 41943040 | bytes 89325568 | tf_op jit(solution)/shard_map/add | solution.py:31
  210.0 16.3 %fusion.2 = f32[256,1280]{1,0:T(8,128)S(1)} fusion(f32[2,256,16,1280]{3,2,1,0:T(8,128)} %param.25, f32[256,16]{1,0:T(8,128)S(1)} %copy.21, f32[256,16]{1,0:T(8,128)S(1)} %copy.20, f32[256,1280]{1,0:T(8,128)S(1)} %get-tuple-element.31, f32[16,1280]{1,0:T(8,128)S(1)} %get-tuple-element.25, f32[256,1280]{1,0:T(8,128)S(1)} %get-tuple-element.32), kind=kLoop, calls=%fused_computation.4 | loop fusion | flops 31129600 | bytes 25018368 | tf_op jit(solution)/shard_map/reduce_sum | solution.py:32
  226.3 6.3 %fusion.17 = bf16[256,2560]{1,0:T(8,128)(2,1)} fusion(bf16[2,1280,2560]{2,1,0:T(8,128)(2,1)} %param.23, f32[256,1280]{1,0:T(8,128)S(1)} %fusion.2, f32[256,1280]{1,0:T(8,128)S(1)} %copy-done.4, bf16[256,2,1280]{2,0,1:T(8,128)(2,1)S(1)} %copy-done.19, f32[1280]{0:T(1024)S(1)} %get-tuple-element.13, f32[1280]{0:T(1024)S(1)} %copy-done.30), kind=kOutput, calls=%fused_computation.27 | convolution fusion | flops 1683619840 | bytes 11157504 | tf_op jit(solution)/shard_map/dot_general | solution.py:34
  232.6 29.1 %pad_maximum_fusion = f32[2,256,16,1280]{3,2,1,0:T(8,128)} fusion(f32[1,256,16,1280]{3,2,1,0:T(8,128)} %get-tuple-element.16, f32[1,256,16,1280]{3,2,1,0:T(8,128)} %get-tuple-element.15), kind=kLoop, calls=%fused_computation | loop fusion | flops 10485760 | bytes 83886080 | tf_op jit(solution)/shard_map/stack | solution.py:38
  261.7 4.8 %all-reduce.11.cloned.1.call-done = bf16[256,2560]{1,0:T(8,128)(2,1)} async-done(((bf16[256,2560]{1,0:T(8,128)(2,1)}), bf16[256,2560]{1,0:T(8,128)(2,1)}) %all-reduce.11.cloned.1.call-update) | async-done | bytes 1310736 | tf_op jit(solution)/shard_map/psum | solution.py:35
  266.5 3.6 %convert_add_fusion = f32[256,2560]{1,0:T(8,128)} fusion(bf16[256,2560]{1,0:T(8,128)(2,1)} %all-reduce.11.cloned.1.call-done, f32[256,2560]{1,0:T(8,128)S(1)} %copy-done, bf16[256,2560]{1,0:T(8,128)(2,1)} %all-reduce.7.cloned.1.call-done), kind=kLoop, calls=%fused_computation.38 | loop fusion | flops 2621440 | bytes 7864320 | tf_op jit(solution)/shard_map/add | solution.py:35
  (85 shorter events, 0.5 us)
Async XLA Ops:
  7.2 2.1 copy-start.25
  7.2 2.1 copy-start.22
  7.2 2.8 %copy-start.26 = (bf16[2,4,1280]{2,1,0:T(4,128)(2,1)S(1)}, bf16[2,4,1280]{2,1,0:T(4,128)(2,1)}, u32[]{:S(2)}) copy-start(bf16[2,4,1280]{2,1,0:T(4,128)(2,1)} %param.16) | copy-start | bytes 61444
  7.2 65.2 %all-reduce.5.cloned.1.call-start = ((), (), s32[]{:S(2)}) async-start(), calls=%async_computation | async-start | bytes 196608 | tf_op jit(solution)/shard_map/psum | solution.py:24
  9.3 30.6 %copy-start.23 = (f32[1280]{0:T(1024)}, f32[1280]{0:T(1024)S(1)}, u32[]{:S(2)}) copy-start(f32[1280]{0:T(1024)S(1)} %get-tuple-element.14) | copy-start | bytes 15364
  13.6 25.2 %copy-start.2 = (bf16[256,3,1280]{2,0,1:T(8,128)(2,1)}, bf16[256,3,1280]{2,0,1:T(8,128)(2,1)S(1)}, u32[]{:S(2)}) copy-start(bf16[256,3,1280]{2,0,1:T(8,128)(2,1)S(1)} %get-tuple-element.20) | copy-start | bytes 5898244
  13.6 21.6 %copy-start = (f32[256,2560]{1,0:T(8,128)S(1)}, f32[256,2560]{1,0:T(8,128)}, u32[]{:S(2)}) copy-start(f32[256,2560]{1,0:T(8,128)} %param.13) | copy-start | bytes 7864324
  38.8 1.1 copy-start.20
  39.9 1.1 copy-start.5
  39.9 2.4 copy-start.33
  39.9 3.5 %copy-start.28 = (f32[2,1280]{1,0:T(2,128)S(1)}, f32[2,1280]{1,0:T(2,128)}, u32[]{:S(2)}) copy-start(f32[2,1280]{1,0:T(2,128)} %param.20) | copy-start | bytes 30724
  39.9 5.7 %copy-start.29 = (f32[2,1280]{1,0:T(2,128)S(1)}, f32[2,1280]{1,0:T(2,128)}, u32[]{:S(2)}) copy-start(f32[2,1280]{1,0:T(2,128)} %param.22) | copy-start | bytes 30724
  41.4 0.9 copy-start.15
  43.3 91.3 %all-reduce.7.cloned.1.call-start = ((), (), s32[]{:S(2)}) async-start(), calls=%async_computation.1 | async-start | bytes 2621440 | tf_op jit(solution)/shard_map/psum | solution.py:35
  73.3 0.7 copy-start.12
  74.8 2.4 copy-start.13
  74.8 2.4 copy-start.17
  77.1 17.2 %copy-start.8 = (f32[256,1280]{1,0:T(8,128)}, f32[256,1280]{1,0:T(8,128)S(1)}, u32[]{:S(2)}) copy-start(f32[256,1280]{1,0:T(8,128)S(1)} %get-tuple-element.29) | copy-start | bytes 3932164
  77.2 17.2 %copy-start.10 = (f32[256,1280]{1,0:T(8,128)}, f32[256,1280]{1,0:T(8,128)S(1)}, u32[]{:S(2)}) copy-start(f32[256,1280]{1,0:T(8,128)S(1)} %get-tuple-element.30) | copy-start | bytes 3932164
  77.2 17.2 %copy-start.6 = (f32[256,1280]{1,0:T(8,128)S(1)}, f32[256,1280]{1,0:T(8,128)}, u32[]{:S(2)}) copy-start(f32[256,1280]{1,0:T(8,128)} %copy-done.5) | copy-start | bytes 3932164
  77.2 17.2 %copy-start.21 = (bf16[256,2,1280]{2,0,1:T(8,128)(2,1)S(1)}, bf16[256,2,1280]{2,0,1:T(8,128)(2,1)}, u32[]{:S(2)}) copy-start(bf16[256,2,1280]{2,0,1:T(8,128)(2,1)} %copy-done.20) | copy-start | bytes 3932164
  77.2 17.2 %copy-start.24 = (f32[1280]{0:T(1024)S(1)}, f32[1280]{0:T(1024)}, u32[]{:S(2)}) copy-start(f32[1280]{0:T(1024)} %copy-done.23) | copy-start | bytes 15364
  77.2 17.2 %copy-start.32 = (f32[1280]{0:T(1024)S(1)}, f32[1280]{0:T(1024)}, u32[]{:S(2)}) copy-start(f32[1280]{0:T(1024)} %get-tuple-element.8) | copy-start | bytes 15364
  100.7 75.5 %all-reduce.9.cloned.1.call-start = ((), (), s32[]{:S(2)}) async-start(), calls=%async_computation.2 | async-start | bytes 196608 | tf_op jit(solution)/shard_map/psum | solution.py:24
  103.7 32.7 %copy-start.27 = (f32[2560]{0:T(1024)S(1)}, f32[2560]{0:T(1024)}, u32[]{:S(2)}) copy-start(f32[2560]{0:T(1024)} %get-tuple-element.12) | copy-start | bytes 30724
  134.6 1.9 copy-start.7
  136.4 8.6 %copy-start.1 = (bf16[256,3,1280]{2,0,1:T(8,128)(2,1)S(1)}, bf16[256,3,1280]{2,0,1:T(8,128)(2,1)}, u32[]{:S(2)}) copy-start(bf16[256,3,1280]{2,0,1:T(8,128)(2,1)} %get-tuple-element.19) | copy-start | bytes 5898244
  145.0 1.7 copy-start.18
  147.2 1.1 copy-start.3
  147.2 1.7 copy-start.34
  148.9 5.5 %copy-start.16 = (bf16[256,1280]{1,0:T(8,128)(2,1)}, bf16[256,1280]{1,0:T(8,128)(2,1)S(1)}, u32[]{:S(2)}) copy-start(bf16[256,1280]{1,0:T(8,128)(2,1)S(1)} %multiply_convert_fusion.3) | copy-start | bytes 1966084
  149.9 27.4 %copy-start.31 = (f32[1280]{0:T(1024)S(1)}, f32[1280]{0:T(1024)}, u32[]{:S(2)}) copy-start(f32[1280]{0:T(1024)} %get-tuple-element.9) | copy-start | bytes 15364
  150.0 116.5 %all-reduce.11.cloned.1.call-start = ((), (), s32[]{:S(2)}) async-start(), calls=%async_computation.3 | async-start | bytes 2621440 | tf_op jit(solution)/shard_map/psum | solution.py:35
  177.4 2.4 copy-start.9
  177.4 2.4 copy-start.11
  177.4 2.4 copy-start.14
  210.0 16.3 %copy-start.4 = (f32[256,1280]{1,0:T(8,128)S(1)}, f32[256,1280]{1,0:T(8,128)}, u32[]{:S(2)}) copy-start(f32[256,1280]{1,0:T(8,128)} %copy-done.3) | copy-start | bytes 3932164
  210.0 16.3 %copy-start.19 = (bf16[256,2,1280]{2,0,1:T(8,128)(2,1)S(1)}, bf16[256,2,1280]{2,0,1:T(8,128)(2,1)}, u32[]{:S(2)}) copy-start(bf16[256,2,1280]{2,0,1:T(8,128)(2,1)} %copy-done.18) | copy-start | bytes 3932164
  210.0 16.3 %copy-start.30 = (f32[1280]{0:T(1024)S(1)}, f32[1280]{0:T(1024)}, u32[]{:S(2)}) copy-start(f32[1280]{0:T(1024)} %get-tuple-element.7) | copy-start | bytes 15364
Sparse Core Ops, SparseCore 0:
  43.4 28.8 all-reduce.4
  100.8 33.7 all-reduce.6
  150.1 26.0 all-reduce.8
  232.7 33.7 all-reduce.10
where the time goes:
time: 277 us
  other arithmetic  115 us (42%)
  waiting for transfers between devices  83.6 us (30%)
  local copies, waits for them, and re-layouts  31.9 us (12%)
  matrix products  31.4 us (11%)
  between operations  14.3 us (5%)
    psum x2, waiting for transfers between devices, device_step(): proj_sum = lax.psum(proj_part, 'tp').astype(jnp.float32)  47.9 us
    another operation x4, other arithmetic, device_step(): return (residual, jnp.stack(conv_list), jnp.stack(ssm_list))  37.9 us
    psum x2, waiting for transfers between devices, device_step(): residual = residual + lax.psum(out_part, 'tp').astype(jnp.float32)  35.7 us
    reduce_sum x2, other arithmetic, device_step(): jnp.sum(new_ssm * c_vec[:, :, None], axis=1) + d_skip[layer_idx] * x_float  33.4 us
    add x1, other arithmetic, device_step(): decay_fac * ssm_state[layer_idx]  30.1 us
    slice x1, local copies, waits for them, and re-layouts, device_step(): w_in[layer_idx]  21.6 us
    dot_general x2, matrix products, device_step(): jnp.dot(gated_y, w_out[layer_idx], preferred_element_type=jnp.float32)  12.5 us
    dot_general x2, matrix products, device_step(): jnp.einsum('bd,dwe->bwe', hidden, w_in[layer_idx], preferred_element_type...  12.1 us
  transfers between devices with their start and end apart: 4, of which 4 were waited for; matrix products, arithmetic and copies ran while one was open for 14% of the time, Pallas kernels for 0%

commit v1 on v0

v1 whole, which is shorter than its diff:
```python
import functools
import math

import jax
import jax.numpy as jnp
from jax import lax
from jax.experimental import pallas as pl
from jax.experimental.pallas import tpu as pltpu
from jax.sharding import PartitionSpec as P

F32 = jnp.float32
BF16 = jnp.bfloat16
ANY = pl.BlockSpec(memory_space=pl.ANY)
VMEM = pl.BlockSpec(memory_space=pltpu.VMEM)
NCH = 256
SB = 16
LOG2E = math.log2(math.e)
VLIM = 62 * 2 ** 20


def silu(v):
    return v * jax.nn.sigmoid(v)


def expand_matrix():
    row = lax.broadcasted_iota(jnp.int32, (128, 512), 0)
    col = lax.broadcasted_iota(jnp.int32, (128, 512), 1)
    target = 2 * row + jnp.where(col < 256, 0, 257)
    return jnp.where(col == target, 1.0, 0.0).astype(BF16)


def in_kernel(layer, row0, rows, has_o, *refs):
    refs = list(refs)
    res_hbm = refs.pop(0)
    pieces = [refs.pop(0) for _ in range(4)] if has_o else None
    norm_w, w_in, conv_w, conv_b, w_x, conv_st = refs[:6]
    refs = refs[6:]
    if layer > 0 or row0 > 0:
        refs.pop(0)
    z_out, xc_out, p_out, conv_out = refs[:4]
    refs = refs[4:]
    r_out = refs.pop(0) if has_o else None
    wbuf, hx, rbuf, cbuf, xbuf, rsem, wsem, csem, osem = refs
    feat = rbuf.shape[1]
    nchunk = wbuf.shape[0]
    w_flat = w_in.reshape(w_in.shape[0], 2 * feat, w_in.shape[3])

    r_rows = rows if res_hbm.shape[0] == rows else res_hbm.shape[0]
    r_src = res_hbm if r_rows == rows else res_hbm.at[pl.ds(row0, rows)]
    r_copy = pltpu.make_async_copy(r_src, rbuf, rsem)
    r_copy.start()

    def w_copy(c):
        return pltpu.make_async_copy(w_flat.at[layer, :, pl.ds(c * NCH, NCH)], wbuf.at[c], wsem.at[c])

    w_copy(0).start()
    c_copy = pltpu.make_async_copy(conv_st.at[layer, :, pl.ds(row0, rows)], cbuf, csem)
    c_copy.start()
    for c in range(1, nchunk):
        w_copy(c).start()
    r_copy.wait()
    r = rbuf[...]
    if has_o:
        core = lax.rem(lax.axis_index('tp'), 2)
        half = feat // 2
        u, up, v, vp = pieces
        lo = pl.ds(pl.multiple_of(core * half, 128), half)
        hi = pl.ds(pl.multiple_of((1 - core) * half, 128), half)
        rbuf[:, lo] = rbuf[:, lo] + (u[...].astype(F32) + v[...].astype(F32))
        rbuf[:, hi] = rbuf[:, hi] + (up[...].astype(F32) + vp[...].astype(F32))
        pltpu.make_async_copy(rbuf, r_out, osem.at[0]).start()
        r = rbuf[...]
    inv = lax.rsqrt(jnp.mean(r * r, axis=-1, keepdims=True) + 1e-5)
    h = (r * inv * norm_w[layer:layer + 1, :].astype(F32)).astype(BF16)
    ex = expand_matrix()
    for j in range(feat // 128):
        e = jnp.dot(h[:, j * 128:(j + 1) * 128], ex, preferred_element_type=F32).astype(BF16)
        hx[0:rows, j * 256:(j + 1) * 256] = e[:, :256]
        hx[rows:2 * rows, j * 256:(j + 1) * 256] = e[:, 256:]
    c_copy.wait()
    pltpu.make_async_copy(cbuf.at[pl.ds(1, 2)], conv_out.at[layer, pl.ds(0, 2), pl.ds(row0, rows)], osem.at[1]).start()
    p_acc = jnp.zeros((rows, w_x.shape[1]), F32)
    for c in range(nchunk):
        w_copy(c).wait()
        sl = slice(c * NCH, (c + 1) * NCH)
        acc = jnp.dot(hx[...], wbuf[c], preferred_element_type=F32)
        x = acc[:rows].astype(BF16)
        z_out[:, sl] = acc[rows:].astype(BF16)
        xbuf[:, sl] = x
        cw = conv_w[layer, :, sl].astype(F32)
        pre = cbuf[0, :, sl].astype(F32) * cw[0:1] + cbuf[1, :, sl].astype(F32) * cw[1:2]
        pre = pre + cbuf[2, :, sl].astype(F32) * cw[2:3] + x.astype(F32) * cw[3:4]
        pre = pre + conv_b[layer:layer + 1, sl].astype(F32)
        xc = silu(pre).astype(BF16)
        xc_out[:, sl] = xc
        p_acc = p_acc + lax.dot_general(xc, w_x[layer, :, sl], (((1,), (1,)), ((), ())), preferred_element_type=F32)
    p_out[...] = p_acc.astype(BF16)
    x_copy = pltpu.make_async_copy(xbuf, conv_out.at[layer, 2, pl.ds(row0, rows)], osem.at[2])
    x_copy.start()
    x_copy.wait()
    pltpu.make_async_copy(cbuf.at[pl.ds(1, 2)], conv_out.at[layer, pl.ds(0, 2), pl.ds(row0, rows)], osem.at[1]).wait()
    if has_o:
        pltpu.make_async_copy(rbuf, r_out, osem.at[0]).wait()


def in_call(layer, row0, rows, residual, pieces, weights, conv_st, conv_prev):
    norm_w, w_in, conv_w, conv_b, w_x = weights
    has_o = pieces is not None
    feat = residual.shape[1]
    chan = w_in.shape[3]
    args = [residual] + (list(pieces) if has_o else []) + [norm_w, w_in, conv_w, conv_b, w_x, conv_st]
    specs = [ANY] + ([VMEM] * 4 if has_o else []) + [VMEM, ANY, VMEM, VMEM, VMEM, ANY]
    alias = {}
    if layer > 0 or row0 > 0:
        alias = {len(args): 3}
        args.append(conv_prev)
        specs.append(ANY)
    outs = [jax.ShapeDtypeStruct((rows, chan), BF16), jax.ShapeDtypeStruct((rows, chan), BF16),
            jax.ShapeDtypeStruct((rows, w_x.shape[1]), BF16), jax.ShapeDtypeStruct(conv_st.shape, BF16)]
    out_specs = [VMEM, VMEM, VMEM, ANY]
    if has_o:
        outs.append(jax.ShapeDtypeStruct((rows, feat), F32))
        out_specs.append(ANY)
    nchunk = chan // NCH
    return pl.pallas_call(
        functools.partial(in_kernel, layer, row0, rows, has_o),
        out_shape=outs, in_specs=specs, out_specs=out_specs, input_output_aliases=alias,
        scratch_shapes=[
            pltpu.VMEM((nchunk, 2 * feat, NCH), BF16),
            pltpu.VMEM((2 * rows, 2 * feat), BF16),
            pltpu.VMEM((rows, feat), F32),
            pltpu.VMEM((3, rows, chan), BF16),
            pltpu.VMEM((rows, chan), BF16),
            pltpu.SemaphoreType.DMA, pltpu.SemaphoreType.DMA((nchunk,)), pltpu.SemaphoreType.DMA,
            pltpu.SemaphoreType.DMA((3,)),
        ],
        compiler_params=pltpu.CompilerParams(vmem_limit_bytes=VLIM),
        cost_estimate=pl.CostEstimate(flops=rows * 2 * feat * 2 * chan * 2, bytes_accessed=20 * 2 ** 20, transcendentals=0),
        name=f"in{layer}r{row0}",
    )(*args)


def rms(v):
    return v * lax.rsqrt(jnp.mean(v * v, axis=-1, keepdims=True) + 1e-6)


def sublane_sums(parts):
    sub = lax.broadcasted_iota(jnp.int32, parts[0].shape, 0)
    for step in (4, 2, 1):
        keep = (sub & step) == 0
        half = len(parts) // 2
        parts = [jnp.where(keep, parts[k], parts[k + half])
                 + pltpu.roll(jnp.where(keep, parts[k + half], parts[k]), step, 0) if step == 4 else
                 jnp.where(keep, parts[k], parts[k + half])
                 + jnp.where(keep, pltpu.roll(parts[k], 8 - step, 0), pltpu.roll(parts[k + half], step, 0))
                 for k in range(half)]
    return parts[0]


def s_kernel(layer, row0, rows, aliased, *refs):
    (st, p0, p1, p2, p3, xc_ref, z_ref, w_dt, b_dt, a_log, d_skip, w_out) = refs[:12]
    refs = list(refs[12:])
    if aliased:
        refs.pop(0)
    st_out, mine, theirs = refs[:3]
    dt_s, dtx_s, bc_s, a_s, y_s, part, wo, wsem = refs[3:]
    step = pl.program_id(0)
    chan = dt_s.shape[1]
    rank = w_dt.shape[1]
    nst = a_s.shape[0]
    w_copy = pltpu.make_async_copy(w_out.at[layer], wo, wsem)

    @pl.when(step == 0)
    def _():
        w_copy.start()
        p = (p0[...].astype(F32) + p1[...].astype(F32)) + (p2[...].astype(F32) + p3[...].astype(F32))
        low = rms(p[:, :rank]).astype(BF16)
        pre = jnp.dot(low, w_dt[0], preferred_element_type=F32) + b_dt[layer:layer + 1, :]
        dt = jnp.maximum(pre, 0.0) + jnp.log1p(jnp.exp(-jnp.abs(pre)))
        dt_s[...] = dt
        dtx_s[...] = dt * xc_ref[...].astype(F32)
        bc_s[:, 0:nst] = rms(p[:, rank:rank + nst])
        bc_s[:, nst:2 * nst] = rms(p[:, rank + nst:])
        a_s[...] = -jnp.exp(a_log[0]) * LOG2E

    base = pl.multiple_of(step * SB, SB)
    sl = pl.ds(base, SB)
    dt = dt_s[sl, :]
    dtx = dtx_s[sl, :]
    bc = bc_s[sl, :]
    lane = lax.broadcasted_iota(jnp.int32, (nst, 128), 1)
    row = lax.broadcasted_iota(jnp.int32, (nst, 128), 0)
    a2 = a_s[...]
    tiles = chan // 128
    for b in range(SB):
        bcb = jnp.broadcast_to(bc[b:b + 1, :], (nst, 128))
        bcol = jnp.sum(jnp.where(lane == row, bcb, 0.0), axis=1, keepdims=True)
        ccol = jnp.sum(jnp.where(lane == row + nst, bcb, 0.0), axis=1, keepdims=True)
        s = jnp.exp2(dt[b:b + 1, :] * a2) * st[0, b] + dtx[b:b + 1, :] * bcol
        st_out[0, b] = s
        t = s * ccol
        part[b] = t[0:8] + t[8:16]
    for g in range(SB // 8):
        y_s[pl.ds(base + 8 * g, 8), :] = sublane_sums([part[8 * g + k] for k in range(8)])

    @pl.when(step == pl.num_programs(0) - 1)
    def _():
        y = y_s[...] + d_skip[layer:layer + 1, :] * xc_ref[...].astype(F32)
        yg = (y * silu(z_ref[...].astype(F32))).astype(BF16)
        core = lax.rem(lax.axis_index('tp'), 2)
        half = wo.shape[1] // 2
        w_copy.wait()
        mine[...] = jnp.dot(yg, wo[:, pl.ds(pl.multiple_of(core * half, 128), half)], preferred_element_type=F32)
        theirs[...] = jnp.dot(yg, wo[:, pl.ds(pl.multiple_of((1 - core) * half, 128), half)],
                              preferred_element_type=F32).astype(BF16)


def s_call(layer, row0, rows, state, p_list, xc, z, weights, prev):
    w_dt, b_dt, a_log, d_skip, w_out = weights
    chan = w_dt.shape[2]
    nst = a_log.shape[1]
    feat = w_out.shape[2]
    off = row0 // SB

    def whole(a):
        return pl.BlockSpec(a.shape, lambda i: (0,) * a.ndim)

    def layered(a):
        return pl.BlockSpec((1,) + a.shape[1:], lambda i: (layer,) + (0,) * (a.ndim - 1))

    st_spec = pl.BlockSpec((1, SB, nst, chan), lambda i: (layer, i + off, 0, 0))
    args = [state] + list(p_list) + [xc, z, w_dt, b_dt, a_log, d_skip, w_out]
    specs = [st_spec] + [whole(p) for p in p_list] + [whole(xc), whole(z), layered(w_dt), whole(b_dt), layered(a_log),
                                                     whole(d_skip), ANY]
    alias = {}
    if prev is not None:
        alias = {len(args): 0}
        args.append(prev)
        specs.append(ANY)
    return pl.pallas_call(
        functools.partial(s_kernel, layer, row0, rows, prev is not None),
        grid=(rows // SB,),
        out_shape=[jax.ShapeDtypeStruct(state.shape, F32), jax.ShapeDtypeStruct((rows, feat // 2), F32),
                   jax.ShapeDtypeStruct((rows, feat // 2), BF16)],
        in_specs=specs,
        out_specs=[st_spec, pl.BlockSpec((rows, feat // 2), lambda i: (0, 0)),
                   pl.BlockSpec((rows, feat // 2), lambda i: (0, 0))],
        input_output_aliases=alias,
        scratch_shapes=[
            pltpu.VMEM((rows, chan), F32), pltpu.VMEM((rows, chan), F32), pltpu.VMEM((rows, 128), F32),
            pltpu.VMEM((nst, chan), F32), pltpu.VMEM((rows, chan), F32), pltpu.VMEM((SB, 8, chan), F32),
            pltpu.VMEM(w_out.shape[1:], BF16), pltpu.SemaphoreType.DMA,
        ],
        compiler_params=pltpu.CompilerParams(vmem_limit_bytes=VLIM),
        cost_estimate=pl.CostEstimate(flops=rows * 8 * 10 ** 7, bytes_accessed=rows * 164 * 1024 + 8 * 2 ** 20,
                                      transcendentals=0),
        name=f"s{layer}r{row0}",
    )(*args)


def fin_kernel(r_ref, u, up, v, vp, out):
    core = lax.rem(lax.axis_index('tp'), 2)
    half = u.shape[1]
    lo = pl.ds(pl.multiple_of(core * half, 128), half)
    hi = pl.ds(pl.multiple_of((1 - core) * half, 128), half)
    out[:, lo] = r_ref[:, lo] + (u[...].astype(F32) + v[...].astype(F32))
    out[:, hi] = r_ref[:, hi] + (up[...].astype(F32) + vp[...].astype(F32))


def fin_call(r1, pieces):
    rows, feat = r1.shape
    blk = 64
    spec = pl.BlockSpec((blk, feat), lambda i: (i, 0))
    hspec = pl.BlockSpec((blk, feat // 2), lambda i: (i, 0))
    return pl.pallas_call(
        fin_kernel, grid=(rows // blk,), out_shape=jax.ShapeDtypeStruct(r1.shape, F32),
        in_specs=[spec] + [hspec] * 4, out_specs=spec, name="fin",
    )(r1, *pieces)


PART = [(0, 1), (1, 0), (2, 3), (3, 2)]
CROSS = [(0, 2), (2, 0), (1, 3), (3, 1)]
DIAG = [(0, 3), (3, 0), (1, 2), (2, 1)]


def exchange(mine, theirs):
    got = lax.ppermute(theirs, 'tp', PART)
    u = (mine + got.astype(F32)).astype(BF16)
    v = lax.ppermute(u, 'tp', CROSS)
    up = lax.ppermute(u, 'tp', PART)
    vp = lax.ppermute(v, 'tp', PART)
    return u, up, v, vp


def solution(mesh):
    def step(residual, norm_w, w_in, conv_w, conv_b, w_x, w_dt, b_dt, a_log, d_skip, w_out, conv_state, ssm_state):
        w_xt = jnp.transpose(w_x, (0, 2, 1))
        conv_t = jnp.transpose(conv_state, (0, 2, 1, 3))
        in_w = (norm_w, w_in, conv_w, conv_b, w_xt)
        s_w = (w_dt, b_dt, a_log, d_skip, w_out)
        rows = residual.shape[0]
        r = residual
        conv_out = None
        ssm_out = None
        pieces = None
        for layer in range(norm_w.shape[0]):
            got = in_call(layer, 0, rows, r, pieces, in_w, conv_t, conv_out)
            z, xc, p, conv_out = got[:4]
            if pieces is not None:
                r = got[4]
            p_list = [p, lax.ppermute(p, 'tp', PART), lax.ppermute(p, 'tp', CROSS), lax.ppermute(p, 'tp', DIAG)]
            ssm_out, mine, theirs = s_call(layer, 0, rows, ssm_state, p_list, xc, z, s_w, ssm_out)
            pieces = exchange(mine, theirs)
        out = fin_call(r, pieces)
        return out, jnp.transpose(conv_out, (0, 2, 1, 3)), ssm_out

    cache_spec = P(None, 'dp', None, 'tp')
    in_specs = (P('dp', None), P(None, None), P(None, None, None, 'tp'), P(None, None, 'tp'), P(None, 'tp'), P(None, 'tp', None), P(None, None, 'tp'), P(None, 'tp'), P(None, None, 'tp'), P(None, 'tp'), P(None, 'tp', None), cache_spec, cache_spec)
    out_specs = (P('dp', None), cache_spec, cache_spec)
    return jax.shard_map(step, mesh=mesh, in_specs=in_specs, out_specs=out_specs, check_vma=False)
```

time: 277 us -> 171 us (0.62)
  other arithmetic: 115 us -> 2.92 us
  Pallas kernels: 0 us -> 103 us
  waiting for transfers between devices: 83.6 us -> 51.3 us
  matrix products: 31.4 us -> 0 us
  local copies, waits for them, and re-layouts: 31.9 us -> 3.08 us
  between operations: 14.3 us -> 0.76 us
  starting transfers between devices: 0.34 us -> 9.49 us
    pallas_call x0 -> x5, Pallas kernels: none -> 103 us  [the longest x2 56.8 us: s_call(): pl.pallas_call(functools.partial(s_kernel, layer, row0, rows, prev is not...]
    psum x4 -> x0, waiting for transfers between devices: 83.5 us -> none  [the longest x2 47.9 us: device_step(): proj_sum = lax.psum(proj_part, 'tp').astype(jnp.float32)]
    ppermute x0 -> x14, waiting for transfers between devices: none -> 51.3 us  [the longest x2 30.1 us: exchange(): v = lax.ppermute(u, 'tp', CROSS)]
    reduce_sum x10 -> x0, other arithmetic: 38.4 us -> none  [the longest x2 33.4 us: device_step(): jnp.sum(new_ssm * c_vec[:, :, None], axis=1) + d_skip[layer_idx] * x_float]
    another operation x4 -> x0, other arithmetic: 37.9 us -> none  [device_step(): return (residual, jnp.stack(conv_list), jnp.stack(ssm_list))]
    add x3 -> x0, other arithmetic: 33.8 us -> none  [the longest x1 30.1 us: device_step(): decay_fac * ssm_state[layer_idx]]
    dot_general x8 -> x0, matrix products: 31.4 us -> none  [the longest x2 12.5 us: device_step(): jnp.dot(gated_y, w_out[layer_idx], preferred_element_type=jnp.float32)]
    slice x5 -> x0, local copies, waits for them, and re-layouts: 22.9 us -> none  [the longest x1 21.6 us: device_step(): w_in[layer_idx]]
  transfers between devices with their start and end apart: 4 -> 14, of which waited for: 4 -> 10; matrix products, arithmetic and copies ran while one was open for 14% -> 0% of each run, Pallas kernels for 0% -> 0%
where the time goes in v1:
time: 171 us; the launch traced here: 170 us
  Pallas kernels  103 us (60%)
  waiting for transfers between devices  51.3 us (30%)
  starting transfers between devices  9.49 us (6%)
  local copies, waits for them, and re-layouts  3.08 us (2%)
  other arithmetic  2.92 us (2%)
    pallas_call x2, Pallas kernels, s_call(): pl.pallas_call(functools.partial(s_kernel, layer, row0, rows, prev is not...  56.8 us
    pallas_call x2, Pallas kernels, in_call(): pl.pallas_call(functools.partial(in_kernel, layer, row0, rows, has_o), ou...  41.1 us
    ppermute x2, waiting for transfers between devices, exchange(): v = lax.ppermute(u, 'tp', CROSS)  30.1 us
    ppermute x2, waiting for transfers between devices, step(): lax.ppermute(p, 'tp', DIAG)  6.84 us
    ppermute x2, waiting for transfers between devices, step(): lax.ppermute(p, 'tp', CROSS)  6.09 us
    pallas_call x1, Pallas kernels, fin_call(): pl.pallas_call(fin_kernel, grid=(rows // blk,), out_shape=jax.ShapeDtypeS...  4.57 us
    ppermute x2, starting transfers between devices, step(): lax.ppermute(p, 'tp', DIAG)  4.28 us
    ppermute x2, waiting for transfers between devices, exchange(): got = lax.ppermute(theirs, 'tp', PART)  4.17 us
  transfers between devices with their start and end apart: 14, of which 10 were waited for; matrix products, arithmetic and copies ran while one was open for 0% of the time, Pallas kernels for 0%

profile of v1, /device:TPU:0, one launch (start us, length us, event | category | flops | bytes accessed | tf_op | source)
XLA Modules:
  0.0 170.1 jit_solution(11033974348024200423)
XLA Ops:
  0.6 19.8 %in0r0.1 = (bf16[256,1280]{1,0:T(8,128)(2,1)}, bf16[256,1280]{1,0:T(8,128)(2,1)}, bf16[256,192]{1,0:T(8,128)(2,1)}, bf16[2,3,256,1280]{3,2,1,0:T(8,128)(2,1)}) custom-call(f32[256,2560]{1,0:T(8,128)} %refs_0_.6, bf16[2,2560]{1,0:T(2,128)(2,1)} %refs_5_.1, bf16[2,2560,2,1280]{3,2,1,0:T(2,128)(2,1)} %refs_6_.1, bf16[2,4,1280]{2,1,0:T(4,128)(2,1)} %refs_7_.4, ...), custom_call_target="tpu_custom_call" | custom-call | flops 6710886400 | bytes 20971520 | tf_op jit(solution)/shard_map/in0r0/pallas_call | solution.py:125
  20.5 2.8 %collective-permute-start.2 = (bf16[256,192]{1,0:T(8,128)(2,1)}, bf16[256,192]{1,0:T(8,128)(2,1)S(1)}, u32[]{:S(2)}, u32[]{:S(2)}) collective-permute-start(bf16[256,192]{1,0:T(8,128)(2,1)} %get-tuple-element.18.refs_1_), channel_id=1, source_target_pairs={{0,3},{3,0},{1,2},{2,1},{4,7},{7,4},{5,6},{6,5}} | collective-permute-start | bytes 294920 | tf_op jit(solution)/shard_map/ppermute | solution.py:311
  23.3 0.6 collective-permute-start.1
  23.9 0.1 collective-permute-start
  24.0 3.2 %collective-permute-done.2.refs_4_ = bf16[256,192]{1,0:T(8,128)(2,1)S(1)} collective-permute-done((bf16[256,192]{1,0:T(8,128)(2,1)}, bf16[256,192]{1,0:T(8,128)(2,1)S(1)}, u32[]{:S(2)}, u32[]{:S(2)}) %collective-permute-start.2) | collective-permute-done | bytes 98336 | tf_op jit(solution)/shard_map/ppermute | solution.py:311
  27.2 3.0 %collective-permute-done.1.refs_3_ = bf16[256,192]{1,0:T(8,128)(2,1)S(1)} collective-permute-done((bf16[256,192]{1,0:T(8,128)(2,1)}, bf16[256,192]{1,0:T(8,128)(2,1)S(1)}, u32[]{:S(2)}, u32[]{:S(2)}) %collective-permute-start.1) | collective-permute-done | bytes 98336 | tf_op jit(solution)/shard_map/ppermute | solution.py:311
  30.1 0.0 collective-permute-done.refs_2_
  30.2 0.0 copy-done.11
  30.2 0.6 copy-done.12
  30.8 0.0 copy-done.13
  30.8 28.4 %s0r0.1 = (f32[2,256,16,1280]{3,2,1,0:T(8,128)}, f32[256,1280]{1,0:T(8,128)}, bf16[256,1280]{1,0:T(8,128)(2,1)}) custom-call(f32[2,256,16,1280]{3,2,1,0:T(8,128)} %refs_0_.7, bf16[256,192]{1,0:T(8,128)(2,1)} %get-tuple-element.18.refs_1_, bf16[256,192]{1,0:T(8,128)(2,1)} %copy-done.13, bf16[256,192]{1,0:T(8,128)(2,1)} %copy-done.12, ...), custom_call_target="tpu_custom_call" | custom-call | flops 20480000000 | bytes 51380224 | tf_op jit(solution)/shard_map/s0r0/pallas_call | solution.py:240
  59.2 0.0 collective-permute-start.3
  59.3 2.1 %collective-permute-done.3 = bf16[256,1280]{1,0:T(8,128)(2,1)S(1)} collective-permute-done((bf16[256,1280]{1,0:T(8,128)(2,1)}, bf16[256,1280]{1,0:T(8,128)(2,1)S(1)}, u32[]{:S(2)}, u32[]{:S(2)}) %collective-permute-start.3) | collective-permute-done | bytes 655392 | tf_op jit(solution)/shard_map/ppermute | solution.py:287
  61.4 1.5 add_convert_fusion.1.refs_1_
  62.8 0.0 copy-start.1
  62.8 2.3 %collective-permute-start.5 = (bf16[256,1280]{1,0:T(8,128)(2,1)S(1)}, bf16[256,1280]{1,0:T(8,128)(2,1)S(1)}, u32[]{:S(2)}, u32[]{:S(2)}) collective-permute-start(bf16[256,1280]{1,0:T(8,128)(2,1)S(1)} %add_convert_fusion.1.refs_1_), channel_id=1, source_target_pairs={{0,2},{2,0},{1,3},{3,1},{4,6},{6,4},{5,7},{7,5}} | collective-permute-start | bytes 1966088 | tf_op jit(solution)/shard_map/ppermute | solution.py:289
  65.2 0.0 collective-permute-start.4
  65.2 15.0 %collective-permute-done.5.refs_3_ = bf16[256,1280]{1,0:T(8,128)(2,1)S(1)} collective-permute-done((bf16[256,1280]{1,0:T(8,128)(2,1)S(1)}, bf16[256,1280]{1,0:T(8,128)(2,1)S(1)}, u32[]{:S(2)}, u32[]{:S(2)}) %collective-permute-start.5) | collective-permute-done | bytes 655392 | tf_op jit(solution)/shard_map/ppermute | solution.py:289
  80.2 0.0 collective-permute-start.6
  80.2 0.0 collective-permute-done.4.refs_2_
  80.2 0.0 copy-start.6
  80.2 2.1 %collective-permute-done.6.refs_4_ = bf16[256,1280]{1,0:T(8,128)(2,1)S(1)} collective-permute-done((bf16[256,1280]{1,0:T(8,128)(2,1)S(1)}, bf16[256,1280]{1,0:T(8,128)(2,1)S(1)}, u32[]{:S(2)}, u32[]{:S(2)}) %collective-permute-start.6) | collective-permute-done | bytes 655392 | tf_op jit(solution)/shard_map/ppermute | solution.py:291
  82.3 0.8 copy-done.7
  83.1 0.0 copy-done.1
  83.1 0.0 copy-done.5
  83.1 0.0 copy-done.6
  83.1 21.3 %in1r0.1 = (bf16[256,1280]{1,0:T(8,128)(2,1)}, bf16[256,1280]{1,0:T(8,128)(2,1)}, bf16[256,192]{1,0:T(8,128)(2,1)}, bf16[2,3,256,1280]{3,2,1,0:T(8,128)(2,1)}, f32[256,2560]{1,0:T(8,128)}) custom-call(f32[256,2560]{1,0:T(8,128)} %refs_0_.6, bf16[256,1280]{1,0:T(8,128)(2,1)} %copy-done.1, ...), custom_call_target="tpu_custom_call", output_to_operand_aliasing={{3}: (11, {})} | custom-call | flops 6710886400 | bytes 20971520 | tf_op jit(solution)/shard_map/in1r0/pallas_call | solution.py:125
  104.4 1.5 collective-permute-start.9
  105.9 0.3 collective-permute-start.8
  106.2 0.1 collective-permute-start.7
  106.3 3.6 %collective-permute-done.9.refs_4_ = bf16[256,192]{1,0:T(8,128)(2,1)S(1)} collective-permute-done((bf16[256,192]{1,0:T(8,128)(2,1)}, bf16[256,192]{1,0:T(8,128)(2,1)S(1)}, u32[]{:S(2)}, u32[]{:S(2)}) %collective-permute-start.9) | collective-permute-done | bytes 98336 | tf_op jit(solution)/shard_map/ppermute | solution.py:311
  110.0 3.1 %collective-permute-done.8.refs_3_ = bf16[256,192]{1,0:T(8,128)(2,1)S(1)} collective-permute-done((bf16[256,192]{1,0:T(8,128)(2,1)}, bf16[256,192]{1,0:T(8,128)(2,1)S(1)}, u32[]{:S(2)}, u32[]{:S(2)}) %collective-permute-start.8) | collective-permute-done | bytes 98336 | tf_op jit(solution)/shard_map/ppermute | solution.py:311
  113.1 0.0 collective-permute-done.7.refs_2_
  113.1 0.6 copy-done.9
  113.7 0.1 copy-done.10
  113.8 28.4 %s1r0.1 = (f32[2,256,16,1280]{3,2,1,0:T(8,128)}, f32[256,1280]{1,0:T(8,128)}, bf16[256,1280]{1,0:T(8,128)(2,1)}) custom-call(f32[2,256,16,1280]{3,2,1,0:T(8,128)} %refs_0_.7, bf16[256,192]{1,0:T(8,128)(2,1)} %get-tuple-element.25.refs_1_, bf16[256,192]{1,0:T(8,128)(2,1)} %copy-done.10, bf16[256,192]{1,0:T(8,128)(2,1)} %copy-done.9, ...), custom_call_target="tpu_custom_call", output_to_operand_aliasing={{0}: (12, {})} | custom-call | flops 20480000000 | bytes 51380224 | tf_op jit(solution)/shard_map/s1r0/pallas_call | solution.py:240
  142.2 0.0 collective-permute-start.10
  142.2 2.1 %collective-permute-done.10 = bf16[256,1280]{1,0:T(8,128)(2,1)S(1)} collective-permute-done((bf16[256,1280]{1,0:T(8,128)(2,1)}, bf16[256,1280]{1,0:T(8,128)(2,1)S(1)}, u32[]{:S(2)}, u32[]{:S(2)}) %collective-permute-start.10) | collective-permute-done | bytes 655392 | tf_op jit(solution)/shard_map/ppermute | solution.py:287
  144.3 1.5 add_convert_fusion.u
  145.8 1.8 %collective-permute-start.12 = (bf16[256,1280]{1,0:T(8,128)(2,1)S(1)}, bf16[256,1280]{1,0:T(8,128)(2,1)S(1)}, u32[]{:S(2)}, u32[]{:S(2)}) collective-permute-start(bf16[256,1280]{1,0:T(8,128)(2,1)S(1)} %add_convert_fusion.u), channel_id=1, source_target_pairs={{0,2},{2,0},{1,3},{3,1},{4,6},{6,4},{5,7},{7,5}} | collective-permute-start | bytes 1966088 | tf_op jit(solution)/shard_map/ppermute | solution.py:289
  147.5 0.0 collective-permute-start.11
  147.5 15.0 %collective-permute-done.12.v = bf16[256,1280]{1,0:T(8,128)(2,1)S(1)} collective-permute-done((bf16[256,1280]{1,0:T(8,128)(2,1)S(1)}, bf16[256,1280]{1,0:T(8,128)(2,1)S(1)}, u32[]{:S(2)}, u32[]{:S(2)}) %collective-permute-start.12) | collective-permute-done | bytes 655392 | tf_op jit(solution)/shard_map/ppermute | solution.py:289
  162.6 0.0 collective-permute-start.13
  162.6 0.0 collective-permute-done.11.up
  162.6 2.1 %collective-permute-done.13.vp = bf16[256,1280]{1,0:T(8,128)(2,1)S(1)} collective-permute-done((bf16[256,1280]{1,0:T(8,128)(2,1)S(1)}, bf16[256,1280]{1,0:T(8,128)(2,1)S(1)}, u32[]{:S(2)}, u32[]{:S(2)}) %collective-permute-start.13) | collective-permute-done | bytes 655392 | tf_op jit(solution)/shard_map/ppermute | solution.py:291
  164.7 0.0 copy-done.2
  164.7 0.8 copy-done.4
  165.5 4.6 %fin.1 = f32[256,2560]{1,0:T(8,128)} custom-call(f32[256,2560]{1,0:T(8,128)} %get-tuple-element.24.r_ref, bf16[256,1280]{1,0:T(8,128)(2,1)} %copy-done, bf16[256,1280]{1,0:T(8,128)(2,1)} %copy-done.3, bf16[256,1280]{1,0:T(8,128)(2,1)} %copy-done.2, bf16[256,1280]{1,0:T(8,128)(2,1)} %copy-done.4), custom_call_target="tpu_custom_call" | custom-call | tf_op jit(solution)/shard_map/fin/pallas_call | solution.py:275
  (15 shorter events, 0.0 us)
Async XLA Ops:
  20.5 6.7 %collective-permute-start.2 = (bf16[256,192]{1,0:T(8,128)(2,1)}, bf16[256,192]{1,0:T(8,128)(2,1)S(1)}, u32[]{:S(2)}, u32[]{:S(2)}) collective-permute-start(bf16[256,192]{1,0:T(8,128)(2,1)} %get-tuple-element.18.refs_1_), channel_id=1, source_target_pairs={{0,3},{3,0},{1,2},{2,1},{4,7},{7,4},{5,6},{6,5}} | collective-permute-start | bytes 294920 | tf_op jit(solution)/shard_map/ppermute | solution.py:311
  23.3 6.9 %collective-permute-start.1 = (bf16[256,192]{1,0:T(8,128)(2,1)}, bf16[256,192]{1,0:T(8,128)(2,1)S(1)}, u32[]{:S(2)}, u32[]{:S(2)}) collective-permute-start(bf16[256,192]{1,0:T(8,128)(2,1)} %get-tuple-element.18.refs_1_), channel_id=1, source_target_pairs={{0,2},{2,0},{1,3},{3,1},{4,6},{6,4},{5,7},{7,5}} | collective-permute-start | bytes 294920 | tf_op jit(solution)/shard_map/ppermute | solution.py:311
  23.9 6.3 %collective-permute-start = (bf16[256,192]{1,0:T(8,128)(2,1)}, bf16[256,192]{1,0:T(8,128)(2,1)S(1)}, u32[]{:S(2)}, u32[]{:S(2)}) collective-permute-start(bf16[256,192]{1,0:T(8,128)(2,1)} %get-tuple-element.18.refs_1_), channel_id=1, source_target_pairs={{0,1},{1,0},{2,3},{3,2},{4,5},{5,4},{6,7},{7,6}} | collective-permute-start | bytes 294920 | tf_op jit(solution)/shard_map/ppermute | solution.py:311
  27.1 3.0 %copy-start.11 = (bf16[256,192]{1,0:T(8,128)(2,1)}, bf16[256,192]{1,0:T(8,128)(2,1)S(1)}, u32[]{:S(2)}) copy-start(bf16[256,192]{1,0:T(8,128)(2,1)S(1)} %collective-permute-done.2.refs_4_) | copy-start | bytes 294916
  30.1 0.7 copy-start.12
  30.1 0.7 copy-start.13
  59.2 2.1 %collective-permute-start.3 = (bf16[256,1280]{1,0:T(8,128)(2,1)}, bf16[256,1280]{1,0:T(8,128)(2,1)S(1)}, u32[]{:S(2)}, u32[]{:S(2)}) collective-permute-start(bf16[256,1280]{1,0:T(8,128)(2,1)} %get-tuple-element.22), channel_id=1, source_target_pairs={{0,1},{1,0},{2,3},{3,2},{4,5},{5,4},{6,7},{7,6}} | collective-permute-start | bytes 1966088 | tf_op jit(solution)/shard_map/ppermute | solution.py:287
  62.8 20.3 %copy-start.1 = (bf16[256,1280]{1,0:T(8,128)(2,1)}, bf16[256,1280]{1,0:T(8,128)(2,1)S(1)}, u32[]{:S(2)}) copy-start(bf16[256,1280]{1,0:T(8,128)(2,1)S(1)} %add_convert_fusion.1.refs_1_) | copy-start | bytes 1966084
  62.8 17.4 %collective-permute-start.5 = (bf16[256,1280]{1,0:T(8,128)(2,1)S(1)}, bf16[256,1280]{1,0:T(8,128)(2,1)S(1)}, u32[]{:S(2)}, u32[]{:S(2)}) collective-permute-start(bf16[256,1280]{1,0:T(8,128)(2,1)S(1)} %add_convert_fusion.1.refs_1_), channel_id=1, source_target_pairs={{0,2},{2,0},{1,3},{3,1},{4,6},{6,4},{5,7},{7,5}} | collective-permute-start | bytes 1966088 | tf_op jit(solution)/shard_map/ppermute | solution.py:289
  65.2 15.0 %collective-permute-start.4 = (bf16[256,1280]{1,0:T(8,128)(2,1)S(1)}, bf16[256,1280]{1,0:T(8,128)(2,1)S(1)}, u32[]{:S(2)}, u32[]{:S(2)}) collective-permute-start(bf16[256,1280]{1,0:T(8,128)(2,1)S(1)} %add_convert_fusion.1.refs_1_), channel_id=1, source_target_pairs={{0,1},{1,0},{2,3},{3,2},{4,5},{5,4},{6,7},{7,6}} | collective-permute-start | bytes 1966088 | tf_op jit(solution)/shard_map/ppermute | solution.py:290
  80.2 2.9 %copy-start.5 = (bf16[256,1280]{1,0:T(8,128)(2,1)}, bf16[256,1280]{1,0:T(8,128)(2,1)S(1)}, u32[]{:S(2)}) copy-start(bf16[256,1280]{1,0:T(8,128)(2,1)S(1)} %collective-permute-done.5.refs_3_) | copy-start | bytes 1966084
  80.2 2.1 %collective-permute-start.6 = (bf16[256,1280]{1,0:T(8,128)(2,1)S(1)}, bf16[256,1280]{1,0:T(8,128)(2,1)S(1)}, u32[]{:S(2)}, u32[]{:S(2)}) collective-permute-start(bf16[256,1280]{1,0:T(8,128)(2,1)S(1)} %collective-permute-done.5.refs_3_), channel_id=1, source_target_pairs={{0,1},{1,0},{2,3},{3,2},{4,5},{5,4},{6,7},{7,6}} | collective-permute-start | bytes 1966088 | tf_op jit(solution)/shard_map/ppermute | solution.py:291
  80.2 2.9 %copy-start.6 = (bf16[256,1280]{1,0:T(8,128)(2,1)}, bf16[256,1280]{1,0:T(8,128)(2,1)S(1)}, u32[]{:S(2)}) copy-start(bf16[256,1280]{1,0:T(8,128)(2,1)S(1)} %collective-permute-done.4.refs_2_) | copy-start | bytes 1966084
  82.3 0.8 copy-start.7
  104.4 5.5 %collective-permute-start.9 = (bf16[256,192]{1,0:T(8,128)(2,1)}, bf16[256,192]{1,0:T(8,128)(2,1)S(1)}, u32[]{:S(2)}, u32[]{:S(2)}) collective-permute-start(bf16[256,192]{1,0:T(8,128)(2,1)} %get-tuple-element.25.refs_1_), channel_id=1, source_target_pairs={{0,3},{3,0},{1,2},{2,1},{4,7},{7,4},{5,6},{6,5}} | collective-permute-start | bytes 294920 | tf_op jit(solution)/shard_map/ppermute | solution.py:311
  105.9 7.1 %collective-permute-start.8 = (bf16[256,192]{1,0:T(8,128)(2,1)}, bf16[256,192]{1,0:T(8,128)(2,1)S(1)}, u32[]{:S(2)}, u32[]{:S(2)}) collective-permute-start(bf16[256,192]{1,0:T(8,128)(2,1)} %get-tuple-element.25.refs_1_), channel_id=1, source_target_pairs={{0,2},{2,0},{1,3},{3,1},{4,6},{6,4},{5,7},{7,5}} | collective-permute-start | bytes 294920 | tf_op jit(solution)/shard_map/ppermute | solution.py:311
  106.2 6.8 %collective-permute-start.7 = (bf16[256,192]{1,0:T(8,128)(2,1)}, bf16[256,192]{1,0:T(8,128)(2,1)S(1)}, u32[]{:S(2)}, u32[]{:S(2)}) collective-permute-start(bf16[256,192]{1,0:T(8,128)(2,1)} %get-tuple-element.25.refs_1_), channel_id=1, source_target_pairs={{0,1},{1,0},{2,3},{3,2},{4,5},{5,4},{6,7},{7,6}} | collective-permute-start | bytes 294920 | tf_op jit(solution)/shard_map/ppermute | solution.py:311
  110.0 3.1 %copy-start.8 = (bf16[256,192]{1,0:T(8,128)(2,1)}, bf16[256,192]{1,0:T(8,128)(2,1)S(1)}, u32[]{:S(2)}) copy-start(bf16[256,192]{1,0:T(8,128)(2,1)S(1)} %collective-permute-done.9.refs_4_) | copy-start | bytes 294916
  113.0 0.6 copy-start.9
  113.1 0.7 copy-start.10
  142.2 2.1 %collective-permute-start.10 = (bf16[256,1280]{1,0:T(8,128)(2,1)}, bf16[256,1280]{1,0:T(8,128)(2,1)S(1)}, u32[]{:S(2)}, u32[]{:S(2)}) collective-permute-start(bf16[256,1280]{1,0:T(8,128)(2,1)} %get-tuple-element.30), channel_id=1, source_target_pairs={{0,1},{1,0},{2,3},{3,2},{4,5},{5,4},{6,7},{7,6}} | collective-permute-start | bytes 1966088 | tf_op jit(solution)/shard_map/ppermute | solution.py:287
  145.8 18.9 %copy-start = (bf16[256,1280]{1,0:T(8,128)(2,1)}, bf16[256,1280]{1,0:T(8,128)(2,1)S(1)}, u32[]{:S(2)}) copy-start(bf16[256,1280]{1,0:T(8,128)(2,1)S(1)} %add_convert_fusion.u) | copy-start | bytes 1966084
  145.8 16.8 %collective-permute-start.12 = (bf16[256,1280]{1,0:T(8,128)(2,1)S(1)}, bf16[256,1280]{1,0:T(8,128)(2,1)S(1)}, u32[]{:S(2)}, u32[]{:S(2)}) collective-permute-start(bf16[256,1280]{1,0:T(8,128)(2,1)S(1)} %add_convert_fusion.u), channel_id=1, source_target_pairs={{0,2},{2,0},{1,3},{3,1},{4,6},{6,4},{5,7},{7,5}} | collective-permute-start | bytes 1966088 | tf_op jit(solution)/shard_map/ppermute | solution.py:289
  147.5 15.0 %collective-permute-start.11 = (bf16[256,1280]{1,0:T(8,128)(2,1)S(1)}, bf16[256,1280]{1,0:T(8,128)(2,1)S(1)}, u32[]{:S(2)}, u32[]{:S(2)}) collective-permute-start(bf16[256,1280]{1,0:T(8,128)(2,1)S(1)} %add_convert_fusion.u), channel_id=1, source_target_pairs={{0,1},{1,0},{2,3},{3,2},{4,5},{5,4},{6,7},{7,6}} | collective-permute-start | bytes 1966088 | tf_op jit(solution)/shard_map/ppermute | solution.py:290
  162.6 2.1 %copy-start.2 = (bf16[256,1280]{1,0:T(8,128)(2,1)}, bf16[256,1280]{1,0:T(8,128)(2,1)S(1)}, u32[]{:S(2)}) copy-start(bf16[256,1280]{1,0:T(8,128)(2,1)S(1)} %collective-permute-done.12.v) | copy-start | bytes 1966084
  162.6 2.1 %collective-permute-start.13 = (bf16[256,1280]{1,0:T(8,128)(2,1)S(1)}, bf16[256,1280]{1,0:T(8,128)(2,1)S(1)}, u32[]{:S(2)}, u32[]{:S(2)}) collective-permute-start(bf16[256,1280]{1,0:T(8,128)(2,1)S(1)} %collective-permute-done.12.v), channel_id=1, source_target_pairs={{0,1},{1,0},{2,3},{3,2},{4,5},{5,4},{6,7},{7,6}} | collective-permute-start | bytes 1966088 | tf_op jit(solution)/shard_map/ppermute | solution.py:291
  162.6 2.1 %copy-start.3 = (bf16[256,1280]{1,0:T(8,128)(2,1)}, bf16[256,1280]{1,0:T(8,128)(2,1)S(1)}, u32[]{:S(2)}) copy-start(bf16[256,1280]{1,0:T(8,128)(2,1)S(1)} %collective-permute-done.11.up) | copy-start | bytes 1966084
  164.7 0.9 copy-start.4

commit v2 on v1

v2 whole, which is shorter than its diff:
```python
import functools
import math

import jax
import jax.numpy as jnp
from jax import lax
from jax.experimental import pallas as pl
from jax.experimental.pallas import tpu as pltpu
from jax.sharding import PartitionSpec as P

F32 = jnp.float32
BF16 = jnp.bfloat16
ANY = pl.BlockSpec(memory_space=pl.ANY)
VMEM = pl.BlockSpec(memory_space=pltpu.VMEM)
NCH = 256
SB = 16
HALF = 128
LOG2E = math.log2(math.e)
MESH = pl.DeviceIdType.MESH


def silu(v):
    return v * jax.nn.sigmoid(v)


def expand_matrix():
    row = lax.broadcasted_iota(jnp.int32, (128, 512), 0)
    col = lax.broadcasted_iota(jnp.int32, (128, 512), 1)
    target = 2 * row + jnp.where(col < 256, 0, 257)
    return jnp.where(col == target, 1.0, 0.0).astype(BF16)


def in_kernel(layer, has_o, *refs):
    refs = list(refs)
    res_hbm = refs.pop(0)
    pieces = [[refs.pop(0) for _ in range(4)] for _ in range(2)] if has_o else None
    norm_w, w_in, conv_w, conv_b, w_x, conv_st = refs[:6]
    refs = refs[6:]
    if layer > 0:
        refs.pop(0)
    z_out, xc_out, p_out, conv_out = refs[:4]
    refs = refs[4:]
    r_out = refs.pop(0) if has_o else None
    wbuf, hx, rbuf, cbuf, xbuf, rsem, wsem, csem, osem = refs
    rows, feat = rbuf.shape
    nchunk = wbuf.shape[0]
    w_flat = w_in.reshape(w_in.shape[0], 2 * feat, w_in.shape[3])

    r_copy = pltpu.make_async_copy(res_hbm, rbuf, rsem)
    c_copy = pltpu.make_async_copy(conv_st.at[layer], cbuf, csem)
    state_copy = pltpu.make_async_copy(cbuf.at[pl.ds(1, 2)], conv_out.at[layer, pl.ds(0, 2)], osem.at[1])
    x_copy = pltpu.make_async_copy(xbuf, conv_out.at[layer, 2], osem.at[2])

    def w_copy(c):
        return pltpu.make_async_copy(w_flat.at[layer, :, pl.ds(c * NCH, NCH)], wbuf.at[c], wsem.at[c])

    r_copy.start()
    w_copy(0).start()
    w_copy(1).start()
    r_copy.wait()
    c_copy.start()
    if has_o:
        core = lax.rem(lax.axis_index('tp'), 2)
        half = feat // 2
        lo = pl.ds(pl.multiple_of(core * half, 128), half)
        hi = pl.ds(pl.multiple_of((1 - core) * half, 128), half)
        for k, (u, up, v, vp) in enumerate(pieces):
            rs = slice(k * HALF, (k + 1) * HALF)
            rbuf[rs, lo] = rbuf[rs, lo] + (u[...].astype(F32) + v[...].astype(F32))
            rbuf[rs, hi] = rbuf[rs, hi] + (up[...].astype(F32) + vp[...].astype(F32))
        pltpu.make_async_copy(rbuf, r_out, osem.at[0]).start()
    r = rbuf[...]
    inv = lax.rsqrt(jnp.mean(r * r, axis=-1, keepdims=True) + 1e-5)
    h = (r * inv * norm_w[layer:layer + 1, :].astype(F32)).astype(BF16)
    ex = expand_matrix()
    for j in range(feat // 128):
        e = jnp.dot(h[:, j * 128:(j + 1) * 128], ex, preferred_element_type=F32).astype(BF16)
        hx[0:rows, j * 256:(j + 1) * 256] = e[:, :256]
        hx[rows:2 * rows, j * 256:(j + 1) * 256] = e[:, 256:]
    c_copy.wait()
    state_copy.start()
    p_acc = jnp.zeros((w_x.shape[1], rows), F32)
    for c in range(nchunk):
        w_copy(c).wait()
        if c + 2 < nchunk:
            w_copy(c + 2).start()
        sl = slice(c * NCH, (c + 1) * NCH)
        acc = jnp.dot(hx[...], wbuf[c], preferred_element_type=F32)
        x = acc[:rows].astype(BF16)
        z_out[:, sl] = acc[rows:].astype(BF16)
        xbuf[:, sl] = x
        cw = conv_w[layer, :, sl].astype(F32)
        pre = cbuf[0, :, sl].astype(F32) * cw[0:1] + cbuf[1, :, sl].astype(F32) * cw[1:2]
        pre = pre + cbuf[2, :, sl].astype(F32) * cw[2:3] + x.astype(F32) * cw[3:4]
        pre = pre + conv_b[layer:layer + 1, sl].astype(F32)
        xc = silu(pre).astype(BF16)
        xc_out[:, sl] = xc
        p_acc = p_acc + lax.dot_general(w_x[layer, :, sl], xc, (((1,), (1,)), ((), ())), preferred_element_type=F32)
    p_out[...] = p_acc.astype(BF16)
    x_copy.start()
    x_copy.wait()
    state_copy.wait()
    if has_o:
        pltpu.make_async_copy(rbuf, r_out, osem.at[0]).wait()


def in_call(layer, residual, pieces, weights, conv_st, conv_prev):
    norm_w, w_in, conv_w, conv_b, w_x = weights
    has_o = pieces is not None
    rows, feat = residual.shape
    chan = w_in.shape[3]
    flat = [a for half in pieces for a in half] if has_o else []
    args = [residual] + flat + [norm_w, w_in, conv_w, conv_b, w_x, conv_st]
    specs = [ANY] + [VMEM] * len(flat) + [VMEM, ANY, VMEM, VMEM, VMEM, ANY]
    alias = {}
    if layer > 0:
        alias = {len(args): 3}
        args.append(conv_prev)
        specs.append(ANY)
    outs = [pltpu.VMEM((rows, chan), BF16), pltpu.VMEM((rows, chan), BF16),
            pltpu.VMEM((w_x.shape[1], rows), BF16), jax.ShapeDtypeStruct(conv_st.shape, BF16)]
    out_specs = [VMEM, VMEM, VMEM, ANY]
    if has_o:
        outs.append(jax.ShapeDtypeStruct((rows, feat), F32))
        out_specs.append(ANY)
    nchunk = chan // NCH
    return pl.pallas_call(
        functools.partial(in_kernel, layer, has_o),
        out_shape=outs, in_specs=specs, out_specs=out_specs, input_output_aliases=alias,
        scratch_shapes=[
            pltpu.VMEM((nchunk, 2 * feat, NCH), BF16),
            pltpu.VMEM((2 * rows, 2 * feat), BF16),
            pltpu.VMEM((rows, feat), F32),
            pltpu.VMEM((3, rows, chan), BF16),
            pltpu.VMEM((rows, chan), BF16),
            pltpu.SemaphoreType.DMA, pltpu.SemaphoreType.DMA((nchunk,)), pltpu.SemaphoreType.DMA,
            pltpu.SemaphoreType.DMA((3,)),
        ],
        compiler_params=pltpu.CompilerParams(vmem_limit_bytes=40 * 2 ** 20),
        cost_estimate=pl.CostEstimate(flops=rows * 2 * feat * 2 * chan * 2, bytes_accessed=20 * 2 ** 20, transcendentals=0),
        name=f"in{layer}",
    )(*args)


def rms0(v):
    return v * lax.rsqrt(jnp.mean(v * v, axis=0, keepdims=True) + 1e-6)


def sublane_sums(parts):
    sub = lax.broadcasted_iota(jnp.int32, parts[0].shape, 0)
    for step in (4, 2, 1):
        keep = (sub & step) == 0
        half = len(parts) // 2
        parts = [jnp.where(keep, parts[k], parts[k + half])
                 + pltpu.roll(jnp.where(keep, parts[k + half], parts[k]), step, 0) if step == 4 else
                 jnp.where(keep, parts[k], parts[k + half])
                 + jnp.where(keep, pltpu.roll(parts[k], 8 - step, 0), pltpu.roll(parts[k + half], step, 0))
                 for k in range(half)]
    return parts[0]


def k_kernel(layer, pt, xc_ref, z_ref, w_dt, b_dt, a_log, d_skip, w_out, state,
             st, ua, ub, upa, upb, va, vpa,
             dt_s, dtx_s, bc_s, a_s, y_s, part, wo, mine, theirs, got, p_sw, p_cs, p_v,
             stsem, wsem, ssem, rsem):
    me = lax.axis_index('tp')
    core = lax.rem(me, 2)
    partner = me + 1 - 2 * core
    other = lax.rem(me + 2, 4)
    rows, chan = dt_s.shape
    rank = w_dt.shape[1]
    nst = a_s.shape[0]
    nblk = rows // SB

    barrier = pltpu.get_barrier_semaphore()
    for dev in (partner, other):
        pl.semaphore_signal(barrier, inc=1, device_id={'tp': dev}, device_id_type=MESH)

    def st_copy(i):
        rs = pl.ds(i * SB, SB)
        return pltpu.make_async_copy(state.at[layer, rs], st.at[rs], stsem.at[i])

    for i in range(nblk):
        st_copy(i).start()
    w_copy = pltpu.make_async_copy(w_out.at[layer], wo, wsem)
    w_copy.start()

    def send(src, dst, k, dev):
        return pltpu.make_async_remote_copy(src_ref=src, dst_ref=dst, send_sem=ssem.at[k], recv_sem=rsem.at[k],
                                            device_id={'tp': dev}, device_id_type=MESH)

    pl.semaphore_wait(barrier, 2)
    p1 = send(pt, p_sw, 0, partner)
    p1.start()
    a_s[...] = -jnp.exp(a_log[layer]) * LOG2E
    p1.wait_recv()
    p_cs[...] = (pt[...].astype(F32) + p_sw[...].astype(F32)).astype(BF16)
    p2 = send(p_cs, p_v, 1, other)
    p2.start()
    p2.wait_recv()
    p = p_cs[...].astype(F32) + p_v[...].astype(F32)
    low = rms0(p[:rank]).astype(BF16)
    pre = lax.dot_general(low, w_dt[layer], (((0,), (0,)), ((), ())), preferred_element_type=F32)
    pre = pre + b_dt[layer:layer + 1, :]
    dt = jnp.maximum(pre, 0.0) + jnp.log1p(jnp.exp(-jnp.abs(pre)))
    dt_s[...] = dt
    dtx_s[...] = dt * xc_ref[...].astype(F32)
    bc = jnp.concatenate([rms0(p[rank:rank + nst]), rms0(p[rank + nst:])], axis=0)
    bc_s[:, 0:2 * nst] = jnp.transpose(bc)

    lane = lax.broadcasted_iota(jnp.int32, (nst, 128), 1)
    row = lax.broadcasted_iota(jnp.int32, (nst, 128), 0)

    def block(i, carry):
        st_copy(i).wait()
        base = pl.multiple_of(i * SB, SB)
        sl = pl.ds(base, SB)
        dt = dt_s[sl, :]
        dtx = dtx_s[sl, :]
        bc = bc_s[sl, :]
        a2 = a_s[...]
        for b in range(SB):
            bcb = jnp.broadcast_to(bc[b:b + 1, :], (nst, 128))
            bcol = jnp.sum(jnp.where(lane == row, bcb, 0.0), axis=1, keepdims=True)
            ccol = jnp.sum(jnp.where(lane == row + nst, bcb, 0.0), axis=1, keepdims=True)
            s = jnp.exp2(dt[b:b + 1, :] * a2) * st[base + b] + dtx[b:b + 1, :] * bcol
            st[base + b] = s
            t = s * ccol
            part[b] = t[0:8] + t[8:16]
        for g in range(SB // 8):
            y_s[pl.ds(base + 8 * g, 8), :] = sublane_sums([part[8 * g + k] for k in range(8)])
        return carry

    half = wo.shape[1] // 2
    lo = pl.ds(pl.multiple_of(core * half, 128), half)
    hi = pl.ds(pl.multiple_of((1 - core) * half, 128), half)

    def project(k):
        rs = pl.ds(k * HALF, HALF)
        y = y_s[rs, :] + d_skip[layer:layer + 1, :] * xc_ref[rs, :].astype(F32)
        yg = (y * silu(z_ref[rs, :].astype(F32))).astype(BF16)
        theirs[k] = jnp.dot(yg, wo[:, hi], preferred_element_type=F32).astype(BF16)
        red = send(theirs.at[k], got.at[k], 2 + k, partner)
        red.start()
        mine[k] = jnp.dot(yg, wo[:, lo], preferred_element_type=F32)
        return red

    lax.fori_loop(0, nblk // 2, block, 0)
    w_copy.wait()
    red_a = project(0)
    lax.fori_loop(nblk // 2, 5 * nblk // 8, block, 0)
    red_a.wait_recv()
    ua[...] = (mine[0] + got[0].astype(F32)).astype(BF16)
    cross_a = send(ua, va, 4, other)
    cross_a.start()
    up_a = send(ua, upa, 5, partner)
    up_a.start()
    lax.fori_loop(5 * nblk // 8, nblk, block, 0)
    red_b = project(1)
    red_b.wait_recv()
    ub[...] = (mine[1] + got[1].astype(F32)).astype(BF16)
    up_b = send(ub, upb, 6, partner)
    up_b.start()
    cross_a.wait_recv()
    fwd_a = send(va, vpa, 7, partner)
    fwd_a.start()
    for c in (up_a, up_b, fwd_a):
        c.wait_recv()
    for c in (p1, p2, red_a, red_b, cross_a, up_a, up_b, fwd_a):
        c.wait_send()


def k_call(layer, pt, xc, z, weights, state):
    w_dt, b_dt, a_log, d_skip, w_out = weights
    rows, chan = xc.shape
    nst = a_log.shape[1]
    feat = w_out.shape[2]
    half = feat // 2
    piece = pltpu.VMEM((HALF, half), BF16)
    ins = [pltpu.with_memory_space_constraint(a, pltpu.VMEM) for a in (pt, xc, z)]
    return pl.pallas_call(
        functools.partial(k_kernel, layer),
        out_shape=[pltpu.VMEM((rows, nst, chan), F32)] + [piece] * 6,
        in_specs=[VMEM] * 7 + [ANY, ANY], out_specs=[VMEM] * 7,
        scratch_shapes=[
            pltpu.VMEM((rows, chan), F32), pltpu.VMEM((rows, chan), F32), pltpu.VMEM((rows, 128), F32),
            pltpu.VMEM((nst, chan), F32), pltpu.VMEM((rows, chan), F32), pltpu.VMEM((SB, 8, chan), F32),
            pltpu.VMEM((chan, feat), BF16), pltpu.VMEM((2, HALF, half), F32), pltpu.VMEM((2, HALF, half), BF16),
            pltpu.VMEM((2, HALF, half), BF16), pltpu.VMEM(pt.shape, BF16), pltpu.VMEM(pt.shape, BF16),
            pltpu.VMEM(pt.shape, BF16),
            pltpu.SemaphoreType.DMA((rows // SB,)), pltpu.SemaphoreType.DMA, pltpu.SemaphoreType.DMA((8,)),
            pltpu.SemaphoreType.DMA((8,)),
        ],
        compiler_params=pltpu.CompilerParams(vmem_limit_bytes=26 * 2 ** 20, collective_id=layer, has_side_effects=True),
        cost_estimate=pl.CostEstimate(flops=2 * 10 ** 10, bytes_accessed=28 * 2 ** 20, transcendentals=0),
        name=f"k{layer}",
    )(*ins, w_dt, b_dt, a_log, d_skip, w_out, state)


def w_kernel(layer, st, *refs):
    out, sem = refs[-2:]
    step = st.shape[0] // 8

    def copy(i):
        rs = pl.ds(i * step, step)
        return pltpu.make_async_copy(st.at[rs], out.at[layer, rs], sem.at[i])

    for i in range(8):
        copy(i).start()
    for i in range(8):
        copy(i).wait()


def w_call(layer, st, shape, prev):
    args = [pltpu.with_memory_space_constraint(st, pltpu.VMEM)]
    specs = [VMEM]
    alias = {}
    if prev is not None:
        alias = {1: 0}
        args.append(prev)
        specs.append(ANY)
    return pl.pallas_call(
        functools.partial(w_kernel, layer), out_shape=jax.ShapeDtypeStruct(shape, F32),
        in_specs=specs, out_specs=ANY, input_output_aliases=alias,
        scratch_shapes=[pltpu.SemaphoreType.DMA((8,))],
        compiler_params=pltpu.CompilerParams(vmem_limit_bytes=2 ** 20),
        cost_estimate=pl.CostEstimate(flops=2 * 10 ** 10, bytes_accessed=42 * 2 ** 20, transcendentals=0),
        name=f"w{layer}",
    )(*args)


def fin_kernel(r_ref, *refs):
    out = refs[-1]
    core = lax.rem(lax.axis_index('tp'), 2)
    half = out.shape[1] // 2
    lo = pl.ds(pl.multiple_of(core * half, 128), half)
    hi = pl.ds(pl.multiple_of((1 - core) * half, 128), half)
    for k in range(2):
        u, up, v, vp = refs[4 * k:4 * k + 4]
        rs = slice(k * HALF, (k + 1) * HALF)
        out[rs, lo] = r_ref[rs, lo] + (u[...].astype(F32) + v[...].astype(F32))
        out[rs, hi] = r_ref[rs, hi] + (up[...].astype(F32) + vp[...].astype(F32))


def fin_call(r1, pieces):
    return pl.pallas_call(
        fin_kernel, out_shape=jax.ShapeDtypeStruct(r1.shape, F32), in_specs=[VMEM] * 9, out_specs=VMEM,
        compiler_params=pltpu.CompilerParams(vmem_limit_bytes=16 * 2 ** 20), name="fin",
    )(r1, *pieces[0], *pieces[1])


PART = [(0, 1), (1, 0), (2, 3), (3, 2)]
CROSS = [(0, 2), (2, 0), (1, 3), (3, 1)]


def solution(mesh):
    def step(residual, norm_w, w_in, conv_w, conv_b, w_x, w_dt, b_dt, a_log, d_skip, w_out, conv_state, ssm_state):
        w_xt = jnp.transpose(w_x, (0, 2, 1))
        conv_t = jnp.transpose(conv_state, (0, 2, 1, 3))
        in_w = (norm_w, w_in, conv_w, conv_b, w_xt)
        s_w = (w_dt, b_dt, a_log, d_skip, w_out)
        r = residual
        conv_out = None
        ssm_out = None
        pieces = None
        for layer in range(norm_w.shape[0]):
            got = in_call(layer, r, pieces, in_w, conv_t, conv_out)
            z, xc, pt, conv_out = got[:4]
            if pieces is not None:
                r = got[4]
            st, ua, ub, upa, upb, va, vpa = k_call(layer, pt, xc, z, s_w, ssm_state)
            vb = lax.ppermute(ub, 'tp', CROSS)
            ssm_out = w_call(layer, st, ssm_state.shape, ssm_out)
            vpb = lax.ppermute(vb, 'tp', PART)
            pieces = ((ua, upa, va, vpa), (ub, upb, vb, vpb))
        out = fin_call(r, pieces)
        return out, jnp.transpose(conv_out, (0, 2, 1, 3)), ssm_out

    cache_spec = P(None, 'dp', None, 'tp')
    in_specs = (P('dp', None), P(None, None), P(None, None, None, 'tp'), P(None, None, 'tp'), P(None, 'tp'), P(None, 'tp', None), P(None, None, 'tp'), P(None, 'tp'), P(None, None, 'tp'), P(None, 'tp'), P(None, 'tp', None), cache_spec, cache_spec)
    out_specs = (P('dp', None), cache_spec, cache_spec)
    return jax.shard_map(step, mesh=mesh, in_specs=in_specs, out_specs=out_specs, check_vma=False)
```

time: 171 us -> 136 us (0.80)
  waiting for transfers between devices: 51.3 us -> 11.1 us
  local copies, waits for them, and re-layouts: 3.08 us -> 21.7 us
  starting transfers between devices: 9.49 us -> 2.29 us
  Pallas kernels: 103 us -> 99.7 us
  other arithmetic: 2.92 us -> 0 us
    ppermute x14 -> x4, waiting for transfers between devices: 51.3 us -> 11.1 us  [the longest x2 9.51 us: step(): vb = lax.ppermute(ub, 'tp', CROSS)]
    unnamed x28 -> x36, local copies, waits for them, and re-layouts: 3.08 us -> 21.7 us
    ppermute x14 -> x4, starting transfers between devices: 9.49 us -> 2.29 us  [the longest x2 2.16 us: step(): vb = lax.ppermute(ub, 'tp', CROSS)]
    convert_element_type x2 -> x0, other arithmetic: 2.92 us -> none  [exchange(): u = (mine + got.astype(F32)).astype(BF16)]
    pallas_call x5 -> x7, Pallas kernels: 103 us -> 99.7 us  [the longest x2 49.7 us: k_call(): pl.pallas_call(functools.partial(k_kernel, layer), out_shape=[pltpu.VMEM(...]
  transfers between devices with their start and end apart: 14 -> 4, of which waited for: 10 -> 2; matrix products, arithmetic and copies ran while one was open for 0% -> 0% of each run, Pallas kernels for 0% -> 11%
where the time goes in v2:
time: 136 us
  Pallas kernels  99.7 us (73%)
  local copies, waits for them, and re-layouts  21.7 us (16%)
  waiting for transfers between devices  11.1 us (8%)
  starting transfers between devices  2.29 us (2%)
    pallas_call x2, Pallas kernels, k_call(): pl.pallas_call(functools.partial(k_kernel, layer), out_shape=[pltpu.VMEM(...  49.7 us
    pallas_call x2, Pallas kernels, in_call(): pl.pallas_call(functools.partial(in_kernel, layer, has_o), out_shape=outs...  33.6 us
    unnamed x36, local copies, waits for them, and re-layouts  21.7 us
    pallas_call x2, Pallas kernels, w_call(): pl.pallas_call(functools.partial(w_kernel, layer), out_shape=jax.ShapeDty...  14.4 us
    ppermute x2, waiting for transfers between devices, step(): vb = lax.ppermute(ub, 'tp', CROSS)  9.51 us
  transfers between devices with their start and end apart: 4, of which 2 were waited for; matrix products, arithmetic and copies ran while one was open for 0% of the time, Pallas kernels for 11%

profile of v2, /device:TPU:0, one launch (start us, length us, event | category | flops | bytes accessed | tf_op | source)
XLA Modules:
  0.0 135.6 jit_solution(18362644169943525219)
XLA Ops:
  0.6 0.0 copy-start
  0.6 2.1 %copy-done = bf16[2,256,3,1280]{3,1,2,0:T(8,128)(2,1)S(1)} copy-done((bf16[2,256,3,1280]{3,1,2,0:T(8,128)(2,1)S(1)}, bf16[2,256,3,1280]{3,1,2,0:T(8,128)(2,1)}, u32[]{:S(2)}) %copy-start) | copy-done | bytes 3932184
  2.7 0.0 copy-start.2
  2.8 1.7 %copy-done.2 = f32[256,2560]{1,0:T(8,128)S(1)} copy-done((f32[256,2560]{1,0:T(8,128)S(1)}, f32[256,2560]{1,0:T(8,128)}, u32[]{:S(2)}) %copy-start.2) | copy-done | bytes 2621464
  4.5 0.0 copy-start.4
  4.5 1.2 copy-done.4
  5.7 0.0 copy-start.6
  5.7 0.7 copy-done.6
  6.4 0.0 copy-start.8
  6.4 0.7 copy-done.8
  7.1 0.0 copy-start.10
  7.1 0.7 copy-done.10
  7.8 0.0 copy-start.12
  7.8 0.0 copy-start.13
  7.8 16.3 %in0.1 = (bf16[256,1280]{1,0:T(8,128)(2,1)S(1)}, bf16[256,1280]{1,0:T(8,128)(2,1)S(1)}, bf16[192,256]{1,0:T(8,128)(2,1)S(1)}, bf16[2,3,256,1280]{3,2,1,0:T(8,128)(2,1)}) custom-call(f32[256,2560]{1,0:T(8,128)S(1)} %copy-done.2, bf16[2,2560]{1,0:T(2,128)(2,1)S(1)} %copy-done.8, bf16[2,2560,2,1280]{3,2,1,0:T(2,128)(2,1)} %refs_10_.1, ...), custom_call_target="tpu_custom_call" | custom-call | flops 6710886400 | bytes 20971520 | tf_op jit(solution)/shard_map/in0/pallas_call | solution.py:127
  24.2 0.0 copy-done.12
  24.2 0.0 copy-done.13
  24.2 0.0 copy-done.14
  24.2 0.0 copy-done.15
  24.2 0.0 copy-start.1
  24.2 0.0 copy-start.3
  24.2 0.0 copy-start.5
  24.2 0.0 copy-start.7
  24.3 0.0 copy-start.9
  24.3 0.0 copy-start.11
  24.3 25.8 %k0.1 = (f32[256,16,1280]{2,1,0:T(8,128)S(1)}, bf16[128,1280]{1,0:T(8,128)(2,1)S(1)}, bf16[128,1280]{1,0:T(8,128)(2,1)S(1)}, bf16[128,1280]{1,0:T(8,128)(2,1)S(1...) custom-call(bf16[192,256]{1,0:T(8,128)(2,1)S(1)} %get-tuple-element.26.pt, ...), custom_call_target="tpu_custom_call" | custom-call | flops 20000000000 | bytes 29360128 | tf_op jit(solution)/shard_map/k0/pallas_call | solution.py:281
  50.1 0.0 copy-start.16
  50.1 7.5 %copy-done.16 = f32[256,16,1280]{2,1,0:T(8,128)} copy-done((f32[256,16,1280]{2,1,0:T(8,128)}, f32[256,16,1280]{2,1,0:T(8,128)S(1)}, u32[]{:S(2)}) %copy-start.16) | copy-done | bytes 20971544
  57.7 0.5 collective-permute-start
  58.2 9.5 %collective-permute-done.refs_7_ = bf16[128,1280]{1,0:T(8,128)(2,1)S(1)} collective-permute-done((bf16[128,1280]{1,0:T(8,128)(2,1)S(1)}, bf16[128,1280]{1,0:T(8,128)(2,1)S(1)}, u32[]{:S(2)}, u32[]{:S(2)}) %collective-permute-start) | collective-permute-done | bytes 327712 | tf_op jit(solution)/shard_map/ppermute | solution.py:372
  67.7 0.0 collective-permute-start.1
  67.7 1.6 %collective-permute-done.1.refs_8_ = bf16[128,1280]{1,0:T(8,128)(2,1)S(1)} collective-permute-done((bf16[128,1280]{1,0:T(8,128)(2,1)S(1)}, bf16[128,1280]{1,0:T(8,128)(2,1)S(1)}, u32[]{:S(2)}, u32[]{:S(2)}) %collective-permute-start.1) | collective-permute-done | bytes 327712 | tf_op jit(solution)/shard_map/ppermute | solution.py:374
  69.3 0.0 copy-done.1
  69.3 0.0 copy-done.3
  69.3 0.0 copy-done.5
  69.3 0.0 copy-done.7
  69.3 0.0 copy-done.9
  69.3 0.0 copy-done.11
  69.3 17.3 %in1.1 = (bf16[256,1280]{1,0:T(8,128)(2,1)S(1)}, bf16[256,1280]{1,0:T(8,128)(2,1)S(1)}, bf16[192,256]{1,0:T(8,128)(2,1)S(1)}, bf16[2,3,256,1280]{3,2,1,0:T(8,128)(2,1)}, f32[256,2560]{1,0:T(8,128)S(1)}) custom-call(f32[256,2560]{1,0:T(8,128)S(1)} %copy-done.3, bf16[128,1280]{1,0:T(8,128)(2,1)S(1)} %get-tuple-element.29.refs_1_, ...), custom_call_target="tpu_custom_call", output_to_operand_aliasing={{3}: (15, {})} | custom-call | flops 6710886400 | bytes 20971520 | tf_op jit(solution)/shard_map/in1/pallas_call | solution.py:127
  86.6 23.9 %k1.1 = (f32[256,16,1280]{2,1,0:T(8,128)S(1)}, bf16[128,1280]{1,0:T(8,128)(2,1)S(1)}, bf16[128,1280]{1,0:T(8,128)(2,1)S(1)}, bf16[128,1280]{1,0:T(8,128)(2,1)S(1...) custom-call(bf16[192,256]{1,0:T(8,128)(2,1)S(1)} %get-tuple-element.37.pt, ...), custom_call_target="tpu_custom_call" | custom-call | flops 20000000000 | bytes 29360128 | tf_op jit(solution)/shard_map/k1/pallas_call | solution.py:281
  110.5 1.7 %collective-permute-start.2 = (bf16[128,1280]{1,0:T(8,128)(2,1)S(1)}, bf16[128,1280]{1,0:T(8,128)(2,1)S(1)}, u32[]{:S(2)}, u32[]{:S(2)}) collective-permute-start(bf16[128,1280]{1,0:T(8,128)(2,1)S(1)} %get-tuple-element.44.refs_4_), channel_id=1, source_target_pairs={{0,2},{2,0},{1,3},{3,1},{4,6},{6,4},{5,7},{7,5}} | collective-permute-start | bytes 983048 | tf_op jit(solution)/shard_map/ppermute | solution.py:372
  112.2 7.0 %copy-done.17 = f32[256,16,1280]{2,1,0:T(8,128)S(1)} copy-done((f32[256,16,1280]{2,1,0:T(8,128)S(1)}, f32[256,16,1280]{2,1,0:T(8,128)}, u32[]{:S(2)}) %copy-start.17) | copy-done | bytes 20971544
  119.1 7.2 %w0.1.refs_0_ = f32[2,256,16,1280]{3,2,1,0:T(8,128)} custom-call(f32[256,16,1280]{2,1,0:T(8,128)S(1)} %copy-done.17), custom_call_target="tpu_custom_call" | custom-call | flops 20000000000 | bytes 44040192 | tf_op jit(solution)/shard_map/w0/pallas_call | solution.py:322
  126.4 0.0 collective-permute-done.2.refs_6_
  126.4 0.1 collective-permute-start.3
  126.5 7.2 %w1.1 = f32[2,256,16,1280]{3,2,1,0:T(8,128)} custom-call(f32[256,16,1280]{2,1,0:T(8,128)S(1)} %get-tuple-element.47.st, f32[2,256,16,1280]{3,2,1,0:T(8,128)} %w0.1.refs_0_), custom_call_target="tpu_custom_call", output_to_operand_aliasing={{}: (1, {})} | custom-call | flops 20000000000 | bytes 44040192 | tf_op jit(solution)/shard_map/w1/pallas_call | solution.py:322
  133.7 0.0 collective-permute-done.3.refs_7_
  133.8 1.9 %fin.1 = f32[256,2560]{1,0:T(8,128)} custom-call(f32[256,2560]{1,0:T(8,128)S(1)} %get-tuple-element.36.r_ref, bf16[128,1280]{1,0:T(8,128)(2,1)S(1)} %get-tuple-element.40.refs_0_, bf16[128,1280]{1,0:T(8,128)(2,1)S(1)} %get-tuple-element.41.refs_1_, bf16[128,1280]{1,0:T(8,128)(2,1)S(1)} %get-tuple-element.42.refs_2_, ...), custom_call_target="tpu_custom_call" | custom-call | tf_op jit(solution)/shard_map/fin/pallas_call | solution.py:346
  (3 shorter events, 0.0 us)
Async XLA Ops:
  0.6 2.1 %copy-start = (bf16[2,256,3,1280]{3,1,2,0:T(8,128)(2,1)S(1)}, bf16[2,256,3,1280]{3,1,2,0:T(8,128)(2,1)}, u32[]{:S(2)}) copy-start(bf16[2,256,3,1280]{3,1,2,0:T(8,128)(2,1)} %param.24) | copy-start | bytes 11796484
  2.7 1.7 %copy-start.2 = (f32[256,2560]{1,0:T(8,128)S(1)}, f32[256,2560]{1,0:T(8,128)}, u32[]{:S(2)}) copy-start(f32[256,2560]{1,0:T(8,128)} %refs_0_.3) | copy-start | bytes 7864324
  4.5 1.2 copy-start.4
  5.7 0.7 copy-start.6
  6.4 0.7 copy-start.8
  7.1 0.7 copy-start.10
  7.8 16.4 %copy-start.12 = (bf16[2,160,1280]{2,1,0:T(8,128)(2,1)S(1)}, bf16[2,160,1280]{2,1,0:T(8,128)(2,1)}, u32[]{:S(2)}) copy-start(bf16[2,160,1280]{2,1,0:T(8,128)(2,1)} %w_dt.3) | copy-start | bytes 2457604
  7.8 16.4 %copy-start.13 = (f32[2,16,1280]{2,1,0:T(8,128)S(1)}, f32[2,16,1280]{2,1,0:T(8,128)}, u32[]{:S(2)}) copy-start(f32[2,16,1280]{2,1,0:T(8,128)} %a_log.3) | copy-start | bytes 491524
  7.8 16.4 %copy-start.14 = (f32[2,1280]{1,0:T(2,128)S(1)}, f32[2,1280]{1,0:T(2,128)}, u32[]{:S(2)}) copy-start(f32[2,1280]{1,0:T(2,128)} %b_dt.3) | copy-start | bytes 30724
  7.8 16.4 %copy-start.15 = (f32[2,1280]{1,0:T(2,128)S(1)}, f32[2,1280]{1,0:T(2,128)}, u32[]{:S(2)}) copy-start(f32[2,1280]{1,0:T(2,128)} %d_skip.3) | copy-start | bytes 30724
  24.2 45.1 %copy-start.1 = (bf16[2,256,3,1280]{3,1,2,0:T(8,128)(2,1)S(1)}, bf16[2,256,3,1280]{3,1,2,0:T(8,128)(2,1)}, u32[]{:S(2)}) copy-start(bf16[2,256,3,1280]{3,1,2,0:T(8,128)(2,1)} %param.24) | copy-start | bytes 11796484
  24.2 45.1 %copy-start.3 = (f32[256,2560]{1,0:T(8,128)S(1)}, f32[256,2560]{1,0:T(8,128)}, u32[]{:S(2)}) copy-start(f32[256,2560]{1,0:T(8,128)} %refs_0_.3) | copy-start | bytes 7864324
  24.2 45.1 %copy-start.5 = (bf16[2,1280,192]{1,2,0:T(8,128)(2,1)S(1)}, bf16[2,1280,192]{1,2,0:T(8,128)(2,1)}, u32[]{:S(2)}) copy-start(bf16[2,1280,192]{1,2,0:T(8,128)(2,1)} %param.18) | copy-start | bytes 2949124
  24.2 45.1 %copy-start.7 = (bf16[2,4,1280]{2,1,0:T(4,128)(2,1)S(1)}, bf16[2,4,1280]{2,1,0:T(4,128)(2,1)}, u32[]{:S(2)}) copy-start(bf16[2,4,1280]{2,1,0:T(4,128)(2,1)} %refs_11_.1) | copy-start | bytes 61444
  24.3 45.1 %copy-start.9 = (bf16[2,2560]{1,0:T(2,128)(2,1)S(1)}, bf16[2,2560]{1,0:T(2,128)(2,1)}, u32[]{:S(2)}) copy-start(bf16[2,2560]{1,0:T(2,128)(2,1)} %refs_9_.1) | copy-start | bytes 30724
  24.3 45.1 %copy-start.11 = (bf16[2,1280]{1,0:T(2,128)(2,1)S(1)}, bf16[2,1280]{1,0:T(2,128)(2,1)}, u32[]{:S(2)}) copy-start(bf16[2,1280]{1,0:T(2,128)(2,1)} %refs_12_.1) | copy-start | bytes 15364
  50.1 7.5 %copy-start.16 = (f32[256,16,1280]{2,1,0:T(8,128)}, f32[256,16,1280]{2,1,0:T(8,128)S(1)}, u32[]{:S(2)}) copy-start(f32[256,16,1280]{2,1,0:T(8,128)S(1)} %get-tuple-element.48.st) | copy-start | bytes 62914564
  57.7 10.0 %collective-permute-start = (bf16[128,1280]{1,0:T(8,128)(2,1)S(1)}, bf16[128,1280]{1,0:T(8,128)(2,1)S(1)}, u32[]{:S(2)}, u32[]{:S(2)}) collective-permute-start(bf16[128,1280]{1,0:T(8,128)(2,1)S(1)} %get-tuple-element.33.refs_5_), channel_id=1, source_target_pairs={{0,2},{2,0},{1,3},{3,1},{4,6},{6,4},{5,7},{7,5}} | collective-permute-start | bytes 983048 | tf_op jit(solution)/shard_map/ppermute | solution.py:372
  67.7 1.6 %collective-permute-start.1 = (bf16[128,1280]{1,0:T(8,128)(2,1)S(1)}, bf16[128,1280]{1,0:T(8,128)(2,1)S(1)}, u32[]{:S(2)}, u32[]{:S(2)}) collective-permute-start(bf16[128,1280]{1,0:T(8,128)(2,1)S(1)} %collective-permute-done.refs_7_), channel_id=1, source_target_pairs={{0,1},{1,0},{2,3},{3,2},{4,5},{5,4},{6,7},{7,6}} | collective-permute-start | bytes 983048 | tf_op jit(solution)/shard_map/ppermute | solution.py:374
  110.5 15.9 %collective-permute-start.2 = (bf16[128,1280]{1,0:T(8,128)(2,1)S(1)}, bf16[128,1280]{1,0:T(8,128)(2,1)S(1)}, u32[]{:S(2)}, u32[]{:S(2)}) collective-permute-start(bf16[128,1280]{1,0:T(8,128)(2,1)S(1)} %get-tuple-element.44.refs_4_), channel_id=1, source_target_pairs={{0,2},{2,0},{1,3},{3,1},{4,6},{6,4},{5,7},{7,5}} | collective-permute-start | bytes 983048 | tf_op jit(solution)/shard_map/ppermute | solution.py:372
  112.2 7.0 %copy-start.17 = (f32[256,16,1280]{2,1,0:T(8,128)S(1)}, f32[256,16,1280]{2,1,0:T(8,128)}, u32[]{:S(2)}) copy-start(f32[256,16,1280]{2,1,0:T(8,128)} %copy-done.16) | copy-start | bytes 62914564
  126.4 7.4 %collective-permute-start.3 = (bf16[128,1280]{1,0:T(8,128)(2,1)S(1)}, bf16[128,1280]{1,0:T(8,128)(2,1)S(1)}, u32[]{:S(2)}, u32[]{:S(2)}) collective-permute-start(bf16[128,1280]{1,0:T(8,128)(2,1)S(1)} %collective-permute-done.2.refs_6_), channel_id=1, source_target_pairs={{0,1},{1,0},{2,3},{3,2},{4,5},{5,4},{6,7},{7,6}} | collective-permute-start | bytes 983048 | tf_op jit(solution)/shard_map/ppermute | solution.py:374

commit v3 on v2

--- a/solution.py
+++ b/solution.py
@@ -10,7 +10,7 @@
 
 F32 = jnp.float32
 BF16 = jnp.bfloat16
-ANY = pl.BlockSpec(memory_space=pl.ANY)
+ANY = pl.BlockSpec(memory_space=pltpu.HBM)
 VMEM = pl.BlockSpec(memory_space=pltpu.VMEM)
 NCH = 256
 SB = 16
@@ -37,11 +37,11 @@
     norm_w, w_in, conv_w, conv_b, w_x, conv_st = refs[:6]
     refs = refs[6:]
     if layer > 0:
-        refs.pop(0)
+        refs = refs[2:]
     z_out, xc_out, p_out, conv_out = refs[:4]
     refs = refs[4:]
     r_out = refs.pop(0) if has_o else None
-    wbuf, hx, rbuf, cbuf, xbuf, rsem, wsem, csem, osem = refs
+    wbuf, hx, hbuf, ex_s, p_acc, rbuf, cbuf, xbuf, rsem, wsem, csem, osem = refs
     rows, feat = rbuf.shape
     nchunk = wbuf.shape[0]
     w_flat = w_in.reshape(w_in.shape[0], 2 * feat, w_in.shape[3])
@@ -52,39 +52,62 @@
     x_copy = pltpu.make_async_copy(xbuf, conv_out.at[layer, 2], osem.at[2])
 
     def w_copy(c):
-        return pltpu.make_async_copy(w_flat.at[layer, :, pl.ds(c * NCH, NCH)], wbuf.at[c], wsem.at[c])
+        cols = pl.ds(pl.multiple_of(c * NCH, NCH), NCH)
+        return pltpu.make_async_copy(w_flat.at[layer, :, cols], wbuf.at[c], wsem.at[c])
 
     r_copy.start()
     w_copy(0).start()
     w_copy(1).start()
+    ex_s[...] = expand_matrix()
+    p_acc[...] = jnp.zeros_like(p_acc)
     r_copy.wait()
     c_copy.start()
+    nw = norm_w[layer:layer + 1, :].astype(F32)
+    half = feat // 2
     if has_o:
         core = lax.rem(lax.axis_index('tp'), 2)
-        half = feat // 2
         lo = pl.ds(pl.multiple_of(core * half, 128), half)
         hi = pl.ds(pl.multiple_of((1 - core) * half, 128), half)
+
         for k, (u, up, v, vp) in enumerate(pieces):
-            rs = slice(k * HALF, (k + 1) * HALF)
-            rbuf[rs, lo] = rbuf[rs, lo] + (u[...].astype(F32) + v[...].astype(F32))
-            rbuf[rs, hi] = rbuf[rs, hi] + (up[...].astype(F32) + vp[...].astype(F32))
+            def add(i, carry, k=k, u=u, up=up, v=v, vp=vp):
+                src = pl.ds(pl.multiple_of(i * 32, 32), 32)
+                dst = pl.ds(pl.multiple_of(i * 32, 32) + k * HALF, 32)
+                rbuf[dst, lo] = rbuf[dst, lo] + (u[src, :].astype(F32) + v[src, :].astype(F32))
+                rbuf[dst, hi] = rbuf[dst, hi] + (up[src, :].astype(F32) + vp[src, :].astype(F32))
+                return carry
+
+            lax.fori_loop(0, HALF // 32, add, 0)
         pltpu.make_async_copy(rbuf, r_out, osem.at[0]).start()
-    r = rbuf[...]
-    inv = lax.rsqrt(jnp.mean(r * r, axis=-1, keepdims=True) + 1e-5)
-    h = (r * inv * norm_w[layer:layer + 1, :].astype(F32)).astype(BF16)
-    ex = expand_matrix()
-    for j in range(feat // 128):
-        e = jnp.dot(h[:, j * 128:(j + 1) * 128], ex, preferred_element_type=F32).astype(BF16)
-        hx[0:rows, j * 256:(j + 1) * 256] = e[:, :256]
-        hx[rows:2 * rows, j * 256:(j + 1) * 256] = e[:, 256:]
+
+    def norm(i, carry):
+        rs = pl.ds(pl.multiple_of(i * 32, 32), 32)
+        r = rbuf[rs, :]
+        inv = lax.rsqrt(jnp.mean(r * r, axis=-1, keepdims=True) + 1e-5)
+        hbuf[rs, :] = (r * inv * nw).astype(BF16)
+        return carry
+
+    lax.fori_loop(0, rows // 32, norm, 0)
+
+    def expand(j, carry):
+        e = jnp.dot(hbuf[:, pl.ds(pl.multiple_of(j * 128, 128), 128)], ex_s[...], preferred_element_type=F32).astype(BF16)
+        cols = pl.ds(pl.multiple_of(j * 256, 256), 256)
+        hx[0:rows, cols] = e[:, :256]
+        hx[rows:2 * rows, cols] = e[:, 256:]
+        return carry
+
+    lax.fori_loop(0, feat // 128, expand, 0)
     c_copy.wait()
     state_copy.start()
-    p_acc = jnp.zeros((w_x.shape[1], rows), F32)
-    for c in range(nchunk):
+
+    def chunk(c, carry):
         w_copy(c).wait()
-        if c + 2 < nchunk:
+
+        @pl.when(c + 2 < nchunk)
+        def _():
             w_copy(c + 2).start()
-        sl = slice(c * NCH, (c + 1) * NCH)
+
+        sl = pl.ds(pl.multiple_of(c * NCH, NCH), NCH)
         acc = jnp.dot(hx[...], wbuf[c], preferred_element_type=F32)
         x = acc[:rows].astype(BF16)
         z_out[:, sl] = acc[rows:].astype(BF16)
@@ -95,16 +118,19 @@
         pre = pre + conv_b[layer:layer + 1, sl].astype(F32)
         xc = silu(pre).astype(BF16)
         xc_out[:, sl] = xc
-        p_acc = p_acc + lax.dot_general(w_x[layer, :, sl], xc, (((1,), (1,)), ((), ())), preferred_element_type=F32)
-    p_out[...] = p_acc.astype(BF16)
+        p_acc[...] += lax.dot_general(w_x[layer, :, sl], xc, (((1,), (1,)), ((), ())), preferred_element_type=F32)
+        return carry
+
+    lax.fori_loop(0, nchunk, chunk, 0)
     x_copy.start()
+    p_out[...] = p_acc[...].astype(BF16)
     x_copy.wait()
     state_copy.wait()
     if has_o:
         pltpu.make_async_copy(rbuf, r_out, osem.at[0]).wait()
 
 
-def in_call(layer, residual, pieces, weights, conv_st, conv_prev):
+def in_call(layer, residual, pieces, weights, conv_st, conv_prev, ssm_prev):
     norm_w, w_in, conv_w, conv_b, w_x = weights
     has_o = pieces is not None
     rows, feat = residual.shape
@@ -115,8 +141,8 @@
     alias = {}
     if layer > 0:
         alias = {len(args): 3}
-        args.append(conv_prev)
-        specs.append(ANY)
+        args += [conv_prev, ssm_prev]
+        specs += [ANY, ANY]
     outs = [pltpu.VMEM((rows, chan), BF16), pltpu.VMEM((rows, chan), BF16),
             pltpu.VMEM((w_x.shape[1], rows), BF16), jax.ShapeDtypeStruct(conv_st.shape, BF16)]
     out_specs = [VMEM, VMEM, VMEM, ANY]
@@ -130,13 +156,16 @@
         scratch_shapes=[
             pltpu.VMEM((nchunk, 2 * feat, NCH), BF16),
             pltpu.VMEM((2 * rows, 2 * feat), BF16),
+            pltpu.VMEM((rows, feat), BF16),
+            pltpu.VMEM((128, 512), BF16),
+            pltpu.VMEM((w_x.shape[1], rows), F32),
             pltpu.VMEM((rows, feat), F32),
             pltpu.VMEM((3, rows, chan), BF16),
             pltpu.VMEM((rows, chan), BF16),
             pltpu.SemaphoreType.DMA, pltpu.SemaphoreType.DMA((nchunk,)), pltpu.SemaphoreType.DMA,
             pltpu.SemaphoreType.DMA((3,)),
         ],
-        compiler_params=pltpu.CompilerParams(vmem_limit_bytes=40 * 2 ** 20),
+        compiler_params=pltpu.CompilerParams(vmem_limit_bytes=60 * 2 ** 20),
         cost_estimate=pl.CostEstimate(flops=rows * 2 * feat * 2 * chan * 2, bytes_accessed=20 * 2 ** 20, transcendentals=0),
         name=f"in{layer}",
     )(*args)
@@ -210,11 +239,45 @@
 
     lane = lax.broadcasted_iota(jnp.int32, (nst, 128), 1)
     row = lax.broadcasted_iota(jnp.int32, (nst, 128), 0)
+    half = wo.shape[1] // 2
+    lo = pl.ds(pl.multiple_of(core * half, 128), half)
+    hi = pl.ds(pl.multiple_of((1 - core) * half, 128), half)
+    qrows = rows // 4
+    per_q = nblk // 4
+
+    def red(q):
+        return send(theirs.at[q], got.at[q], 2 + q, partner)
+
+    def part_of(q):
+        u, up = ((ua, upa), (ub, upb))[q // 2]
+        rs = pl.ds((q % 2) * qrows, qrows)
+        return u.at[rs], up.at[rs]
+
+    def cross(q):
+        rs = pl.ds(q * qrows, qrows)
+        return send(ua.at[rs], va.at[rs], 6 + q, other)
+
+    def to_partner(q):
+        u, up = part_of(q)
+        return send(u, up, 8 + q, partner)
+
+    def forward(q):
+        rs = pl.ds(q * qrows, qrows)
+        return send(va.at[rs], vpa.at[rs], 12 + q, partner)
+
+    def reduce_quarter(q):
+        red(q).wait_recv()
+        u, _ = part_of(q)
+        u[...] = (mine[q] + got[q].astype(F32)).astype(BF16)
+        if q < 2:
+            cross(q).start()
+        to_partner(q).start()
 
     def block(i, carry):
         st_copy(i).wait()
         base = pl.multiple_of(i * SB, SB)
         sl = pl.ds(base, SB)
+        ybase = pl.multiple_of(lax.rem(i, per_q) * SB, SB)
         dt = dt_s[sl, :]
         dtx = dtx_s[sl, :]
         bc = bc_s[sl, :]
@@ -228,46 +291,46 @@
             t = s * ccol
             part[b] = t[0:8] + t[8:16]
         for g in range(SB // 8):
-            y_s[pl.ds(base + 8 * g, 8), :] = sublane_sums([part[8 * g + k] for k in range(8)])
+            y_s[pl.ds(ybase + 8 * g, 8), :] = sublane_sums([part[8 * g + k] for k in range(8)])
+
+        @pl.when(i == per_q - 1)
+        def _():
+            w_copy.wait()
+
+        @pl.when(lax.rem(i, per_q) == per_q - 1)
+        def _():
+            q = i // per_q
+            rs = pl.ds(pl.multiple_of(q * qrows, qrows), qrows)
+            y = y_s[...] + d_skip[layer:layer + 1, :] * xc_ref[rs, :].astype(F32)
+            yg = (y * silu(z_ref[rs, :].astype(F32))).astype(BF16)
+            theirs[q] = jnp.dot(yg, wo[:, hi], preferred_element_type=F32).astype(BF16)
+            red(q).start()
+            mine[q] = jnp.dot(yg, wo[:, lo], preferred_element_type=F32)
+
+        for q in range(3):
+            @pl.when(i == (q + 1) * per_q + 1)
+            def _(q=q):
+                reduce_quarter(q)
+
         return carry
 
-    half = wo.shape[1] // 2
-    lo = pl.ds(pl.multiple_of(core * half, 128), half)
-    hi = pl.ds(pl.multiple_of((1 - core) * half, 128), half)
-
-    def project(k):
-        rs = pl.ds(k * HALF, HALF)
-        y = y_s[rs, :] + d_skip[layer:layer + 1, :] * xc_ref[rs, :].astype(F32)
-        yg = (y * silu(z_ref[rs, :].astype(F32))).astype(BF16)
-        theirs[k] = jnp.dot(yg, wo[:, hi], preferred_element_type=F32).astype(BF16)
-        red = send(theirs.at[k], got.at[k], 2 + k, partner)
-        red.start()
-        mine[k] = jnp.dot(yg, wo[:, lo], preferred_element_type=F32)
-        return red
-
-    lax.fori_loop(0, nblk // 2, block, 0)
-    w_copy.wait()
-    red_a = project(0)
-    lax.fori_loop(nblk // 2, 5 * nblk // 8, block, 0)
-    red_a.wait_recv()
-    ua[...] = (mine[0] + got[0].astype(F32)).astype(BF16)
-    cross_a = send(ua, va, 4, other)
-    cross_a.start()
-    up_a = send(ua, upa, 5, partner)
-    up_a.start()
-    lax.fori_loop(5 * nblk // 8, nblk, block, 0)
-    red_b = project(1)
-    red_b.wait_recv()
-    ub[...] = (mine[1] + got[1].astype(F32)).astype(BF16)
-    up_b = send(ub, upb, 6, partner)
-    up_b.start()
-    cross_a.wait_recv()
-    fwd_a = send(va, vpa, 7, partner)
-    fwd_a.start()
-    for c in (up_a, up_b, fwd_a):
-        c.wait_recv()
-    for c in (p1, p2, red_a, red_b, cross_a, up_a, up_b, fwd_a):
-        c.wait_send()
+    lax.fori_loop(0, nblk, block, 0)
+    reduce_quarter(3)
+    for q in range(2):
+        cross(q).wait_recv()
+        forward(q).start()
+    for q in range(4):
+        to_partner(q).wait_recv()
+    for q in range(2):
+        forward(q).wait_recv()
+    p1.wait_send()
+    p2.wait_send()
+    for q in range(4):
+        red(q).wait_send()
+        to_partner(q).wait_send()
+    for q in range(2):
+        cross(q).wait_send()
+        forward(q).wait_send()
 
 
 def k_call(layer, pt, xc, z, weights, state):
@@ -284,12 +347,12 @@
         in_specs=[VMEM] * 7 + [ANY, ANY], out_specs=[VMEM] * 7,
         scratch_shapes=[
             pltpu.VMEM((rows, chan), F32), pltpu.VMEM((rows, chan), F32), pltpu.VMEM((rows, 128), F32),
-            pltpu.VMEM((nst, chan), F32), pltpu.VMEM((rows, chan), F32), pltpu.VMEM((SB, 8, chan), F32),
-            pltpu.VMEM((chan, feat), BF16), pltpu.VMEM((2, HALF, half), F32), pltpu.VMEM((2, HALF, half), BF16),
-            pltpu.VMEM((2, HALF, half), BF16), pltpu.VMEM(pt.shape, BF16), pltpu.VMEM(pt.shape, BF16),
+            pltpu.VMEM((nst, chan), F32), pltpu.VMEM((rows // 4, chan), F32), pltpu.VMEM((SB, 8, chan), F32),
+            pltpu.VMEM((chan, feat), BF16), pltpu.VMEM((4, rows // 4, half), F32), pltpu.VMEM((4, rows // 4, half), BF16),
+            pltpu.VMEM((4, rows // 4, half), BF16), pltpu.VMEM(pt.shape, BF16), pltpu.VMEM(pt.shape, BF16),
             pltpu.VMEM(pt.shape, BF16),
-            pltpu.SemaphoreType.DMA((rows // SB,)), pltpu.SemaphoreType.DMA, pltpu.SemaphoreType.DMA((8,)),
-            pltpu.SemaphoreType.DMA((8,)),
+            pltpu.SemaphoreType.DMA((rows // SB,)), pltpu.SemaphoreType.DMA, pltpu.SemaphoreType.DMA((14,)),
+            pltpu.SemaphoreType.DMA((14,)),
         ],
         compiler_params=pltpu.CompilerParams(vmem_limit_bytes=26 * 2 ** 20, collective_id=layer, has_side_effects=True),
         cost_estimate=pl.CostEstimate(flops=2 * 10 ** 10, bytes_accessed=28 * 2 ** 20, transcendentals=0),
@@ -298,7 +361,8 @@
 
 
 def w_kernel(layer, st, *refs):
-    out, sem = refs[-2:]
+    out, flag, sem = refs[-3:]
+    flag[...] = jnp.zeros_like(flag)
     step = st.shape[0] // 8
 
     def copy(i):
@@ -320,8 +384,9 @@
         args.append(prev)
         specs.append(ANY)
     return pl.pallas_call(
-        functools.partial(w_kernel, layer), out_shape=jax.ShapeDtypeStruct(shape, F32),
-        in_specs=specs, out_specs=ANY, input_output_aliases=alias,
+        functools.partial(w_kernel, layer),
+        out_shape=[jax.ShapeDtypeStruct(shape, F32), jax.ShapeDtypeStruct((8, 128), F32)],
+        in_specs=specs, out_specs=[ANY, VMEM], input_output_aliases=alias,
         scratch_shapes=[pltpu.SemaphoreType.DMA((8,))],
         compiler_params=pltpu.CompilerParams(vmem_limit_bytes=2 ** 20),
         cost_estimate=pl.CostEstimate(flops=2 * 10 ** 10, bytes_accessed=42 * 2 ** 20, transcendentals=0),
@@ -364,13 +429,14 @@
         ssm_out = None
         pieces = None
         for layer in range(norm_w.shape[0]):
-            got = in_call(layer, r, pieces, in_w, conv_t, conv_out)
+            got = in_call(layer, r, pieces, in_w, conv_t, conv_out, ssm_out)
             z, xc, pt, conv_out = got[:4]
             if pieces is not None:
                 r = got[4]
             st, ua, ub, upa, upb, va, vpa = k_call(layer, pt, xc, z, s_w, ssm_state)
             vb = lax.ppermute(ub, 'tp', CROSS)
-            ssm_out = w_call(layer, st, ssm_state.shape, ssm_out)
+            ssm_out, flag = w_call(layer, st, ssm_state.shape, ssm_out)
+            vb, _ = lax.optimization_barrier((vb, flag))
             vpb = lax.ppermute(vb, 'tp', PART)
             pieces = ((ua, upa, va, vpa), (ub, upb, vb, vpb))
         out = fin_call(r, pieces)

time: 136 us -> 125 us (0.919)
  local copies, waits for them, and re-layouts: 21.7 us -> 0.77 us
  waiting for transfers between devices: 11.1 us -> 16.3 us
  Pallas kernels: 99.7 us -> 104 us
    unnamed x36 -> x26, local copies, waits for them, and re-layouts: 21.7 us -> 0.77 us
    ppermute x2, waiting for transfers between devices: 9.51 us -> 16.3 us  [step(): vb = lax.ppermute(ub, 'tp', CROSS)]
    pallas_call x2, Pallas kernels: 33.6 us -> 37.4 us  [in_call(): pl.pallas_call(functools.partial(in_kernel, layer, has_o), out_shape=outs...]
    ppermute x2, waiting for transfers between devices: 1.63 us -> 0.01 us  [step(): vpb = lax.ppermute(vb, 'tp', PART)]
    pallas_call x2, Pallas kernels: 14.4 us -> 15.9 us  [w_call(): pl.pallas_call(functools.partial(w_kernel, layer), out_shape=[jax.ShapeDt...]
  transfers between devices with their start and end apart: 4 -> 4, of which waited for: 2 -> 2; matrix products, arithmetic and copies ran while one was open for 0% -> 0% of each run, Pallas kernels for 11% -> 13%
where the time goes in v3:
time: 125 us
  Pallas kernels  104 us (83%)
  waiting for transfers between devices  16.3 us (13%)
  starting transfers between devices  3.25 us (3%)
    pallas_call x2, Pallas kernels, k_call(): pl.pallas_call(functools.partial(k_kernel, layer), out_shape=[pltpu.VMEM(...  48.7 us
    pallas_call x2, Pallas kernels, in_call(): pl.pallas_call(functools.partial(in_kernel, layer, has_o), out_shape=outs...  37.4 us
    ppermute x2, waiting for transfers between devices, step(): vb = lax.ppermute(ub, 'tp', CROSS)  16.3 us
    pallas_call x2, Pallas kernels, w_call(): pl.pallas_call(functools.partial(w_kernel, layer), out_shape=[jax.ShapeDt...  15.9 us
    ppermute x2, starting transfers between devices, step(): vb = lax.ppermute(ub, 'tp', CROSS)  3.25 us
  transfers between devices with their start and end apart: 4, of which 2 were waited for; matrix products, arithmetic and copies ran while one was open for 0% of the time, Pallas kernels for 13%

profile of v3, /device:TPU:0, one launch (start us, length us, event | category | flops | bytes accessed | tf_op | source)
XLA Modules:
  0.0 125.0 jit_solution(4734404970192249398)
XLA Ops:
  0.6 0.0 copy-start.7
  0.6 0.0 copy-start.8
  0.7 0.0 copy-start.9
  0.7 0.0 copy-start.10
  0.7 18.1 %in0.1 = (bf16[256,1280]{1,0:T(8,128)(2,1)S(1)}, bf16[256,1280]{1,0:T(8,128)(2,1)S(1)}, bf16[192,256]{1,0:T(8,128)(2,1)S(1)}, bf16[2,3,256,1280]{3,2,1,0:T(8,128)(2,1)}) custom-call(f32[256,2560]{1,0:T(8,128)} %refs_0_.3, bf16[2,2560]{1,0:T(2,128)(2,1)} %refs_9_.1, bf16[2,2560,2,1280]{3,2,1,0:T(2,128)(2,1)} %refs_10_.1, bf16[2,4,1280]{2,1,0:T(4,128)(2,1)} %refs_11_.1, ...), custom_call_target="tpu_custom_call" | custom-call | flops 6710886400 | bytes 20971520 | tf_op jit(solution)/shard_map/in0/pallas_call | solution.py:153
  18.8 0.0 copy-done.7
  18.8 0.0 copy-done.8
  18.8 0.0 copy-done.9
  18.8 0.0 copy-done.10
  18.8 24.9 %k0.1 = (f32[256,16,1280]{2,1,0:T(8,128)S(1)}, bf16[128,1280]{1,0:T(8,128)(2,1)S(1)}, bf16[128,1280]{1,0:T(8,128)(2,1)S(1)}, bf16[128,1280]{1,0:T(8,128)(2,1)S(1...) custom-call(bf16[192,256]{1,0:T(8,128)(2,1)S(1)} %get-tuple-element.28.pt, ...), custom_call_target="tpu_custom_call" | custom-call | flops 20000000000 | bytes 29360128 | tf_op jit(solution)/shard_map/k0/pallas_call | solution.py:344
  43.7 0.0 copy-start.1
  43.7 0.0 copy-start.2
  43.8 0.0 copy-start.3
  43.8 0.0 copy-start.4
  43.8 0.0 copy-start.5
  43.8 0.0 copy-start.6
  43.8 1.7 %collective-permute-start = (bf16[128,1280]{1,0:T(8,128)(2,1)S(1)}, bf16[128,1280]{1,0:T(8,128)(2,1)S(1)}, u32[]{:S(2)}, u32[]{:S(2)}) collective-permute-start(bf16[128,1280]{1,0:T(8,128)(2,1)S(1)} %get-tuple-element.35.refs_5_), channel_id=1, source_target_pairs={{0,2},{2,0},{1,3},{3,1},{4,6},{6,4},{5,7},{7,5}} | collective-permute-start | bytes 983048 | tf_op jit(solution)/shard_map/ppermute | solution.py:437
  45.5 8.0 %collective-permute-done.refs_7_ = bf16[128,1280]{1,0:T(8,128)(2,1)S(1)} collective-permute-done((bf16[128,1280]{1,0:T(8,128)(2,1)S(1)}, bf16[128,1280]{1,0:T(8,128)(2,1)S(1)}, u32[]{:S(2)}, u32[]{:S(2)}) %collective-permute-start) | collective-permute-done | bytes 327712 | tf_op jit(solution)/shard_map/ppermute | solution.py:437
  53.5 0.0 copy-start.11
  53.5 0.0 collective-permute-start.1
  53.5 7.8 %w0.1 = (f32[2,256,16,1280]{3,2,1,0:T(8,128)}, f32[8,128]{1,0:T(8,128)}) custom-call(f32[256,16,1280]{2,1,0:T(8,128)S(1)} %get-tuple-element.38.st), custom_call_target="tpu_custom_call" | custom-call | flops 20000000000 | bytes 44040192 | tf_op jit(solution)/shard_map/w0/pallas_call | solution.py:386
  61.4 0.0 copy-done.1
  61.4 0.0 copy-done.2
  61.4 0.0 copy-done.3
  61.4 0.0 copy-done.4
  61.4 0.0 copy-done.5
  61.4 0.0 copy-done.6
  61.4 0.0 copy-done.11
  61.4 0.0 collective-permute-done.1.refs_8_
  61.5 0.0 copy-start.12
  61.5 0.7 copy-done.12
  62.2 19.3 %in1.1 = (bf16[256,1280]{1,0:T(8,128)(2,1)S(1)}, bf16[256,1280]{1,0:T(8,128)(2,1)S(1)}, bf16[192,256]{1,0:T(8,128)(2,1)S(1)}, bf16[2,3,256,1280]{3,2,1,0:T(8,128)(2,1)}, f32[256,2560]{1,0:T(8,128)}) custom-call(f32[256,2560]{1,0:T(8,128)} %refs_0_.3, bf16[128,1280]{1,0:T(8,128)(2,1)} %copy-done.1, ...), custom_call_target="tpu_custom_call", output_to_operand_aliasing={{3}: (15, {})} | custom-call | flops 6710886400 | bytes 20971520 | tf_op jit(solution)/shard_map/in1/pallas_call | solution.py:153
  81.5 23.7 %k1.1 = (f32[256,16,1280]{2,1,0:T(8,128)S(1)}, bf16[128,1280]{1,0:T(8,128)(2,1)S(1)}, bf16[128,1280]{1,0:T(8,128)(2,1)S(1)}, bf16[128,1280]{1,0:T(8,128)(2,1)S(1...) custom-call(bf16[192,256]{1,0:T(8,128)(2,1)S(1)} %get-tuple-element.41.pt, ...), custom_call_target="tpu_custom_call" | custom-call | flops 20000000000 | bytes 29360128 | tf_op jit(solution)/shard_map/k1/pallas_call | solution.py:344
  105.2 1.5 %collective-permute-start.2 = (bf16[128,1280]{1,0:T(8,128)(2,1)S(1)}, bf16[128,1280]{1,0:T(8,128)(2,1)S(1)}, u32[]{:S(2)}, u32[]{:S(2)}) collective-permute-start(bf16[128,1280]{1,0:T(8,128)(2,1)S(1)} %get-tuple-element.48.refs_4_), channel_id=1, source_target_pairs={{0,2},{2,0},{1,3},{3,1},{4,6},{6,4},{5,7},{7,5}} | collective-permute-start | bytes 983048 | tf_op jit(solution)/shard_map/ppermute | solution.py:437
  106.8 8.2 %collective-permute-done.2.refs_6_ = bf16[128,1280]{1,0:T(8,128)(2,1)S(1)} collective-permute-done((bf16[128,1280]{1,0:T(8,128)(2,1)S(1)}, bf16[128,1280]{1,0:T(8,128)(2,1)S(1)}, u32[]{:S(2)}, u32[]{:S(2)}) %collective-permute-start.2) | collective-permute-done | bytes 327712 | tf_op jit(solution)/shard_map/ppermute | solution.py:437
  115.0 0.0 collective-permute-start.3
  115.0 0.0 copy-start
  115.0 8.1 %w1.1 = (f32[2,256,16,1280]{3,2,1,0:T(8,128)}, f32[8,128]{1,0:T(8,128)}) custom-call(f32[256,16,1280]{2,1,0:T(8,128)S(1)} %get-tuple-element.51.st, f32[2,256,16,1280]{3,2,1,0:T(8,128)} %get-tuple-element.39.refs_16_.refs_0_), custom_call_target="tpu_custom_call", output_to_operand_aliasing={{0}: (1, {})} | custom-call | flops 20000000000 | bytes 44040192 | tf_op jit(solution)/shard_map/w1/pallas_call | solution.py:386
  123.1 0.0 collective-permute-done.3.refs_7_
  123.1 0.0 copy-done
  123.1 1.9 %fin.1 = f32[256,2560]{1,0:T(8,128)} custom-call(f32[256,2560]{1,0:T(8,128)S(1)} %copy-done, bf16[128,1280]{1,0:T(8,128)(2,1)S(1)} %get-tuple-element.44.refs_0_, bf16[128,1280]{1,0:T(8,128)(2,1)S(1)} %get-tuple-element.45.refs_1_, bf16[128,1280]{1,0:T(8,128)(2,1)S(1)} %get-tuple-element.46.refs_2_, bf16[128,1280]{1,0:T(8,128)(2,1)S(1)} %get-tuple-element.47.refs_3_, ...), custom_call_target="tpu_custom_call" | custom-call | tf_op jit(solution)/shard_map/fin/pallas_call | solution.py:411
Async XLA Ops:
  0.6 18.1 %copy-start.7 = (bf16[2,160,1280]{2,1,0:T(8,128)(2,1)S(1)}, bf16[2,160,1280]{2,1,0:T(8,128)(2,1)}, u32[]{:S(2)}) copy-start(bf16[2,160,1280]{2,1,0:T(8,128)(2,1)} %w_dt.3) | copy-start | bytes 2457604
  0.6 18.1 %copy-start.8 = (f32[2,16,1280]{2,1,0:T(8,128)S(1)}, f32[2,16,1280]{2,1,0:T(8,128)}, u32[]{:S(2)}) copy-start(f32[2,16,1280]{2,1,0:T(8,128)} %a_log.3) | copy-start | bytes 491524
  0.7 18.1 %copy-start.9 = (f32[2,1280]{1,0:T(2,128)S(1)}, f32[2,1280]{1,0:T(2,128)}, u32[]{:S(2)}) copy-start(f32[2,1280]{1,0:T(2,128)} %b_dt.3) | copy-start | bytes 30724
  0.7 18.1 %copy-start.10 = (f32[2,1280]{1,0:T(2,128)S(1)}, f32[2,1280]{1,0:T(2,128)}, u32[]{:S(2)}) copy-start(f32[2,1280]{1,0:T(2,128)} %d_skip.3) | copy-start | bytes 30724
  43.7 17.6 %copy-start.1 = (bf16[128,1280]{1,0:T(8,128)(2,1)}, bf16[128,1280]{1,0:T(8,128)(2,1)S(1)}, u32[]{:S(2)}) copy-start(bf16[128,1280]{1,0:T(8,128)(2,1)S(1)} %get-tuple-element.31.refs_1_) | copy-start | bytes 983044
  43.7 17.6 %copy-start.2 = (bf16[128,1280]{1,0:T(8,128)(2,1)}, bf16[128,1280]{1,0:T(8,128)(2,1)S(1)}, u32[]{:S(2)}) copy-start(bf16[128,1280]{1,0:T(8,128)(2,1)S(1)} %get-tuple-element.35.refs_5_) | copy-start | bytes 983044
  43.8 17.6 %copy-start.3 = (bf16[128,1280]{1,0:T(8,128)(2,1)}, bf16[128,1280]{1,0:T(8,128)(2,1)S(1)}, u32[]{:S(2)}) copy-start(bf16[128,1280]{1,0:T(8,128)(2,1)S(1)} %get-tuple-element.32.refs_2_) | copy-start | bytes 983044
  43.8 17.6 %copy-start.4 = (bf16[128,1280]{1,0:T(8,128)(2,1)}, bf16[128,1280]{1,0:T(8,128)(2,1)S(1)}, u32[]{:S(2)}) copy-start(bf16[128,1280]{1,0:T(8,128)(2,1)S(1)} %get-tuple-element.36.refs_6_) | copy-start | bytes 983044
  43.8 17.6 %copy-start.5 = (bf16[128,1280]{1,0:T(8,128)(2,1)}, bf16[128,1280]{1,0:T(8,128)(2,1)S(1)}, u32[]{:S(2)}) copy-start(bf16[128,1280]{1,0:T(8,128)(2,1)S(1)} %get-tuple-element.33.refs_3_) | copy-start | bytes 983044
  43.8 17.6 %copy-start.6 = (bf16[128,1280]{1,0:T(8,128)(2,1)}, bf16[128,1280]{1,0:T(8,128)(2,1)S(1)}, u32[]{:S(2)}) copy-start(bf16[128,1280]{1,0:T(8,128)(2,1)S(1)} %get-tuple-element.34.refs_4_) | copy-start | bytes 983044
  43.8 9.8 %collective-permute-start = (bf16[128,1280]{1,0:T(8,128)(2,1)S(1)}, bf16[128,1280]{1,0:T(8,128)(2,1)S(1)}, u32[]{:S(2)}, u32[]{:S(2)}) collective-permute-start(bf16[128,1280]{1,0:T(8,128)(2,1)S(1)} %get-tuple-element.35.refs_5_), channel_id=1, source_target_pairs={{0,2},{2,0},{1,3},{3,1},{4,6},{6,4},{5,7},{7,5}} | collective-permute-start | bytes 983048 | tf_op jit(solution)/shard_map/ppermute | solution.py:437
  53.5 7.9 %copy-start.11 = (bf16[128,1280]{1,0:T(8,128)(2,1)}, bf16[128,1280]{1,0:T(8,128)(2,1)S(1)}, u32[]{:S(2)}) copy-start(bf16[128,1280]{1,0:T(8,128)(2,1)S(1)} %collective-permute-done.refs_7_) | copy-start | bytes 983044
  53.5 7.9 %collective-permute-start.1 = (bf16[128,1280]{1,0:T(8,128)(2,1)S(1)}, bf16[128,1280]{1,0:T(8,128)(2,1)S(1)}, u32[]{:S(2)}, u32[]{:S(2)}) collective-permute-start(bf16[128,1280]{1,0:T(8,128)(2,1)S(1)} %collective-permute-done.refs_7_), channel_id=1, source_target_pairs={{0,1},{1,0},{2,3},{3,2},{4,5},{5,4},{6,7},{7,6}} | collective-permute-start | bytes 983048 | tf_op jit(solution)/shard_map/ppermute | solution.py:440
  61.5 0.7 copy-start.12
  105.2 9.8 %collective-permute-start.2 = (bf16[128,1280]{1,0:T(8,128)(2,1)S(1)}, bf16[128,1280]{1,0:T(8,128)(2,1)S(1)}, u32[]{:S(2)}, u32[]{:S(2)}) collective-permute-start(bf16[128,1280]{1,0:T(8,128)(2,1)S(1)} %get-tuple-element.48.refs_4_), channel_id=1, source_target_pairs={{0,2},{2,0},{1,3},{3,1},{4,6},{6,4},{5,7},{7,5}} | collective-permute-start | bytes 983048 | tf_op jit(solution)/shard_map/ppermute | solution.py:437
  115.0 8.1 %collective-permute-start.3 = (bf16[128,1280]{1,0:T(8,128)(2,1)S(1)}, bf16[128,1280]{1,0:T(8,128)(2,1)S(1)}, u32[]{:S(2)}, u32[]{:S(2)}) collective-permute-start(bf16[128,1280]{1,0:T(8,128)(2,1)S(1)} %collective-permute-done.2.refs_6_), channel_id=1, source_target_pairs={{0,1},{1,0},{2,3},{3,2},{4,5},{5,4},{6,7},{7,6}} | collective-permute-start | bytes 983048 | tf_op jit(solution)/shard_map/ppermute | solution.py:440
  115.0 8.1 %copy-start = (f32[256,2560]{1,0:T(8,128)S(1)}, f32[256,2560]{1,0:T(8,128)}, u32[]{:S(2)}) copy-start(f32[256,2560]{1,0:T(8,128)} %get-tuple-element.40.r_ref) | copy-start | bytes 7864324

commit v4 on v3

--- a/solution.py
+++ b/solution.py
@@ -7,6 +7,7 @@
 from jax.experimental import pallas as pl
 from jax.experimental.pallas import tpu as pltpu
 from jax.sharding import PartitionSpec as P
+
 
 F32 = jnp.float32
 BF16 = jnp.bfloat16
@@ -41,7 +42,7 @@
     z_out, xc_out, p_out, conv_out = refs[:4]
     refs = refs[4:]
     r_out = refs.pop(0) if has_o else None
-    wbuf, hx, hbuf, ex_s, p_acc, rbuf, cbuf, xbuf, rsem, wsem, csem, osem = refs
+    wbuf, hx, hbuf, ex_s, p_acc, rbuf, cbuf, xbuf, rsem, wsem, csem, osem, xsem = refs
     rows, feat = rbuf.shape
     nchunk = wbuf.shape[0]
     w_flat = w_in.reshape(w_in.shape[0], 2 * feat, w_in.shape[3])
@@ -49,19 +50,25 @@
     r_copy = pltpu.make_async_copy(res_hbm, rbuf, rsem)
     c_copy = pltpu.make_async_copy(conv_st.at[layer], cbuf, csem)
     state_copy = pltpu.make_async_copy(cbuf.at[pl.ds(1, 2)], conv_out.at[layer, pl.ds(0, 2)], osem.at[1])
-    x_copy = pltpu.make_async_copy(xbuf, conv_out.at[layer, 2], osem.at[2])
+
+    def cols_of(c):
+        return pl.ds(pl.multiple_of(c * NCH, NCH), NCH)
+
+    def x_copy(c):
+        return pltpu.make_async_copy(xbuf.at[:, cols_of(c)], conv_out.at[layer, 2, :, cols_of(c)], xsem.at[c])
 
     def w_copy(c):
-        cols = pl.ds(pl.multiple_of(c * NCH, NCH), NCH)
+        cols = cols_of(c)
         return pltpu.make_async_copy(w_flat.at[layer, :, cols], wbuf.at[c], wsem.at[c])
 
     r_copy.start()
     w_copy(0).start()
-    w_copy(1).start()
     ex_s[...] = expand_matrix()
     p_acc[...] = jnp.zeros_like(p_acc)
     r_copy.wait()
+    w_copy(1).start()
     c_copy.start()
+    w_copy(2).start()
     nw = norm_w[layer:layer + 1, :].astype(F32)
     half = feat // 2
     if has_o:
@@ -90,28 +97,31 @@
     lax.fori_loop(0, rows // 32, norm, 0)
 
     def expand(j, carry):
-        e = jnp.dot(hbuf[:, pl.ds(pl.multiple_of(j * 128, 128), 128)], ex_s[...], preferred_element_type=F32).astype(BF16)
-        cols = pl.ds(pl.multiple_of(j * 256, 256), 256)
-        hx[0:rows, cols] = e[:, :256]
-        hx[rows:2 * rows, cols] = e[:, 256:]
+        for t in range(4):
+            src = pl.ds(pl.multiple_of(j * 512 + t * 128, 128), 128)
+            e = jnp.dot(hbuf[:, src], ex_s[...], preferred_element_type=F32).astype(BF16)
+            cols = pl.ds(pl.multiple_of(j * 1024 + t * 256, 256), 256)
+            hx[0:rows, cols] = e[:, :256]
+            hx[rows:2 * rows, cols] = e[:, 256:]
         return carry
 
-    lax.fori_loop(0, feat // 128, expand, 0)
+    lax.fori_loop(0, feat // 512, expand, 0)
     c_copy.wait()
     state_copy.start()
 
     def chunk(c, carry):
         w_copy(c).wait()
 
-        @pl.when(c + 2 < nchunk)
+        @pl.when(c + 3 < nchunk)
         def _():
-            w_copy(c + 2).start()
-
-        sl = pl.ds(pl.multiple_of(c * NCH, NCH), NCH)
+            w_copy(c + 3).start()
+
+        sl = cols_of(c)
         acc = jnp.dot(hx[...], wbuf[c], preferred_element_type=F32)
         x = acc[:rows].astype(BF16)
         z_out[:, sl] = acc[rows:].astype(BF16)
         xbuf[:, sl] = x
+        x_copy(c).start()
         cw = conv_w[layer, :, sl].astype(F32)
         pre = cbuf[0, :, sl].astype(F32) * cw[0:1] + cbuf[1, :, sl].astype(F32) * cw[1:2]
         pre = pre + cbuf[2, :, sl].astype(F32) * cw[2:3] + x.astype(F32) * cw[3:4]
@@ -122,9 +132,9 @@
         return carry
 
     lax.fori_loop(0, nchunk, chunk, 0)
-    x_copy.start()
     p_out[...] = p_acc[...].astype(BF16)
-    x_copy.wait()
+    for c in range(nchunk):
+        x_copy(c).wait()
     state_copy.wait()
     if has_o:
         pltpu.make_async_copy(rbuf, r_out, osem.at[0]).wait()
@@ -163,11 +173,10 @@
             pltpu.VMEM((3, rows, chan), BF16),
             pltpu.VMEM((rows, chan), BF16),
             pltpu.SemaphoreType.DMA, pltpu.SemaphoreType.DMA((nchunk,)), pltpu.SemaphoreType.DMA,
-            pltpu.SemaphoreType.DMA((3,)),
+            pltpu.SemaphoreType.DMA((2,)), pltpu.SemaphoreType.DMA((nchunk,)),
         ],
         compiler_params=pltpu.CompilerParams(vmem_limit_bytes=60 * 2 ** 20),
         cost_estimate=pl.CostEstimate(flops=rows * 2 * feat * 2 * chan * 2, bytes_accessed=20 * 2 ** 20, transcendentals=0),
-        name=f"in{layer}",
     )(*args)
 
 
@@ -196,7 +205,7 @@
     core = lax.rem(me, 2)
     partner = me + 1 - 2 * core
     other = lax.rem(me + 2, 4)
-    rows, chan = dt_s.shape
+    rows, _ = dt_s.shape
     rank = w_dt.shape[1]
     nst = a_s.shape[0]
     nblk = rows // SB
@@ -209,10 +218,11 @@
         rs = pl.ds(i * SB, SB)
         return pltpu.make_async_copy(state.at[layer, rs], st.at[rs], stsem.at[i])
 
+    w_copy = pltpu.make_async_copy(w_out.at[layer], wo, wsem)
     for i in range(nblk):
+        if i == nblk // 4:
+            w_copy.start()
         st_copy(i).start()
-    w_copy = pltpu.make_async_copy(w_out.at[layer], wo, wsem)
-    w_copy.start()
 
     def send(src, dst, k, dev):
         return pltpu.make_async_remote_copy(src_ref=src, dst_ref=dst, send_sem=ssem.at[k], recv_sem=rsem.at[k],
@@ -356,13 +366,11 @@
         ],
         compiler_params=pltpu.CompilerParams(vmem_limit_bytes=26 * 2 ** 20, collective_id=layer, has_side_effects=True),
         cost_estimate=pl.CostEstimate(flops=2 * 10 ** 10, bytes_accessed=28 * 2 ** 20, transcendentals=0),
-        name=f"k{layer}",
     )(*ins, w_dt, b_dt, a_log, d_skip, w_out, state)
 
 
 def w_kernel(layer, st, *refs):
-    out, flag, sem = refs[-3:]
-    flag[...] = jnp.zeros_like(flag)
+    out, sem = refs[-2:]
     step = st.shape[0] // 8
 
     def copy(i):
@@ -385,12 +393,10 @@
         specs.append(ANY)
     return pl.pallas_call(
         functools.partial(w_kernel, layer),
-        out_shape=[jax.ShapeDtypeStruct(shape, F32), jax.ShapeDtypeStruct((8, 128), F32)],
-        in_specs=specs, out_specs=[ANY, VMEM], input_output_aliases=alias,
+        out_shape=jax.ShapeDtypeStruct(shape, F32), in_specs=specs, out_specs=ANY, input_output_aliases=alias,
         scratch_shapes=[pltpu.SemaphoreType.DMA((8,))],
         compiler_params=pltpu.CompilerParams(vmem_limit_bytes=2 ** 20),
         cost_estimate=pl.CostEstimate(flops=2 * 10 ** 10, bytes_accessed=42 * 2 ** 20, transcendentals=0),
-        name=f"w{layer}",
     )(*args)
 
 
@@ -435,8 +441,7 @@
                 r = got[4]
             st, ua, ub, upa, upb, va, vpa = k_call(layer, pt, xc, z, s_w, ssm_state)
             vb = lax.ppermute(ub, 'tp', CROSS)
-            ssm_out, flag = w_call(layer, st, ssm_state.shape, ssm_out)
-            vb, _ = lax.optimization_barrier((vb, flag))
+            ssm_out = w_call(layer, st, ssm_state.shape, ssm_out)
             vpb = lax.ppermute(vb, 'tp', PART)
             pieces = ((ua, upa, va, vpa), (ub, upb, vb, vpb))
         out = fin_call(r, pieces)

time: 125 us -> 120 us (0.960)
  Pallas kernels: 104 us -> 98.7 us
    pallas_call x2, Pallas kernels: 37.4 us -> 32.9 us  [in_call(): pl.pallas_call(functools.partial(in_kernel, layer, has_o), out_shape=outs...]
  transfers between devices with their start and end apart: 4 -> 4, of which waited for: 2 -> 2; matrix products, arithmetic and copies ran while one was open for 0% -> 0% of each run, Pallas kernels for 13% -> 12%
where the time goes in v4:
time: 120 us
  Pallas kernels  98.7 us (82%)
  waiting for transfers between devices  16.5 us (14%)
  starting transfers between devices  2.97 us (2%)
    pallas_call x2, Pallas kernels, k_call(): pl.pallas_call(functools.partial(k_kernel, layer), out_shape=[pltpu.VMEM(...  49.3 us
    pallas_call x2, Pallas kernels, in_call(): pl.pallas_call(functools.partial(in_kernel, layer, has_o), out_shape=outs...  32.9 us
    ppermute x2, waiting for transfers between devices, step(): vb = lax.ppermute(ub, 'tp', CROSS)  16.5 us
    pallas_call x2, Pallas kernels, w_call(): pl.pallas_call(functools.partial(w_kernel, layer), out_shape=jax.ShapeDty...  14.7 us
    ppermute x2, starting transfers between devices, step(): vb = lax.ppermute(ub, 'tp', CROSS)  2.97 us
  transfers between devices with their start and end apart: 4, of which 2 were waited for; matrix products, arithmetic and copies ran while one was open for 0% of the time, Pallas kernels for 12%

profile of v4, /device:TPU:0, one launch (start us, length us, event | category | flops | bytes accessed | tf_op | source)
XLA Modules:
  0.0 119.9 jit_solution(776697473975427498)
XLA Ops:
  0.6 0.0 copy-start.7
  0.6 0.0 copy-start.8
  0.7 0.0 copy-start.9
  0.7 0.0 copy-start.10
  0.7 15.8 %shard_map.148 = (bf16[256,1280]{1,0:T(8,128)(2,1)S(1)}, bf16[256,1280]{1,0:T(8,128)(2,1)S(1)}, bf16[192,256]{1,0:T(8,128)(2,1)S(1)}, bf16[2,3,256,1280]{3,2,1,0:T(8,128)(2,1)}) custom-call(f32[256,2560]{1,0:T(8,128)} %refs_0_.3, bf16[2,2560]{1,0:T(2,128)(2,1)} %refs_9_.1, bf16[2,2560,2,1280]{3,2,1,0:T(2,128)(2,1)} %refs_10_.1, ...), custom_call_target="tpu_custom_call" | custom-call | flops 6710886400 | bytes 20971520 | tf_op jit(solution)/shard_map/pallas_call | solution.py:163
  16.5 0.0 copy-done.7
  16.5 0.0 copy-done.8
  16.5 0.0 copy-done.9
  16.5 0.0 copy-done.10
  16.5 24.9 %shard_map.149 = (f32[256,16,1280]{2,1,0:T(8,128)S(1)}, bf16[128,1280]{1,0:T(8,128)(2,1)S(1)}, bf16[128,1280]{1,0:T(8,128)(2,1)S(1)}, bf16[128,1280]{1,0:T(8,128...) custom-call(bf16[192,256]{1,0:T(8,128)(2,1)S(1)} %get-tuple-element.26.pt, ...), custom_call_target="tpu_custom_call" | custom-call | flops 20000000000 | bytes 29360128 | tf_op jit(solution)/shard_map/pallas_call | solution.py:354
  41.4 0.0 copy-start.1
  41.4 0.0 copy-start.2
  41.5 0.0 copy-start.3
  41.5 0.0 copy-start.4
  41.5 0.0 copy-start.5
  41.5 0.0 copy-start.6
  41.5 1.5 %collective-permute-start = (bf16[128,1280]{1,0:T(8,128)(2,1)S(1)}, bf16[128,1280]{1,0:T(8,128)(2,1)S(1)}, u32[]{:S(2)}, u32[]{:S(2)}) collective-permute-start(bf16[128,1280]{1,0:T(8,128)(2,1)S(1)} %get-tuple-element.33.refs_5_), channel_id=1, source_target_pairs={{0,2},{2,0},{1,3},{3,1},{4,6},{6,4},{5,7},{7,5}} | collective-permute-start | bytes 983048 | tf_op jit(solution)/shard_map/ppermute | solution.py:443
  43.0 8.3 %collective-permute-done.refs_7_ = bf16[128,1280]{1,0:T(8,128)(2,1)S(1)} collective-permute-done((bf16[128,1280]{1,0:T(8,128)(2,1)S(1)}, bf16[128,1280]{1,0:T(8,128)(2,1)S(1)}, u32[]{:S(2)}, u32[]{:S(2)}) %collective-permute-start) | collective-permute-done | bytes 327712 | tf_op jit(solution)/shard_map/ppermute | solution.py:443
  51.3 0.0 copy-start.11
  51.3 0.0 collective-permute-start.1
  51.3 7.2 %shard_map.150.refs_16_.refs_0_ = f32[2,256,16,1280]{3,2,1,0:T(8,128)} custom-call(f32[256,16,1280]{2,1,0:T(8,128)S(1)} %get-tuple-element.36.st), custom_call_target="tpu_custom_call" | custom-call | flops 20000000000 | bytes 44040192 | tf_op jit(solution)/shard_map/pallas_call | solution.py:394
  58.5 0.0 copy-done.1
  58.5 0.0 copy-done.2
  58.5 0.0 copy-done.3
  58.5 0.0 copy-done.4
  58.5 0.0 copy-done.5
  58.5 0.0 copy-done.6
  58.5 0.0 copy-done.11
  58.6 0.0 collective-permute-done.1.refs_8_
  58.6 0.0 copy-start.12
  58.6 0.7 copy-done.12
  59.3 17.0 %shard_map.151 = (bf16[256,1280]{1,0:T(8,128)(2,1)S(1)}, bf16[256,1280]{1,0:T(8,128)(2,1)S(1)}, bf16[192,256]{1,0:T(8,128)(2,1)S(1)}, bf16[2,3,256,1280]{3,2,1,0:T(8,128)(2,1)}, f32[256,2560]{1,0:T(8,128)}) custom-call(f32[256,2560]{1,0:T(8,128)} %refs_0_.3, bf16[128,1280]{1,0:T(8,128)(2,1)} %copy-done.1, ...), custom_call_target="tpu_custom_call", output_to_operand_aliasing={{3}: (15, {})} | custom-call | flops 6710886400 | bytes 20971520 | tf_op jit(solution)/shard_map/pallas_call | solution.py:163
  76.3 24.4 %shard_map.152 = (f32[256,16,1280]{2,1,0:T(8,128)S(1)}, bf16[128,1280]{1,0:T(8,128)(2,1)S(1)}, bf16[128,1280]{1,0:T(8,128)(2,1)S(1)}, bf16[128,1280]{1,0:T(8,128...) custom-call(bf16[192,256]{1,0:T(8,128)(2,1)S(1)} %get-tuple-element.38.pt, ...), custom_call_target="tpu_custom_call" | custom-call | flops 20000000000 | bytes 29360128 | tf_op jit(solution)/shard_map/pallas_call | solution.py:354
  100.7 1.5 %collective-permute-start.2 = (bf16[128,1280]{1,0:T(8,128)(2,1)S(1)}, bf16[128,1280]{1,0:T(8,128)(2,1)S(1)}, u32[]{:S(2)}, u32[]{:S(2)}) collective-permute-start(bf16[128,1280]{1,0:T(8,128)(2,1)S(1)} %get-tuple-element.45.refs_4_), channel_id=1, source_target_pairs={{0,2},{2,0},{1,3},{3,1},{4,6},{6,4},{5,7},{7,5}} | collective-permute-start | bytes 983048 | tf_op jit(solution)/shard_map/ppermute | solution.py:443
  102.2 8.3 %collective-permute-done.2.refs_6_ = bf16[128,1280]{1,0:T(8,128)(2,1)S(1)} collective-permute-done((bf16[128,1280]{1,0:T(8,128)(2,1)S(1)}, bf16[128,1280]{1,0:T(8,128)(2,1)S(1)}, u32[]{:S(2)}, u32[]{:S(2)}) %collective-permute-start.2) | collective-permute-done | bytes 327712 | tf_op jit(solution)/shard_map/ppermute | solution.py:443
  110.5 0.0 collective-permute-start.3
  110.5 0.0 copy-start
  110.5 7.5 %shard_map.153 = f32[2,256,16,1280]{3,2,1,0:T(8,128)} custom-call(f32[256,16,1280]{2,1,0:T(8,128)S(1)} %get-tuple-element.48.st, f32[2,256,16,1280]{3,2,1,0:T(8,128)} %shard_map.150.refs_16_.refs_0_), custom_call_target="tpu_custom_call", output_to_operand_aliasing={{}: (1, {})} | custom-call | flops 20000000000 | bytes 44040192 | tf_op jit(solution)/shard_map/pallas_call | solution.py:394
  118.0 0.0 collective-permute-done.3.refs_7_
  118.0 0.0 copy-done
  118.0 1.9 %fin.1 = f32[256,2560]{1,0:T(8,128)} custom-call(f32[256,2560]{1,0:T(8,128)S(1)} %copy-done, bf16[128,1280]{1,0:T(8,128)(2,1)S(1)} %get-tuple-element.41.refs_0_, bf16[128,1280]{1,0:T(8,128)(2,1)S(1)} %get-tuple-element.42.refs_1_, bf16[128,1280]{1,0:T(8,128)(2,1)S(1)} %get-tuple-element.43.refs_2_, bf16[128,1280]{1,0:T(8,128)(2,1)S(1)} %get-tuple-element.44.refs_3_, ...), custom_call_target="tpu_custom_call" | custom-call | tf_op jit(solution)/shard_map/fin/pallas_call | solution.py:417
Async XLA Ops:
  0.6 15.9 %copy-start.7 = (bf16[2,160,1280]{2,1,0:T(8,128)(2,1)S(1)}, bf16[2,160,1280]{2,1,0:T(8,128)(2,1)}, u32[]{:S(2)}) copy-start(bf16[2,160,1280]{2,1,0:T(8,128)(2,1)} %w_dt.3) | copy-start | bytes 2457604
  0.6 15.9 %copy-start.8 = (f32[2,16,1280]{2,1,0:T(8,128)S(1)}, f32[2,16,1280]{2,1,0:T(8,128)}, u32[]{:S(2)}) copy-start(f32[2,16,1280]{2,1,0:T(8,128)} %a_log.3) | copy-start | bytes 491524
  0.7 15.9 %copy-start.9 = (f32[2,1280]{1,0:T(2,128)S(1)}, f32[2,1280]{1,0:T(2,128)}, u32[]{:S(2)}) copy-start(f32[2,1280]{1,0:T(2,128)} %b_dt.3) | copy-start | bytes 30724
  0.7 15.9 %copy-start.10 = (f32[2,1280]{1,0:T(2,128)S(1)}, f32[2,1280]{1,0:T(2,128)}, u32[]{:S(2)}) copy-start(f32[2,1280]{1,0:T(2,128)} %d_skip.3) | copy-start | bytes 30724
  41.4 17.1 %copy-start.1 = (bf16[128,1280]{1,0:T(8,128)(2,1)}, bf16[128,1280]{1,0:T(8,128)(2,1)S(1)}, u32[]{:S(2)}) copy-start(bf16[128,1280]{1,0:T(8,128)(2,1)S(1)} %get-tuple-element.29.refs_1_) | copy-start | bytes 983044
  41.4 17.1 %copy-start.2 = (bf16[128,1280]{1,0:T(8,128)(2,1)}, bf16[128,1280]{1,0:T(8,128)(2,1)S(1)}, u32[]{:S(2)}) copy-start(bf16[128,1280]{1,0:T(8,128)(2,1)S(1)} %get-tuple-element.33.refs_5_) | copy-start | bytes 983044
  41.5 17.1 %copy-start.3 = (bf16[128,1280]{1,0:T(8,128)(2,1)}, bf16[128,1280]{1,0:T(8,128)(2,1)S(1)}, u32[]{:S(2)}) copy-start(bf16[128,1280]{1,0:T(8,128)(2,1)S(1)} %get-tuple-element.30.refs_2_) | copy-start | bytes 983044
  41.5 17.1 %copy-start.4 = (bf16[128,1280]{1,0:T(8,128)(2,1)}, bf16[128,1280]{1,0:T(8,128)(2,1)S(1)}, u32[]{:S(2)}) copy-start(bf16[128,1280]{1,0:T(8,128)(2,1)S(1)} %get-tuple-element.34.refs_6_) | copy-start | bytes 983044
  41.5 17.1 %copy-start.5 = (bf16[128,1280]{1,0:T(8,128)(2,1)}, bf16[128,1280]{1,0:T(8,128)(2,1)S(1)}, u32[]{:S(2)}) copy-start(bf16[128,1280]{1,0:T(8,128)(2,1)S(1)} %get-tuple-element.31.refs_3_) | copy-start | bytes 983044
  41.5 17.1 %copy-start.6 = (bf16[128,1280]{1,0:T(8,128)(2,1)}, bf16[128,1280]{1,0:T(8,128)(2,1)S(1)}, u32[]{:S(2)}) copy-start(bf16[128,1280]{1,0:T(8,128)(2,1)S(1)} %get-tuple-element.32.refs_4_) | copy-start | bytes 983044
  41.5 9.8 %collective-permute-start = (bf16[128,1280]{1,0:T(8,128)(2,1)S(1)}, bf16[128,1280]{1,0:T(8,128)(2,1)S(1)}, u32[]{:S(2)}, u32[]{:S(2)}) collective-permute-start(bf16[128,1280]{1,0:T(8,128)(2,1)S(1)} %get-tuple-element.33.refs_5_), channel_id=1, source_target_pairs={{0,2},{2,0},{1,3},{3,1},{4,6},{6,4},{5,7},{7,5}} | collective-permute-start | bytes 983048 | tf_op jit(solution)/shard_map/ppermute | solution.py:443
  51.3 7.3 %copy-start.11 = (bf16[128,1280]{1,0:T(8,128)(2,1)}, bf16[128,1280]{1,0:T(8,128)(2,1)S(1)}, u32[]{:S(2)}) copy-start(bf16[128,1280]{1,0:T(8,128)(2,1)S(1)} %collective-permute-done.refs_7_) | copy-start | bytes 983044
  51.3 7.3 %collective-permute-start.1 = (bf16[128,1280]{1,0:T(8,128)(2,1)S(1)}, bf16[128,1280]{1,0:T(8,128)(2,1)S(1)}, u32[]{:S(2)}, u32[]{:S(2)}) collective-permute-start(bf16[128,1280]{1,0:T(8,128)(2,1)S(1)} %collective-permute-done.refs_7_), channel_id=1, source_target_pairs={{0,1},{1,0},{2,3},{3,2},{4,5},{5,4},{6,7},{7,6}} | collective-permute-start | bytes 983048 | tf_op jit(solution)/shard_map/ppermute | solution.py:445
  58.6 0.7 copy-start.12
  100.7 9.8 %collective-permute-start.2 = (bf16[128,1280]{1,0:T(8,128)(2,1)S(1)}, bf16[128,1280]{1,0:T(8,128)(2,1)S(1)}, u32[]{:S(2)}, u32[]{:S(2)}) collective-permute-start(bf16[128,1280]{1,0:T(8,128)(2,1)S(1)} %get-tuple-element.45.refs_4_), channel_id=1, source_target_pairs={{0,2},{2,0},{1,3},{3,1},{4,6},{6,4},{5,7},{7,5}} | collective-permute-start | bytes 983048 | tf_op jit(solution)/shard_map/ppermute | solution.py:443
  110.5 7.5 %collective-permute-start.3 = (bf16[128,1280]{1,0:T(8,128)(2,1)S(1)}, bf16[128,1280]{1,0:T(8,128)(2,1)S(1)}, u32[]{:S(2)}, u32[]{:S(2)}) collective-permute-start(bf16[128,1280]{1,0:T(8,128)(2,1)S(1)} %collective-permute-done.2.refs_6_), channel_id=1, source_target_pairs={{0,1},{1,0},{2,3},{3,2},{4,5},{5,4},{6,7},{7,6}} | collective-permute-start | bytes 983048 | tf_op jit(solution)/shard_map/ppermute | solution.py:445
  110.5 7.5 %copy-start = (f32[256,2560]{1,0:T(8,128)S(1)}, f32[256,2560]{1,0:T(8,128)}, u32[]{:S(2)}) copy-start(f32[256,2560]{1,0:T(8,128)} %get-tuple-element.37.r_ref) | copy-start | bytes 7864324

commit v5 on v0

v5 whole, which is shorter than its diff:
```python
import functools
import math

import jax
import jax.numpy as jnp
from jax import lax
from jax.experimental import pallas as pl
from jax.experimental.pallas import tpu as pltpu
from jax.sharding import PartitionSpec as P


F32 = jnp.float32
BF16 = jnp.bfloat16
ANY = pl.BlockSpec(memory_space=pltpu.HBM)
VMEM = pl.BlockSpec(memory_space=pltpu.VMEM)
NCH = 256
SB = 16
HALF = 128
LOG2E = math.log2(math.e)
MESH = pl.DeviceIdType.MESH


def silu(v):
    return v * jax.nn.sigmoid(v)


def expand_matrix():
    row = lax.broadcasted_iota(jnp.int32, (128, 512), 0)
    col = lax.broadcasted_iota(jnp.int32, (128, 512), 1)
    target = 2 * row + jnp.where(col < 256, 0, 257)
    return jnp.where(col == target, 1.0, 0.0).astype(BF16)


def rms0(v):
    return v * lax.rsqrt(jnp.mean(v * v, axis=0, keepdims=True) + 1e-6)


def sublane_sums(parts):
    sub = lax.broadcasted_iota(jnp.int32, parts[0].shape, 0)
    for step in (4, 2, 1):
        keep = (sub & step) == 0
        half = len(parts) // 2
        parts = [jnp.where(keep, parts[k], parts[k + half])
                 + pltpu.roll(jnp.where(keep, parts[k + half], parts[k]), step, 0) if step == 4 else
                 jnp.where(keep, parts[k], parts[k + half])
                 + jnp.where(keep, pltpu.roll(parts[k], 8 - step, 0), pltpu.roll(parts[k + half], step, 0))
                 for k in range(half)]
    return parts[0]


def layer_kernel(layer, has_o, *refs):
    refs = list(refs)
    res = refs.pop(0)
    pieces = [refs.pop(0) for _ in range(7)] if has_o else None
    (norm_w, w_in, conv_w, conv_b, w_x, conv_st, w_dt, b_dt, a_log, d_skip, w_out, state) = refs[:12]
    refs = refs[12:]
    st, cw, ua, ub, upa, upb, va, vpa = refs[:8]
    refs = refs[8:]
    r_out = refs.pop(0) if has_o else None
    (wbuf, hx, hbuf, ex_s, p_acc, p_own, p_sw, p_cs, p_v, rbuf, cold, z_s, xc_s, dt_s, bc_s, a_s, y_s, part,
     mine_a, mine_b, theirs_a, theirs_b, got_a, got_b, vpb, lsem, wsem, stsem, osem, ssem, rsem) = refs
    _, feat = rbuf.shape
    nchunk = wbuf.shape[0]
    chan = z_s.shape[1]
    rank = w_dt.shape[1]
    nst = a_s.shape[0]
    nblk = HALF // SB
    half = feat // 2
    quarter = HALF // 2
    w_flat = w_in.reshape(w_in.shape[0], 2 * feat, w_in.shape[3])

    me = lax.axis_index('tp')
    core = lax.rem(me, 2)
    partner = me + 1 - 2 * core
    other = lax.rem(me + 2, 4)
    lo = pl.ds(pl.multiple_of(core * half, 128), half)
    hi = pl.ds(pl.multiple_of((1 - core) * half, 128), half)

    barrier = pltpu.get_barrier_semaphore()
    for dev in (partner, other):
        pl.semaphore_signal(barrier, inc=1, device_id={'tp': dev}, device_id_type=MESH)

    def send(src, dst, k, dev):
        return pltpu.make_async_remote_copy(src_ref=src, dst_ref=dst, send_sem=ssem.at[k], recv_sem=rsem.at[k],
                                            device_id={'tp': dev}, device_id_type=MESH)

    def cols_of(c):
        return pl.ds(pl.multiple_of(c * NCH, NCH), NCH)

    def half_rows(k):
        return pl.ds(k * HALF, HALF)

    def r_copy(k):
        return pltpu.make_async_copy(res.at[half_rows(k)], rbuf.at[half_rows(k)], lsem.at[k])

    old_copy = pltpu.make_async_copy(conv_st.at[layer, 0], cold, lsem.at[2])
    win_copy = pltpu.make_async_copy(conv_st.at[layer, pl.ds(1, 2)], cw.at[pl.ds(0, 2)], lsem.at[3])

    def w_copy(c):
        return pltpu.make_async_copy(w_flat.at[layer, :, cols_of(c)], wbuf.at[c], wsem.at[c])

    def st_copy(i):
        rs = pl.ds(i * SB, SB)
        return pltpu.make_async_copy(state.at[layer, rs], st.at[rs], stsem.at[i])

    def out_tile(j):
        return wbuf.at[j // 4, pl.ds(pl.multiple_of(lax.rem(j, 4) * chan, 128), chan)]

    def o_copy(j):
        return pltpu.make_async_copy(w_out.at[layer, :, cols_of(j)], out_tile(j), osem.at[j])

    r_copy(0).start()
    w_copy(0).start()
    r_copy(1).start()
    w_copy(1).start()
    old_copy.start()
    win_copy.start()
    w_copy(2).start()
    ex_s[...] = expand_matrix()
    a_s[...] = -jnp.exp(a_log[layer]) * LOG2E
    nw = norm_w[layer:layer + 1, :].astype(F32)
    pl.semaphore_wait(barrier, 2)
    relay = None
    if has_o:
        relay = send(pieces[6], vpb, 14, partner)
        relay.start()

    def p_first(k):
        return send(p_own.at[k], p_sw.at[k], k, partner)

    def p_second(k):
        return send(p_cs.at[k], p_v.at[k], 2 + k, other)

    def p_middle(k):
        p_first(k).wait_recv()
        p_cs[k] = (p_own[k].astype(F32) + p_sw[k].astype(F32)).astype(BF16)
        p_second(k).start()

    for k in range(2):
        r_copy(k).wait()
        if has_o:
            if k == 0:
                u, up, v, vp = pieces[0:4]
            else:
                u, up, v, vp = pieces[4], pieces[5], pieces[6], vpb
                relay.wait_recv()

            def add(i, carry, k=k, u=u, up=up, v=v, vp=vp):
                src = pl.ds(pl.multiple_of(i * 32, 32), 32)
                dst = pl.ds(pl.multiple_of(i * 32, 32) + k * HALF, 32)
                rbuf[dst, lo] = rbuf[dst, lo] + (u[src, :].astype(F32) + v[src, :].astype(F32))
                rbuf[dst, hi] = rbuf[dst, hi] + (up[src, :].astype(F32) + vp[src, :].astype(F32))
                return carry

            lax.fori_loop(0, HALF // 32, add, 0)
            pltpu.make_async_copy(rbuf.at[half_rows(k)], r_out.at[half_rows(k)], lsem.at[4 + k]).start()

        def norm(i, carry, k=k):
            off = pl.multiple_of(i * 32, 32)
            r = rbuf[pl.ds(off + k * HALF, 32), :]
            inv = lax.rsqrt(jnp.mean(r * r, axis=-1, keepdims=True) + 1e-5)
            hbuf[pl.ds(off, 32), :] = (r * inv * nw).astype(BF16)
            return carry

        lax.fori_loop(0, HALF // 32, norm, 0)

        def expand(j, carry):
            for t in range(4):
                src = pl.ds(pl.multiple_of(j * 512 + t * 128, 128), 128)
                e = jnp.dot(hbuf[:, src], ex_s[...], preferred_element_type=F32).astype(BF16)
                cols = pl.ds(pl.multiple_of(j * 1024 + t * 256, 256), 256)
                hx[0:HALF, cols] = e[:, :256]
                hx[HALF:2 * HALF, cols] = e[:, 256:]
            return carry

        lax.fori_loop(0, feat // 512, expand, 0)
        if k == 0:
            old_copy.wait()
            win_copy.wait()
        p_acc[...] = jnp.zeros_like(p_acc)

        def chunk(c, carry, k=k):
            if k == 0:
                w_copy(c).wait()

                @pl.when(c + 3 < nchunk)
                def _():
                    w_copy(c + 3).start()
            else:
                for t in range(3):
                    st_copy(3 * c + t).start()

            sl = cols_of(c)
            rs = half_rows(k)
            acc = jnp.dot(hx[...], wbuf[c], preferred_element_type=F32)
            x = acc[:HALF].astype(BF16)
            z_s[rs, sl] = acc[HALF:].astype(BF16)
            cw[2, rs, sl] = x
            taps = conv_w[layer, :, sl].astype(F32)
            pre = cold[rs, sl].astype(F32) * taps[0:1] + cw[0, rs, sl].astype(F32) * taps[1:2]
            pre = pre + cw[1, rs, sl].astype(F32) * taps[2:3] + x.astype(F32) * taps[3:4]
            pre = pre + conv_b[layer:layer + 1, sl].astype(F32)
            xc = silu(pre).astype(BF16)
            xc_s[rs, sl] = xc
            p_acc[...] += lax.dot_general(w_x[layer, :, sl], xc, (((1,), (1,)), ((), ())), preferred_element_type=F32)
            if k == 1:
                @pl.when(c < 2)
                def _():
                    for t in range(4):
                        o_copy(4 * c + t).start()

                @pl.when(c == 2)
                def _():
                    for t in range(2):
                        o_copy(8 + t).start()
                    p_middle(0)

            return carry

        lax.fori_loop(0, nchunk, chunk, 0)
        p_own[k] = p_acc[...].astype(BF16)
        p_first(k).start()
    st_copy(2 * nblk - 1).start()

    def red_a(q):
        return send(theirs_a.at[q], got_a.at[q], 4 + q, partner)

    red_b = send(theirs_b, got_b, 6, partner)

    def quarter_rows(q):
        return pl.ds(q * quarter, quarter)

    def cross(q):
        return send(ua.at[quarter_rows(q)], va.at[quarter_rows(q)], 7 + q, other)

    def up_a(q):
        return send(ua.at[quarter_rows(q)], upa.at[quarter_rows(q)], 9 + q, partner)

    up_b = send(ub, upb, 11, partner)

    def forward(q):
        return send(va.at[quarter_rows(q)], vpa.at[quarter_rows(q)], 12 + q, partner)

    def reduce_a(q):
        red_a(q).wait_recv()
        ua[quarter_rows(q), :] = (mine_a[q] + got_a[q].astype(F32)).astype(BF16)
        cross(q).start()
        up_a(q).start()

    lane = lax.broadcasted_iota(jnp.int32, (nst, 128), 1)
    row = lax.broadcasted_iota(jnp.int32, (nst, 128), 0)

    def gated(rs, y):
        y = y + d_skip[layer:layer + 1, :] * xc_s[rs, :].astype(F32)
        return (y * silu(z_s[rs, :].astype(F32))).astype(BF16)

    def project(yg, first, dst, dtype):
        for t in range(half // NCH):
            j = first * (half // NCH) + t
            dst[:, t * NCH:(t + 1) * NCH] = jnp.dot(yg, out_tile(j)[...], preferred_element_type=F32).astype(dtype)

    for k in range(2):
        p_second(k).wait_recv()
        p = p_cs[k].astype(F32) + p_v[k].astype(F32)
        low = rms0(p[:rank]).astype(BF16)
        pre = lax.dot_general(low, w_dt[layer], (((0,), (0,)), ((), ())), preferred_element_type=F32)
        pre = pre + b_dt[layer:layer + 1, :]
        dt_s[...] = jnp.maximum(pre, 0.0) + jnp.log1p(jnp.exp(-jnp.abs(pre)))
        bc = jnp.concatenate([rms0(p[rank:rank + nst]), rms0(p[rank + nst:])], axis=0)
        bc_s[:, 0:2 * nst] = jnp.transpose(bc)

        def block(i, carry, k=k):
            st_copy(i + k * nblk).wait()
            local = pl.multiple_of(i * SB, SB)
            base = local + k * HALF
            dt = dt_s[pl.ds(local, SB), :]
            dtx = dt * xc_s[pl.ds(base, SB), :].astype(F32)
            bc = bc_s[pl.ds(local, SB), :]
            a2 = a_s[...]
            for b in range(SB):
                bcb = jnp.broadcast_to(bc[b:b + 1, :], (nst, 128))
                bcol = jnp.sum(jnp.where(lane == row, bcb, 0.0), axis=1, keepdims=True)
                ccol = jnp.sum(jnp.where(lane == row + nst, bcb, 0.0), axis=1, keepdims=True)
                s = jnp.exp2(dt[b:b + 1, :] * a2) * st[base + b] + dtx[b:b + 1, :] * bcol
                st[base + b] = s
                t = s * ccol
                part[b] = t[0:8] + t[8:16]
            for g in range(SB // 8):
                y_s[pl.ds(local + 8 * g, 8), :] = sublane_sums([part[8 * g + n] for n in range(8)])

            if k == 0:
                @pl.when(i == 2)
                def _():
                    p_middle(1)

                @pl.when(i == nblk // 2 - 1)
                def _():
                    for j in range(feat // NCH):
                        o_copy(j).wait()

                @pl.when(lax.rem(i, nblk // 2) == nblk // 2 - 1)
                def _():
                    q = i // (nblk // 2)
                    rs = pl.ds(pl.multiple_of(q * quarter, quarter), quarter)
                    yg = gated(rs, y_s[rs, :])
                    project(yg, 1 - core, theirs_a.at[q], BF16)
                    red_a(q).start()
                    project(yg, core, mine_a.at[q], F32)

                @pl.when(i == nblk // 2 + 1)
                def _():
                    reduce_a(0)
            else:
                @pl.when(i == 1)
                def _():
                    reduce_a(1)

            return carry

        lax.fori_loop(0, nblk, block, 0)

    yg = gated(half_rows(1), y_s[...])
    project(yg, 1 - core, theirs_b, BF16)
    red_b.start()
    project(yg, core, mine_b, F32)
    cross(0).wait_recv()
    forward(0).start()
    red_b.wait_recv()
    ub[...] = (mine_b[...] + got_b[...].astype(F32)).astype(BF16)
    up_b.start()
    cross(1).wait_recv()
    forward(1).start()
    for q in range(2):
        up_a(q).wait_recv()
    up_b.wait_recv()
    for q in range(2):
        forward(q).wait_recv()
    for k in range(2):
        p_first(k).wait_send()
        p_second(k).wait_send()
        red_a(k).wait_send()
        cross(k).wait_send()
        up_a(k).wait_send()
        forward(k).wait_send()
    red_b.wait_send()
    up_b.wait_send()
    if has_o:
        relay.wait_send()
        for k in range(2):
            pltpu.make_async_copy(rbuf.at[half_rows(k)], r_out.at[half_rows(k)], lsem.at[4 + k]).wait()


def layer_call(layer, residual, pieces, weights, conv_st, state):
    norm_w, w_in, conv_w, conv_b, w_x, w_dt, b_dt, a_log, d_skip, w_out = weights
    has_o = pieces is not None
    rows, feat = residual.shape
    chan = w_in.shape[3]
    nst = a_log.shape[1]
    half = feat // 2
    nproj = w_x.shape[1]
    nchunk = chan // NCH
    flat = list(pieces) if has_o else []
    args = [residual] + flat + [norm_w, w_in, conv_w, conv_b, w_x, conv_st, w_dt, b_dt, a_log, d_skip, w_out, state]
    specs = [ANY] + [VMEM] * len(flat) + [VMEM, ANY, VMEM, VMEM, VMEM, ANY, VMEM, VMEM, VMEM, VMEM, ANY, ANY]
    piece = pltpu.VMEM((HALF, half), BF16)
    outs = [pltpu.VMEM((rows, nst, chan), F32), pltpu.VMEM((3, rows, chan), BF16)] + [piece] * 6
    out_specs = [VMEM] * 8
    if has_o:
        outs.append(jax.ShapeDtypeStruct((rows, feat), F32))
        out_specs.append(ANY)
    vm = pltpu.VMEM
    dma = pltpu.SemaphoreType.DMA
    quarter = HALF // 2
    return pl.pallas_call(
        functools.partial(layer_kernel, layer, has_o),
        out_shape=outs, in_specs=specs, out_specs=out_specs,
        scratch_shapes=[
            vm((nchunk, 2 * feat, NCH), BF16), vm((2 * HALF, 2 * feat), BF16), vm((HALF, feat), BF16), vm((128, 512), BF16),
            vm((nproj, HALF), F32), vm((2, nproj, HALF), BF16), vm((2, nproj, HALF), BF16), vm((2, nproj, HALF), BF16),
            vm((2, nproj, HALF), BF16), vm((rows, feat), F32), vm((rows, chan), BF16), vm((rows, chan), BF16),
            vm((rows, chan), BF16), vm((HALF, chan), F32), vm((HALF, 128), F32), vm((nst, chan), F32), vm((HALF, chan), F32),
            vm((SB, 8, chan), F32), vm((2, quarter, half), F32), vm((HALF, half), F32), vm((2, quarter, half), BF16),
            vm((HALF, half), BF16), vm((2, quarter, half), BF16), vm((HALF, half), BF16), vm((HALF, half), BF16),
            dma((6,)), dma((nchunk,)), dma((rows // SB,)), dma((feat // NCH,)), dma((15,)), dma((15,)),
        ],
        compiler_params=pltpu.CompilerParams(vmem_limit_bytes=34 * 2 ** 20, collective_id=layer, has_side_effects=True),
        cost_estimate=pl.CostEstimate(flops=2 * 10 ** 10, bytes_accessed=46 * 2 ** 20, transcendentals=0),
    )(*args)


def w_kernel(layer, st, cw, *refs):
    ssm_out, conv_out, sem = refs[-3:]
    step = st.shape[0] // 8

    def copy(i):
        rs = pl.ds(i * step, step)
        return pltpu.make_async_copy(st.at[rs], ssm_out.at[layer, rs], sem.at[i])

    c_copy = pltpu.make_async_copy(cw, conv_out.at[layer], sem.at[8])
    for i in range(8):
        copy(i).start()
    c_copy.start()
    for i in range(8):
        copy(i).wait()
    c_copy.wait()


def w_call(layer, st, cw, shapes, prev):
    args = [pltpu.with_memory_space_constraint(a, pltpu.VMEM) for a in (st, cw)]
    specs = [VMEM, VMEM]
    alias = {}
    if prev is not None:
        alias = {2: 0, 3: 1}
        args += list(prev)
        specs += [ANY, ANY]
    return pl.pallas_call(
        functools.partial(w_kernel, layer),
        out_shape=[jax.ShapeDtypeStruct(shapes[0], F32), jax.ShapeDtypeStruct(shapes[1], BF16)],
        in_specs=specs, out_specs=[ANY, ANY], input_output_aliases=alias,
        scratch_shapes=[pltpu.SemaphoreType.DMA((9,))],
        compiler_params=pltpu.CompilerParams(vmem_limit_bytes=2 ** 20),
        cost_estimate=pl.CostEstimate(flops=2 * 10 ** 10, bytes_accessed=42 * 2 ** 20, transcendentals=0),
    )(*args)


def fin_kernel(r_ref, *refs):
    out = refs[-1]
    core = lax.rem(lax.axis_index('tp'), 2)
    half = out.shape[1] // 2
    lo = pl.ds(pl.multiple_of(core * half, 128), half)
    hi = pl.ds(pl.multiple_of((1 - core) * half, 128), half)
    for k in range(2):
        u, up, v, vp = refs[4 * k:4 * k + 4]
        rs = slice(k * HALF, (k + 1) * HALF)
        out[rs, lo] = r_ref[rs, lo] + (u[...].astype(F32) + v[...].astype(F32))
        out[rs, hi] = r_ref[rs, hi] + (up[...].astype(F32) + vp[...].astype(F32))


def fin_call(r1, pieces):
    return pl.pallas_call(
        fin_kernel, out_shape=jax.ShapeDtypeStruct(r1.shape, F32), in_specs=[VMEM] * 9, out_specs=VMEM,
        compiler_params=pltpu.CompilerParams(vmem_limit_bytes=16 * 2 ** 20), name="fin",
    )(r1, *pieces[0], *pieces[1])


PART = [(0, 1), (1, 0), (2, 3), (3, 2)]
CROSS = [(0, 2), (2, 0), (1, 3), (3, 1)]


def solution(mesh):
    def step(residual, norm_w, w_in, conv_w, conv_b, w_x, w_dt, b_dt, a_log, d_skip, w_out, conv_state, ssm_state):
        w_xt = jnp.transpose(w_x, (0, 2, 1))
        conv_t = jnp.transpose(conv_state, (0, 2, 1, 3))
        weights = (norm_w, w_in, conv_w, conv_b, w_xt, w_dt, b_dt, a_log, d_skip, w_out)
        shapes = (ssm_state.shape, conv_t.shape)
        r = residual
        written = None
        pieces = None
        for layer in range(norm_w.shape[0]):
            got = layer_call(layer, r, pieces, weights, conv_t, ssm_state)
            st, cw, ua, ub, upa, upb, va, vpa = got[:8]
            if pieces is not None:
                r = got[8]
            vb = lax.ppermute(ub, 'tp', CROSS)
            written = w_call(layer, st, cw, shapes, written)
            pieces = (ua, upa, va, vpa, ub, upb, vb)
        pieces = (pieces[:4], pieces[4:] + (lax.ppermute(pieces[6], 'tp', PART),))
        ssm_out, conv_out = written
        out = fin_call(r, pieces)
        return out, jnp.transpose(conv_out, (0, 2, 1, 3)), ssm_out

    cache_spec = P(None, 'dp', None, 'tp')
    in_specs = (P('dp', None), P(None, None), P(None, None, None, 'tp'), P(None, None, 'tp'), P(None, 'tp'), P(None, 'tp', None), P(None, None, 'tp'), P(None, 'tp'), P(None, None, 'tp'), P(None, 'tp'), P(None, 'tp', None), cache_spec, cache_spec)
    out_specs = (P('dp', None), cache_spec, cache_spec)
    return jax.shard_map(step, mesh=mesh, in_specs=in_specs, out_specs=out_specs, check_vma=False)
```

time: 277 us -> 123 us (0.44)
  other arithmetic: 115 us -> 0 us
  Pallas kernels: 0 us -> 92.5 us
  waiting for transfers between devices: 83.6 us -> 9.41 us
  matrix products: 31.4 us -> 0 us
  between operations: 14.3 us -> 0.72 us
  local copies, waits for them, and re-layouts: 31.9 us -> 18.9 us
    pallas_call x0 -> x5, Pallas kernels: none -> 92.5 us  [the longest x2 74.8 us: layer_call(): pl.pallas_call(functools.partial(layer_kernel, layer, has_o), out_shape=o...]
    psum x4 -> x0, waiting for transfers between devices: 83.5 us -> none  [the longest x2 47.9 us: device_step(): proj_sum = lax.psum(proj_part, 'tp').astype(jnp.float32)]
    reduce_sum x10 -> x0, other arithmetic: 38.4 us -> none  [the longest x2 33.4 us: device_step(): jnp.sum(new_ssm * c_vec[:, :, None], axis=1) + d_skip[layer_idx] * x_float]
    another operation x4 -> x0, other arithmetic: 37.9 us -> none  [device_step(): return (residual, jnp.stack(conv_list), jnp.stack(ssm_list))]
    add x3 -> x0, other arithmetic: 33.8 us -> none  [the longest x1 30.1 us: device_step(): decay_fac * ssm_state[layer_idx]]
    dot_general x8 -> x0, matrix products: 31.4 us -> none  [the longest x2 12.5 us: device_step(): jnp.dot(gated_y, w_out[layer_idx], preferred_element_type=jnp.float32)]
    slice x5 -> x0, local copies, waits for them, and re-layouts: 22.9 us -> none  [the longest x1 21.6 us: device_step(): w_in[layer_idx]]
    unnamed x70 -> x20, local copies, waits for them, and re-layouts: 4.3 us -> 18.9 us
  transfers between devices with their start and end apart: 4 -> 3, of which waited for: 4 -> 1; matrix products, arithmetic and copies ran while one was open for 14% -> 0% of each run, Pallas kernels for 0% -> 13%
where the time goes in v5:
time: 123 us
  Pallas kernels  92.5 us (75%)
  local copies, waits for them, and re-layouts  18.9 us (15%)
  waiting for transfers between devices  9.41 us (8%)
  starting transfers between devices  1.81 us (1%)
    pallas_call x2, Pallas kernels, layer_call(): pl.pallas_call(functools.partial(layer_kernel, layer, has_o), out_shape=o...  74.8 us
    unnamed x20, local copies, waits for them, and re-layouts  18.9 us
    pallas_call x2, Pallas kernels, w_call(): pl.pallas_call(functools.partial(w_kernel, layer), out_shape=[jax.ShapeDt...  15.9 us
    ppermute x2, waiting for transfers between devices, step(): vb = lax.ppermute(ub, 'tp', CROSS)  9.4 us
  transfers between devices with their start and end apart: 3, of which 1 were waited for; matrix products, arithmetic and copies ran while one was open for 0% of the time, Pallas kernels for 13%

profile of v5, /device:TPU:0, one launch (start us, length us, event | category | flops | bytes accessed | tf_op | source)
XLA Modules:
  0.0 123.3 jit_solution(7920424409837493190)
XLA Ops:
  0.6 38.0 %shard_map.148 = (f32[256,16,1280]{2,1,0:T(8,128)S(1)}, bf16[3,256,1280]{2,1,0:T(8,128)(2,1)S(1)}, bf16[128,1280]{1,0:T(8,128)(2,1)S(1)}, bf16[128,1280]{1,0:T(8...) custom-call(f32[256,2560]{1,0:T(8,128)} %refs_0_.3, ...), custom_call_target="tpu_custom_call" | custom-call | flops 20000000000 | bytes 48234496 | tf_op jit(solution)/shard_map/pallas_call | solution.py:374
  38.6 0.0 copy-start.1
  38.7 0.7 copy-done.1
  39.4 0.0 copy-start.3
  39.4 0.7 copy-done.3
  40.1 0.0 copy-start.4
  40.1 0.7 copy-done.4
  40.8 0.0 copy-start.5
  40.8 0.7 copy-done.5
  41.6 0.0 copy-start.6
  41.6 0.7 copy-done.6
  42.3 0.0 copy-start.7
  42.3 7.5 %copy-done.7 = f32[256,16,1280]{2,1,0:T(8,128)} copy-done((f32[256,16,1280]{2,1,0:T(8,128)}, f32[256,16,1280]{2,1,0:T(8,128)S(1)}, u32[]{:S(2)}) %copy-start.7) | copy-done | bytes 20971544
  49.9 0.0 copy-start.2
  49.9 0.3 collective-permute-start
  50.2 9.4 %collective-permute-done.refs_7_ = bf16[128,1280]{1,0:T(8,128)(2,1)S(1)} collective-permute-done((bf16[128,1280]{1,0:T(8,128)(2,1)S(1)}, bf16[128,1280]{1,0:T(8,128)(2,1)S(1)}, u32[]{:S(2)}, u32[]{:S(2)}) %collective-permute-start) | collective-permute-done | bytes 327712 | tf_op jit(solution)/shard_map/ppermute | solution.py:464
  59.6 0.0 copy-start.9
  59.6 0.0 copy-done.2
  59.6 0.7 copy-done.9
  60.3 36.7 %shard_map.149 = (f32[256,16,1280]{2,1,0:T(8,128)S(1)}, bf16[3,256,1280]{2,1,0:T(8,128)(2,1)S(1)}, bf16[128,1280]{1,0:T(8,128)(2,1)S(1)}, bf16[128,1280]{1,0:T(8...) custom-call(f32[256,2560]{1,0:T(8,128)} %refs_0_.3, ...), custom_call_target="tpu_custom_call" | custom-call | flops 20000000000 | bytes 48234496 | tf_op jit(solution)/shard_map/pallas_call | solution.py:374
  97.1 1.5 %collective-permute-start.1 = (bf16[128,1280]{1,0:T(8,128)(2,1)S(1)}, bf16[128,1280]{1,0:T(8,128)(2,1)S(1)}, u32[]{:S(2)}, u32[]{:S(2)}) collective-permute-start(bf16[128,1280]{1,0:T(8,128)(2,1)S(1)} %get-tuple-element.35.refs_4_), channel_id=1, source_target_pairs={{0,2},{2,0},{1,3},{3,1},{4,6},{6,4},{5,7},{7,5}} | collective-permute-start | bytes 983048 | tf_op jit(solution)/shard_map/ppermute | solution.py:464
  98.5 0.0 copy-start.8
  98.5 7.0 %copy-done.8 = f32[256,16,1280]{2,1,0:T(8,128)S(1)} copy-done((f32[256,16,1280]{2,1,0:T(8,128)S(1)}, f32[256,16,1280]{2,1,0:T(8,128)}, u32[]{:S(2)}) %copy-start.8) | copy-done | bytes 20971544
  105.5 7.8 %shard_map.150 = (f32[2,256,16,1280]{3,2,1,0:T(8,128)}, bf16[2,3,256,1280]{3,2,1,0:T(8,128)(2,1)}) custom-call(f32[256,16,1280]{2,1,0:T(8,128)S(1)} %copy-done.8, bf16[3,256,1280]{2,1,0:T(8,128)(2,1)S(1)} %get-tuple-element.40.cw), custom_call_target="tpu_custom_call" | custom-call | flops 20000000000 | bytes 44040192 | tf_op jit(solution)/shard_map/pallas_call | solution.py:416
  113.3 0.0 collective-permute-done.1.refs_6_
  113.3 0.0 collective-permute-start.2
  113.3 0.0 copy-start
  113.3 8.1 %shard_map.151 = (f32[2,256,16,1280]{3,2,1,0:T(8,128)}, bf16[2,3,256,1280]{3,2,1,0:T(8,128)(2,1)}) custom-call(f32[256,16,1280]{2,1,0:T(8,128)S(1)} %get-tuple-element.37.st, bf16[3,256,1280]{2,1,0:T(8,128)(2,1)S(1)} %get-tuple-element.38.cw, f32[2,256,16,1280]{3,2,1,0:T(8,128)} %get-tuple-element.41.refs_0_, ...), custom_call_target="tpu_custom_call", output_to_operand_aliasing={{0}: (2, {}), {1}: (3, {})} | custom-call | flops 20000000000 | bytes 44040192 | tf_op jit(solution)/shard_map/pallas_call | solution.py:416
  121.4 0.0 collective-permute-done.2.refs_7_
  121.4 0.0 copy-done
  121.4 1.9 %fin.1 = f32[256,2560]{1,0:T(8,128)} custom-call(f32[256,2560]{1,0:T(8,128)S(1)} %copy-done, bf16[128,1280]{1,0:T(8,128)(2,1)S(1)} %get-tuple-element.31.refs_0_, bf16[128,1280]{1,0:T(8,128)(2,1)S(1)} %get-tuple-element.32.refs_1_, bf16[128,1280]{1,0:T(8,128)(2,1)S(1)} %get-tuple-element.33.refs_2_, bf16[128,1280]{1,0:T(8,128)(2,1)S(1)} %get-tuple-element.34.refs_3_, ...), custom_call_target="tpu_custom_call" | custom-call | tf_op jit(solution)/shard_map/fin/pallas_call | solution.py:440
Async XLA Ops:
  38.6 0.7 copy-start.1
  39.4 0.7 copy-start.3
  40.1 0.7 copy-start.4
  40.8 0.7 copy-start.5
  41.6 0.7 copy-start.6
  42.3 7.5 %copy-start.7 = (f32[256,16,1280]{2,1,0:T(8,128)}, f32[256,16,1280]{2,1,0:T(8,128)S(1)}, u32[]{:S(2)}) copy-start(f32[256,16,1280]{2,1,0:T(8,128)S(1)} %get-tuple-element.39.st) | copy-start | bytes 62914564
  49.9 9.7 %copy-start.2 = (bf16[128,1280]{1,0:T(8,128)(2,1)}, bf16[128,1280]{1,0:T(8,128)(2,1)S(1)}, u32[]{:S(2)}) copy-start(bf16[128,1280]{1,0:T(8,128)(2,1)S(1)} %get-tuple-element.28.refs_5_) | copy-start | bytes 983044
  49.9 9.7 %collective-permute-start = (bf16[128,1280]{1,0:T(8,128)(2,1)S(1)}, bf16[128,1280]{1,0:T(8,128)(2,1)S(1)}, u32[]{:S(2)}, u32[]{:S(2)}) collective-permute-start(bf16[128,1280]{1,0:T(8,128)(2,1)S(1)} %get-tuple-element.28.refs_5_), channel_id=1, source_target_pairs={{0,2},{2,0},{1,3},{3,1},{4,6},{6,4},{5,7},{7,5}} | collective-permute-start | bytes 983048 | tf_op jit(solution)/shard_map/ppermute | solution.py:464
  59.6 0.7 copy-start.9
  97.1 16.2 %collective-permute-start.1 = (bf16[128,1280]{1,0:T(8,128)(2,1)S(1)}, bf16[128,1280]{1,0:T(8,128)(2,1)S(1)}, u32[]{:S(2)}, u32[]{:S(2)}) collective-permute-start(bf16[128,1280]{1,0:T(8,128)(2,1)S(1)} %get-tuple-element.35.refs_4_), channel_id=1, source_target_pairs={{0,2},{2,0},{1,3},{3,1},{4,6},{6,4},{5,7},{7,5}} | collective-permute-start | bytes 983048 | tf_op jit(solution)/shard_map/ppermute | solution.py:464
  98.5 7.0 %copy-start.8 = (f32[256,16,1280]{2,1,0:T(8,128)S(1)}, f32[256,16,1280]{2,1,0:T(8,128)}, u32[]{:S(2)}) copy-start(f32[256,16,1280]{2,1,0:T(8,128)} %copy-done.7) | copy-start | bytes 62914564
  113.3 8.1 %collective-permute-start.2 = (bf16[128,1280]{1,0:T(8,128)(2,1)S(1)}, bf16[128,1280]{1,0:T(8,128)(2,1)S(1)}, u32[]{:S(2)}, u32[]{:S(2)}) collective-permute-start(bf16[128,1280]{1,0:T(8,128)(2,1)S(1)} %collective-permute-done.1.refs_6_), channel_id=1, source_target_pairs={{0,1},{1,0},{2,3},{3,2},{4,5},{5,4},{6,7},{7,6}} | collective-permute-start | bytes 983048 | tf_op jit(solution)/shard_map/ppermute | solution.py:467
  113.3 8.1 %copy-start = (f32[256,2560]{1,0:T(8,128)S(1)}, f32[256,2560]{1,0:T(8,128)}, u32[]{:S(2)}) copy-start(f32[256,2560]{1,0:T(8,128)} %get-tuple-element.30.r_ref) | copy-start | bytes 7864324

commit v6 on v5

v6 whole, which is shorter than its diff:
```python
import functools
import math

import jax
import jax.numpy as jnp
from jax import lax
from jax.experimental import pallas as pl
from jax.experimental.pallas import tpu as pltpu
from jax.sharding import PartitionSpec as P


F32 = jnp.float32
BF16 = jnp.bfloat16
ANY = pl.BlockSpec(memory_space=pltpu.HBM)
VMEM = pl.BlockSpec(memory_space=pltpu.VMEM)
NCH = 256
SB = 16
HALF = 128
LOG2E = math.log2(math.e)
MESH = pl.DeviceIdType.MESH


def silu(v):
    return v * jax.nn.sigmoid(v)


def expand_matrix():
    row = lax.broadcasted_iota(jnp.int32, (128, 512), 0)
    col = lax.broadcasted_iota(jnp.int32, (128, 512), 1)
    target = 2 * row + jnp.where(col < 256, 0, 257)
    return jnp.where(col == target, 1.0, 0.0).astype(BF16)


def rms0(v):
    return v * lax.rsqrt(jnp.mean(v * v, axis=0, keepdims=True) + 1e-6)


def sublane_sums(parts):
    sub = lax.broadcasted_iota(jnp.int32, parts[0].shape, 0)
    for step in (4, 2, 1):
        keep = (sub & step) == 0
        half = len(parts) // 2
        parts = [jnp.where(keep, parts[k], parts[k + half])
                 + pltpu.roll(jnp.where(keep, parts[k + half], parts[k]), step, 0) if step == 4 else
                 jnp.where(keep, parts[k], parts[k + half])
                 + jnp.where(keep, pltpu.roll(parts[k], 8 - step, 0), pltpu.roll(parts[k + half], step, 0))
                 for k in range(half)]
    return parts[0]


def add_pieces(rbuf, start, sides, u, up, v, vp):
    lo, hi = sides

    def add(i, carry):
        src = pl.ds(pl.multiple_of(i * 32, 32), 32)
        dst = pl.ds(pl.multiple_of(i * 32, 32) + start, 32)
        rbuf[dst, lo] = rbuf[dst, lo] + (u[src, :].astype(F32) + v[src, :].astype(F32))
        rbuf[dst, hi] = rbuf[dst, hi] + (up[src, :].astype(F32) + vp[src, :].astype(F32))
        return carry

    lax.fori_loop(0, HALF // 32, add, 0)


def norm_expand(rbuf, start, norm_row, hbuf, ex_s, hx):
    nw = norm_row.astype(F32)
    feat = rbuf.shape[1]

    def norm(i, carry):
        off = pl.multiple_of(i * 32, 32)
        r = rbuf[pl.ds(off + start, 32), :]
        inv = lax.rsqrt(jnp.mean(r * r, axis=-1, keepdims=True) + 1e-5)
        hbuf[pl.ds(off, 32), :] = (r * inv * nw).astype(BF16)
        return carry

    lax.fori_loop(0, HALF // 32, norm, 0)

    def expand(j, carry):
        for t in range(4):
            src = pl.ds(pl.multiple_of(j * 512 + t * 128, 128), 128)
            e = jnp.dot(hbuf[:, src], ex_s[...], preferred_element_type=F32).astype(BF16)
            cols = pl.ds(pl.multiple_of(j * 1024 + t * 256, 256), 256)
            hx[0:HALF, cols] = e[:, :256]
            hx[HALF:2 * HALF, cols] = e[:, 256:]
        return carry

    lax.fori_loop(0, feat // 512, expand, 0)


def cols_of(c):
    return pl.ds(pl.multiple_of(c * NCH, NCH), NCH)


def in_chunk(layer, c, hx, wbuf, conv_w, conv_b, window, z_out, xc_out):
    old0, old1, old2, x_out = window
    sl = cols_of(c)
    acc = jnp.dot(hx[...], wbuf[c], preferred_element_type=F32)
    x = acc[:HALF].astype(BF16)
    z_out[:, sl] = acc[HALF:].astype(BF16)
    x_out[:, sl] = x
    taps = conv_w[layer, :, sl].astype(F32)
    pre = old0[:, sl].astype(F32) * taps[0:1] + old1[:, sl].astype(F32) * taps[1:2]
    pre = pre + old2[:, sl].astype(F32) * taps[2:3] + x.astype(F32) * taps[3:4]
    pre = pre + conv_b[layer:layer + 1, sl].astype(F32)
    xc_out[:, sl] = silu(pre).astype(BF16)


def x_project(w_x_layer, xc):
    return lax.dot_general(w_x_layer, xc, (((1,), (1,)), ((), ())), preferred_element_type=F32).astype(BF16)


def halves_of(core, half):
    return (pl.ds(pl.multiple_of(core * half, 128), half), pl.ds(pl.multiple_of((1 - core) * half, 128), half))


def layer_kernel(layer, first, *refs):
    refs = list(refs)
    res = refs.pop(0)
    if not first:
        ub_in, vb_in, z_a, xc_a, p_a = refs[:5]
        refs = refs[5:]
    (norm_w, w_in, conv_w, conv_b, w_x, conv_st, w_dt, b_dt, a_log, d_skip, w_out, state) = refs[:12]
    refs = refs[12:]
    st, cw, ua, ub, upa, va, vpa = refs[:7]
    refs = refs[7:]
    r_out = None if first else refs.pop(0)
    (wbuf, hx, hbuf, ex_s, p_own, p_sw, p_cs, p_v, rbuf, cold, z_s, xc_s, dt_s, bc_s, a_s, y_s, part,
     mine_a, mine_b, theirs_a, theirs_b, got_a, got_b, upb, vpb, lsem, wsem, stsem, osem, ssem, rsem) = refs
    feat = rbuf.shape[1]
    nchunk = wbuf.shape[0]
    chan = z_s.shape[1]
    rank = w_dt.shape[1]
    nst = a_s.shape[0]
    nblk = HALF // SB
    half = feat // 2
    quarter = HALF // 2
    w_flat = w_in.reshape(w_in.shape[0], 2 * feat, w_in.shape[3])
    in_halves = (0, 1) if first else (1,)

    me = lax.axis_index('tp')
    core = lax.rem(me, 2)
    partner = me + 1 - 2 * core
    other = lax.rem(me + 2, 4)
    barrier = pltpu.get_barrier_semaphore()
    for dev in (partner, other):
        pl.semaphore_signal(barrier, inc=1, device_id={'tp': dev}, device_id_type=MESH)

    def send(src, dst, k, dev):
        return pltpu.make_async_remote_copy(src_ref=src, dst_ref=dst, send_sem=ssem.at[k], recv_sem=rsem.at[k],
                                            device_id={'tp': dev}, device_id_type=MESH)

    def half_rows(k):
        return pl.ds(k * HALF, HALF)

    def held_rows(k):
        return pl.ds(k * HALF if first else 0, HALF)

    def r_copy(k):
        return pltpu.make_async_copy(res.at[half_rows(k)], rbuf.at[held_rows(k)], lsem.at[k])

    nwin = cold.shape[0]
    win_rows = pl.ds(0 if first else HALF, nwin)
    old_copy = pltpu.make_async_copy(conv_st.at[layer, 0, win_rows], cold, lsem.at[2])
    win_copy = pltpu.make_async_copy(conv_st.at[layer, pl.ds(1, 2), win_rows], cw.at[pl.ds(0, 2)], lsem.at[3])

    def w_copy(c):
        return pltpu.make_async_copy(w_flat.at[layer, :, cols_of(c)], wbuf.at[c], wsem.at[c])

    def st_copy(i):
        rs = pl.ds(i * SB, SB)
        return pltpu.make_async_copy(state.at[layer, rs], st.at[rs], stsem.at[i])

    def out_tile(j):
        return wbuf.at[j // 4, pl.ds(pl.multiple_of(lax.rem(j, 4) * chan, 128), chan)]

    def o_copy(j):
        return pltpu.make_async_copy(w_out.at[layer, :, cols_of(j)], out_tile(j), osem.at[j])

    r_copy(in_halves[0]).start()
    w_copy(0).start()
    if first:
        r_copy(1).start()
    w_copy(1).start()
    old_copy.start()
    win_copy.start()
    w_copy(2).start()
    ex_s[...] = expand_matrix()
    a_s[...] = -jnp.exp(a_log[layer]) * LOG2E
    pl.semaphore_wait(barrier, 2)
    relays = []
    if not first:
        relays = [send(vb_in, vpb, 11, partner), send(ub_in, upb, 14, partner)]
        for c in relays:
            c.start()

    def p_first(k):
        return send(p_own.at[k], p_sw.at[k], k, partner)

    def p_second(k):
        return send(p_cs.at[k], p_v.at[k], 2 + k, other)

    def p_middle(k):
        p_first(k).wait_recv()
        p_cs[k] = (p_own[k].astype(F32) + p_sw[k].astype(F32)).astype(BF16)
        p_second(k).start()

    if not first:
        p_own[0] = p_a[...]
        p_first(0).start()
        xc_s[0:HALF, :] = xc_a[...]
        z_s[0:HALF, :] = z_a[...]
    for k in in_halves:
        start = k * HALF if first else 0
        r_copy(k).wait()
        if not first:
            for c in relays:
                c.wait_recv()
            add_pieces(rbuf, start, halves_of(core, half), ub_in, upb, vb_in, vpb)
            pltpu.make_async_copy(rbuf, r_out, lsem.at[4]).start()
        norm_expand(rbuf, start, norm_w[layer:layer + 1, :], hbuf, ex_s, hx)
        if k == in_halves[0]:
            old_copy.wait()
            win_copy.wait()

        def chunk(c, carry, k=k):
            if k == in_halves[0]:
                w_copy(c).wait()

                @pl.when(c + 3 < nchunk)
                def _():
                    w_copy(c + 3).start()

            if k == 1:
                for t in range(3):
                    st_copy(3 * c + t).start()
            held = held_rows(k)
            window = (cold.at[held], cw.at[0, held], cw.at[1, held], cw.at[2, held])
            in_chunk(layer, c, hx, wbuf, conv_w, conv_b, window, z_s.at[half_rows(k)], xc_s.at[half_rows(k)])
            if k == 1:
                @pl.when(c < 2)
                def _():
                    for t in range(4):
                        o_copy(4 * c + t).start()

                @pl.when(c == 2)
                def _():
                    for t in range(2):
                        o_copy(8 + t).start()
                    p_middle(0)

            return carry

        lax.fori_loop(0, nchunk, chunk, 0)
        p_own[k] = x_project(w_x[layer], xc_s[half_rows(k), :])
        p_first(k).start()
    st_copy(2 * nblk - 1).start()

    def red_a(q):
        return send(theirs_a.at[q], got_a.at[q], 4 + q, partner)

    red_b = send(theirs_b, got_b, 6, partner)

    def quarter_rows(q):
        return pl.ds(q * quarter, quarter)

    def cross(q):
        return send(ua.at[quarter_rows(q)], va.at[quarter_rows(q)], 7 + q, other)

    def up_a(q):
        return send(ua.at[quarter_rows(q)], upa.at[quarter_rows(q)], 9 + q, partner)

    def forward(q):
        return send(va.at[quarter_rows(q)], vpa.at[quarter_rows(q)], 12 + q, partner)

    def reduce_a(q):
        red_a(q).wait_recv()
        ua[quarter_rows(q), :] = (mine_a[q] + got_a[q].astype(F32)).astype(BF16)
        cross(q).start()
        up_a(q).start()

    lane = lax.broadcasted_iota(jnp.int32, (nst, 128), 1)
    row = lax.broadcasted_iota(jnp.int32, (nst, 128), 0)

    def gated(rs, y):
        y = y + d_skip[layer:layer + 1, :] * xc_s[rs, :].astype(F32)
        return (y * silu(z_s[rs, :].astype(F32))).astype(BF16)

    def project(yg, first, dst, dtype):
        for t in range(half // NCH):
            j = first * (half // NCH) + t
            dst[:, t * NCH:(t + 1) * NCH] = jnp.dot(yg, out_tile(j)[...], preferred_element_type=F32).astype(dtype)

    for k in range(2):
        p_second(k).wait_recv()
        p = p_cs[k].astype(F32) + p_v[k].astype(F32)
        low = rms0(p[:rank]).astype(BF16)
        pre = lax.dot_general(low, w_dt[layer], (((0,), (0,)), ((), ())), preferred_element_type=F32)
        pre = pre + b_dt[layer:layer + 1, :]
        dt_s[...] = jnp.maximum(pre, 0.0) + jnp.log1p(jnp.exp(-jnp.abs(pre)))
        bc = jnp.concatenate([rms0(p[rank:rank + nst]), rms0(p[rank + nst:])], axis=0)
        bc_s[:, 0:2 * nst] = jnp.transpose(bc)

        def block(i, carry, k=k):
            st_copy(i + k * nblk).wait()
            local = pl.multiple_of(i * SB, SB)
            base = local + k * HALF
            dt = dt_s[pl.ds(local, SB), :]
            dtx = dt * xc_s[pl.ds(base, SB), :].astype(F32)
            bc = bc_s[pl.ds(local, SB), :]
            a2 = a_s[...]
            for b in range(SB):
                bcb = jnp.broadcast_to(bc[b:b + 1, :], (nst, 128))
                bcol = jnp.sum(jnp.where(lane == row, bcb, 0.0), axis=1, keepdims=True)
                ccol = jnp.sum(jnp.where(lane == row + nst, bcb, 0.0), axis=1, keepdims=True)
                s = jnp.exp2(dt[b:b + 1, :] * a2) * st[base + b] + dtx[b:b + 1, :] * bcol
                st[base + b] = s
                t = s * ccol
                part[b] = t[0:8] + t[8:16]
            for g in range(SB // 8):
                y_s[pl.ds(local + 8 * g, 8), :] = sublane_sums([part[8 * g + n] for n in range(8)])

            if k == 0:
                @pl.when(i == 2)
                def _():
                    p_middle(1)

                @pl.when(i == nblk // 2 - 1)
                def _():
                    for j in range(feat // NCH):
                        o_copy(j).wait()

                @pl.when(lax.rem(i, nblk // 2) == nblk // 2 - 1)
                def _():
                    q = i // (nblk // 2)
                    rs = pl.ds(pl.multiple_of(q * quarter, quarter), quarter)
                    yg = gated(rs, y_s[rs, :])
                    project(yg, 1 - core, theirs_a.at[q], BF16)
                    red_a(q).start()
                    project(yg, core, mine_a.at[q], F32)

                @pl.when(i == nblk // 2 + 1)
                def _():
                    reduce_a(0)
            else:
                @pl.when(i == 1)
                def _():
                    reduce_a(1)

            return carry

        lax.fori_loop(0, nblk, block, 0)

    yg = gated(half_rows(1), y_s[...])
    project(yg, 1 - core, theirs_b, BF16)
    red_b.start()
    project(yg, core, mine_b, F32)
    cross(0).wait_recv()
    forward(0).start()
    red_b.wait_recv()
    ub[...] = (mine_b[...] + got_b[...].astype(F32)).astype(BF16)
    cross(1).wait_recv()
    forward(1).start()
    for q in range(2):
        up_a(q).wait_recv()
    for q in range(2):
        forward(q).wait_recv()
    for k in range(2):
        p_first(k).wait_send()
        p_second(k).wait_send()
        red_a(k).wait_send()
        cross(k).wait_send()
        up_a(k).wait_send()
        forward(k).wait_send()
    red_b.wait_send()
    for c in relays:
        c.wait_send()
    if not first:
        pltpu.make_async_copy(rbuf, r_out, lsem.at[4]).wait()


def layer_call(layer, residual, ready, weights, conv_st, state):
    norm_w, w_in, conv_w, conv_b, w_x, w_dt, b_dt, a_log, d_skip, w_out = weights
    first = ready is None
    rows, feat = residual.shape
    chan = w_in.shape[3]
    nst = a_log.shape[1]
    half = feat // 2
    nproj = w_x.shape[1]
    nchunk = chan // NCH
    flat = [] if first else list(ready)
    held = rows if first else HALF
    args = [residual] + flat + [norm_w, w_in, conv_w, conv_b, w_x, conv_st, w_dt, b_dt, a_log, d_skip, w_out, state]
    specs = [ANY] + [VMEM] * len(flat) + [VMEM, ANY, VMEM, VMEM, VMEM, ANY, VMEM, VMEM, VMEM, VMEM, ANY, ANY]
    piece = pltpu.VMEM((HALF, half), BF16)
    outs = [pltpu.VMEM((rows, nst, chan), F32), pltpu.VMEM((3, held, chan), BF16)] + [piece] * 5
    out_specs = [VMEM] * 7
    if not first:
        outs.append(jax.ShapeDtypeStruct((HALF, feat), F32))
        out_specs.append(ANY)
    vm = pltpu.VMEM
    dma = pltpu.SemaphoreType.DMA
    quarter = HALF // 2
    return pl.pallas_call(
        functools.partial(layer_kernel, layer, first),
        out_shape=outs, in_specs=specs, out_specs=out_specs,
        scratch_shapes=[
            vm((nchunk, 2 * feat, NCH), BF16), vm((2 * HALF, 2 * feat), BF16), vm((HALF, feat), BF16), vm((128, 512), BF16),
            vm((2, nproj, HALF), BF16), vm((2, nproj, HALF), BF16), vm((2, nproj, HALF), BF16),
            vm((2, nproj, HALF), BF16), vm((held, feat), F32), vm((held, chan), BF16), vm((rows, chan), BF16),
            vm((rows, chan), BF16), vm((HALF, chan), F32), vm((HALF, 128), F32), vm((nst, chan), F32), vm((HALF, chan), F32),
            vm((SB, 8, chan), F32), vm((2, quarter, half), F32), vm((HALF, half), F32), vm((2, quarter, half), BF16),
            vm((HALF, half), BF16), vm((2, quarter, half), BF16), vm((HALF, half), BF16), vm((HALF, half), BF16),
            vm((HALF, half), BF16),
            dma((5,)), dma((nchunk,)), dma((rows // SB,)), dma((feat // NCH,)), dma((15,)), dma((15,)),
        ],
        compiler_params=pltpu.CompilerParams(vmem_limit_bytes=34 * 2 ** 20, collective_id=layer, has_side_effects=True),
        cost_estimate=pl.CostEstimate(flops=2 * 10 ** 10, bytes_accessed=46 * 2 ** 20, transcendentals=0),
    )(*args)


def mid_kernel(layer, st, cw, res, ua, upa, va, vpa, norm_w, w_in, conv_w, conv_b, w_x, conv_st,
               ssm_out, conv_out, z_a, xc_a, p_a, cw_a, r_a,
               wbuf, hx, hbuf, ex_s, rbuf, cold, lsem, wsem, sem):
    feat = rbuf.shape[1]
    nchunk = wbuf.shape[0]
    nxt = layer + 1
    w_flat = w_in.reshape(w_in.shape[0], 2 * feat, w_in.shape[3])
    rows_a = pl.ds(0, HALF)

    def w_copy(c):
        return pltpu.make_async_copy(w_flat.at[nxt, :, cols_of(c)], wbuf.at[c], wsem.at[c])

    def st_copy(i):
        rs = pl.ds(i * SB, SB)
        return pltpu.make_async_copy(st.at[rs], ssm_out.at[layer, rs], sem.at[i])

    nst = st.shape[0] // SB
    r_copy = pltpu.make_async_copy(res.at[rows_a], rbuf, lsem.at[0])
    old_copy = pltpu.make_async_copy(conv_st.at[nxt, 0, rows_a], cold, lsem.at[1])
    win_copy = pltpu.make_async_copy(conv_st.at[nxt, pl.ds(1, 2), rows_a], cw_a.at[pl.ds(0, 2)], lsem.at[2])
    r_back = pltpu.make_async_copy(rbuf, r_a, lsem.at[3])
    c_copy = pltpu.make_async_copy(cw, conv_out.at[layer], lsem.at[4])
    r_copy.start()
    w_copy(0).start()
    old_copy.start()
    win_copy.start()
    w_copy(1).start()
    w_copy(2).start()
    ex_s[...] = expand_matrix()
    core = lax.rem(lax.axis_index('tp'), 2)
    r_copy.wait()
    st_copy(nst - 1).start()
    c_copy.start()
    add_pieces(rbuf, 0, halves_of(core, feat // 2), ua, upa, va, vpa)
    r_back.start()
    norm_expand(rbuf, 0, norm_w[nxt:nxt + 1, :], hbuf, ex_s, hx)
    old_copy.wait()
    win_copy.wait()
    window = (cold, cw_a.at[0], cw_a.at[1], cw_a.at[2])

    def chunk(c, carry):
        w_copy(c).wait()

        @pl.when(c + 3 < nchunk)
        def _():
            w_copy(c + 3).start()

        for t in range(3):
            st_copy(3 * c + t).start()
        in_chunk(nxt, c, hx, wbuf, conv_w, conv_b, window, z_a, xc_a)
        return carry

    lax.fori_loop(0, nchunk, chunk, 0)
    p_a[...] = x_project(w_x[nxt], xc_a[...])
    c_copy.wait()
    r_back.wait()
    for i in range(nst):
        st_copy(i).wait()


def mid_call(layer, st, cw, residual, pieces, weights, conv_st, shapes):
    norm_w, w_in, conv_w, conv_b, w_x = weights[:5]
    feat = residual.shape[1]
    chan = w_in.shape[3]
    nchunk = chan // NCH
    vm = pltpu.VMEM
    dma = pltpu.SemaphoreType.DMA
    args = [pltpu.with_memory_space_constraint(a, pltpu.VMEM) for a in (st, cw)]
    args += [residual, *pieces, norm_w, w_in, conv_w, conv_b, w_x, conv_st]
    return pl.pallas_call(
        functools.partial(mid_kernel, layer),
        out_shape=[jax.ShapeDtypeStruct(shapes[0], F32), jax.ShapeDtypeStruct(shapes[1], BF16),
                   vm((HALF, chan), BF16), vm((HALF, chan), BF16), vm((w_x.shape[1], HALF), BF16),
                   vm((3, HALF, chan), BF16), jax.ShapeDtypeStruct((HALF, feat), F32)],
        in_specs=[VMEM, VMEM, ANY] + [VMEM] * 4 + [VMEM, ANY, VMEM, VMEM, VMEM, ANY],
        out_specs=[ANY, ANY, VMEM, VMEM, VMEM, VMEM, ANY],
        scratch_shapes=[vm((nchunk, 2 * feat, NCH), BF16), vm((2 * HALF, 2 * feat), BF16), vm((HALF, feat), BF16),
                        vm((128, 512), BF16), vm((HALF, feat), F32), vm((HALF, chan), BF16),
                        dma((5,)), dma((nchunk,)), dma((st.shape[0] // SB,))],
        compiler_params=pltpu.CompilerParams(vmem_limit_bytes=22 * 2 ** 20),
        cost_estimate=pl.CostEstimate(flops=2 * 10 ** 10, bytes_accessed=42 * 2 ** 20, transcendentals=0),
    )(*args)


def w_kernel(layer, st, cw_a, cw_b, ssm_prev, conv_prev, ssm_out, conv_out, sem):
    def copy(i):
        rs = pl.ds(i * SB, SB)
        return pltpu.make_async_copy(st.at[rs], ssm_out.at[layer, rs], sem.at[i])

    n = st.shape[0] // SB
    copies = [copy(i) for i in range(n)]
    for k, src in enumerate((cw_a, cw_b)):
        copies.append(pltpu.make_async_copy(src, conv_out.at[layer, :, pl.ds(k * HALF, HALF)], sem.at[n + k]))
    for c in copies:
        c.start()
    for c in copies:
        c.wait()


def w_call(layer, st, cw_a, cw_b, prev):
    args = [pltpu.with_memory_space_constraint(a, pltpu.VMEM) for a in (st, cw_a, cw_b)]
    return pl.pallas_call(
        functools.partial(w_kernel, layer),
        out_shape=[jax.ShapeDtypeStruct(a.shape, a.dtype) for a in prev],
        in_specs=[VMEM, VMEM, VMEM, ANY, ANY], out_specs=[ANY, ANY], input_output_aliases={3: 0, 4: 1},
        scratch_shapes=[pltpu.SemaphoreType.DMA((st.shape[0] // SB + 2,))],
        compiler_params=pltpu.CompilerParams(vmem_limit_bytes=2 ** 20),
        cost_estimate=pl.CostEstimate(flops=2 * 10 ** 10, bytes_accessed=42 * 2 ** 20, transcendentals=0),
    )(*args, *prev)


def fin_kernel(r_a, r_b, *refs):
    out = refs[-1]
    core = lax.rem(lax.axis_index('tp'), 2)
    half = out.shape[1] // 2
    lo = pl.ds(pl.multiple_of(core * half, 128), half)
    hi = pl.ds(pl.multiple_of((1 - core) * half, 128), half)
    for k in range(2):
        u, up, v, vp = refs[4 * k:4 * k + 4]
        rs = slice(k * HALF, (k + 1) * HALF)
        r = (r_a, r_b)[k]
        out[rs, lo] = r[:, lo] + (u[...].astype(F32) + v[...].astype(F32))
        out[rs, hi] = r[:, hi] + (up[...].astype(F32) + vp[...].astype(F32))


def fin_call(r_a, r_b, pieces):
    return pl.pallas_call(
        fin_kernel, out_shape=jax.ShapeDtypeStruct((2 * HALF, r_a.shape[1]), F32), in_specs=[VMEM] * 10, out_specs=VMEM,
        compiler_params=pltpu.CompilerParams(vmem_limit_bytes=16 * 2 ** 20), name="fin",
    )(r_a, r_b, *pieces[0], *pieces[1])


PART = [(0, 1), (1, 0), (2, 3), (3, 2)]
CROSS = [(0, 2), (2, 0), (1, 3), (3, 1)]


def solution(mesh):
    def step(residual, norm_w, w_in, conv_w, conv_b, w_x, w_dt, b_dt, a_log, d_skip, w_out, conv_state, ssm_state):
        w_xt = jnp.transpose(w_x, (0, 2, 1))
        conv_t = jnp.transpose(conv_state, (0, 2, 1, 3))
        weights = (norm_w, w_in, conv_w, conv_b, w_xt, w_dt, b_dt, a_log, d_skip, w_out)
        shapes = (ssm_state.shape, conv_t.shape)
        st, cw, ua, ub, upa, va, vpa = layer_call(0, residual, None, weights, conv_t, ssm_state)
        vb = lax.ppermute(ub, 'tp', CROSS)
        *written, z_a, xc_a, p_a, cw_a, r_a = mid_call(0, st, cw, residual, (ua, upa, va, vpa), weights, conv_t, shapes)
        ready = (ub, vb, z_a, xc_a, p_a)
        st, cw_b, ua, ub, upa, va, vpa, r_b = layer_call(1, residual, ready, weights, conv_t, ssm_state)
        vb = lax.ppermute(ub, 'tp', CROSS)
        upb = lax.ppermute(ub, 'tp', PART)
        ssm_out, conv_out = w_call(1, st, cw_a, cw_b, written)
        vpb = lax.ppermute(vb, 'tp', PART)
        out = fin_call(r_a, r_b, ((ua, upa, va, vpa), (ub, upb, vb, vpb)))
        return out, jnp.transpose(conv_out, (0, 2, 1, 3)), ssm_out

    cache_spec = P(None, 'dp', None, 'tp')
    in_specs = (P('dp', None), P(None, None), P(None, None, None, 'tp'), P(None, None, 'tp'), P(None, 'tp'), P(None, 'tp', None), P(None, None, 'tp'), P(None, 'tp'), P(None, None, 'tp'), P(None, 'tp'), P(None, 'tp', None), cache_spec, cache_spec)
    out_specs = (P('dp', None), cache_spec, cache_spec)
    return jax.shard_map(step, mesh=mesh, in_specs=in_specs, out_specs=out_specs, check_vma=False)
```

time: 123 us -> 118 us (0.959)
  Pallas kernels: 92.5 us -> 88.6 us
  local copies, waits for them, and re-layouts: 18.9 us -> 17.3 us
    pallas_call x2 -> x1, Pallas kernels: 15.9 us -> 7.85 us  [w_call(): pl.pallas_call(functools.partial(w_kernel, layer), out_shape=[jax.ShapeDt...]
    pallas_call x3 -> x4, Pallas kernels: 76.6 us -> 80.7 us  [the longest x2 65.8 us: layer_call(): pl.pallas_call(functools.partial(layer_kernel, layer, first), out_shape=o...]
    unnamed x20 -> x26, local copies, waits for them, and re-layouts: 18.9 us -> 17.3 us
  transfers between devices with their start and end apart: 3 -> 4, of which waited for: 1 -> 1; matrix products, arithmetic and copies ran while one was open for 0% -> 0% of each run, Pallas kernels for 13% -> 18%
where the time goes in v6:
time: 118 us; the launch traced here: 117 us
  Pallas kernels  88.6 us (75%)
  local copies, waits for them, and re-layouts  17.3 us (15%)
  waiting for transfers between devices  8.67 us (7%)
  starting transfers between devices  2.17 us (2%)
    pallas_call x2, Pallas kernels, layer_call(): pl.pallas_call(functools.partial(layer_kernel, layer, first), out_shape=o...  65.8 us
    unnamed x26, local copies, waits for them, and re-layouts  17.3 us
    pallas_call x1, Pallas kernels, mid_call(): pl.pallas_call(functools.partial(mid_kernel, layer), out_shape=[jax.Shape...  13 us
    ppermute x2, waiting for transfers between devices, step(): vb = lax.ppermute(ub, 'tp', CROSS)  8.66 us
    pallas_call x1, Pallas kernels, w_call(): pl.pallas_call(functools.partial(w_kernel, layer), out_shape=[jax.ShapeDt...  7.85 us
  transfers between devices with their start and end apart: 4, of which 1 were waited for; matrix products, arithmetic and copies ran while one was open for 0% of the time, Pallas kernels for 18%

profile of v6, /device:TPU:0, one launch (start us, length us, event | category | flops | bytes accessed | tf_op | source)
XLA Modules:
  0.0 117.5 jit_solution(17004865954274987512)
XLA Ops:
  0.6 0.0 copy-start
  0.6 0.0 copy-start.1
  0.7 0.0 copy-start.6
  0.7 0.0 copy-start.8
  0.7 0.0 copy-start.9
  0.7 36.1 %shard_map.148 = (f32[256,16,1280]{2,1,0:T(8,128)S(1)}, bf16[3,256,1280]{2,1,0:T(8,128)(2,1)S(1)}, bf16[128,1280]{1,0:T(8,128)(2,1)S(1)}, bf16[128,1280]{1,0:T(8...) custom-call(f32[256,2560]{1,0:T(8,128)} %refs_0_.3, ...), custom_call_target="tpu_custom_call" | custom-call | flops 20000000000 | bytes 48234496 | tf_op jit(solution)/shard_map/pallas_call | solution.py:402
  36.8 0.0 copy-start.10
  36.9 7.5 %copy-done.10 = f32[256,16,1280]{2,1,0:T(8,128)} copy-done((f32[256,16,1280]{2,1,0:T(8,128)}, f32[256,16,1280]{2,1,0:T(8,128)S(1)}, u32[]{:S(2)}) %copy-start.10) | copy-done | bytes 20971544
  44.4 0.0 copy-start.3
  44.4 0.8 collective-permute-start
  45.2 0.0 copy-done
  45.2 0.0 copy-done.1
  45.2 0.0 copy-done.6
  45.2 0.0 copy-done.8
  45.2 0.0 copy-done.9
  45.2 0.0 copy-start.11
  45.2 7.0 %copy-done.11 = f32[256,16,1280]{2,1,0:T(8,128)S(1)} copy-done((f32[256,16,1280]{2,1,0:T(8,128)S(1)}, f32[256,16,1280]{2,1,0:T(8,128)}, u32[]{:S(2)}) %copy-start.11) | copy-done | bytes 20971544
  52.2 13.0 %shard_map.149 = (f32[2,256,16,1280]{3,2,1,0:T(8,128)}, bf16[2,3,256,1280]{3,2,1,0:T(8,128)(2,1)}, bf16[128,1280]{1,0:T(8,128)(2,1)S(1)}, bf16[128,1280]{1,0:T(8...) custom-call(f32[256,16,1280]{2,1,0:T(8,128)S(1)} %copy-done.11, ...), custom_call_target="tpu_custom_call" | custom-call | flops 20000000000 | bytes 44040192 | tf_op jit(solution)/shard_map/pallas_call | solution.py:489
  65.2 0.0 copy-done.3
  65.2 0.0 copy-start.4
  65.3 0.7 copy-done.4
  66.0 0.0 copy-start.5
  66.0 0.7 copy-done.5
  66.7 0.0 copy-start.7
  66.7 0.6 copy-done.7
  67.3 0.0 collective-permute-done.refs_2_
  67.3 0.0 copy-start.12
  67.3 0.7 copy-done.12
  68.1 29.6 %shard_map.150 = (f32[256,16,1280]{2,1,0:T(8,128)S(1)}, bf16[3,128,1280]{2,1,0:T(8,128)(2,1)S(1)}, bf16[128,1280]{1,0:T(8,128)(2,1)S(1)}, bf16[128,1280]{1,0:T(8...) custom-call(f32[256,2560]{1,0:T(8,128)} %refs_0_.3, ...), custom_call_target="tpu_custom_call" | custom-call | flops 20000000000 | bytes 48234496 | tf_op jit(solution)/shard_map/pallas_call | solution.py:402
  97.7 1.3 %collective-permute-start.2 = (bf16[128,1280]{1,0:T(8,128)(2,1)S(1)}, bf16[128,1280]{1,0:T(8,128)(2,1)S(1)}, u32[]{:S(2)}, u32[]{:S(2)}) collective-permute-start(bf16[128,1280]{1,0:T(8,128)(2,1)S(1)} %get-tuple-element.43.refs_4_), channel_id=1, source_target_pairs={{0,2},{2,0},{1,3},{3,1},{4,6},{6,4},{5,7},{7,5}} | collective-permute-start | bytes 983048 | tf_op jit(solution)/shard_map/ppermute | solution.py:567
  99.0 0.1 collective-permute-start.1
  99.1 8.7 %collective-permute-done.2.refs_6_ = bf16[128,1280]{1,0:T(8,128)(2,1)S(1)} collective-permute-done((bf16[128,1280]{1,0:T(8,128)(2,1)S(1)}, bf16[128,1280]{1,0:T(8,128)(2,1)S(1)}, u32[]{:S(2)}, u32[]{:S(2)}) %collective-permute-start.2) | collective-permute-done | bytes 327712 | tf_op jit(solution)/shard_map/ppermute | solution.py:567
  107.7 0.0 collective-permute-start.3
  107.7 0.0 copy-start.2
  107.7 7.8 %shard_map.151 = (f32[2,256,16,1280]{3,2,1,0:T(8,128)}, bf16[2,3,256,1280]{3,2,1,0:T(8,128)(2,1)}) custom-call(f32[256,16,1280]{2,1,0:T(8,128)S(1)} %get-tuple-element.44.st, bf16[3,128,1280]{2,1,0:T(8,128)(2,1)S(1)} %get-tuple-element.45.cw_a, bf16[3,128,1280]{2,1,0:T(8,128)(2,1)S(1)} %get-tuple-element.46.cw_b, ...), custom_call_target="tpu_custom_call", output_to_operand_aliasing={{0}: (3, {}), {1}: (4, {})} | custom-call | flops 20000000000 | bytes 44040192 | tf_op jit(solution)/shard_map/pallas_call | solution.py:521
  115.6 0.0 collective-permute-done.1.refs_5_
  115.6 0.0 collective-permute-done.3.refs_7_
  115.6 0.0 copy-done.2
  115.6 1.9 %fin.1 = f32[256,2560]{1,0:T(8,128)} custom-call(f32[128,2560]{1,0:T(8,128)S(1)} %get-tuple-element.33.r_a, f32[128,2560]{1,0:T(8,128)S(1)} %copy-done.2, bf16[128,1280]{1,0:T(8,128)(2,1)S(1)} %get-tuple-element.39.refs_0_, bf16[128,1280]{1,0:T(8,128)(2,1)S(1)} %get-tuple-element.40.refs_1_, bf16[128,1280]{1,0:T(8,128)(2,1)S(1)} %get-tuple-element.41.refs_2_, ...), custom_call_target="tpu_custom_call" | custom-call | tf_op jit(solution)/shard_map/fin/pallas_call | solution.py:546
Async XLA Ops:
  0.6 44.6 %copy-start = (f32[256,2560]{1,0:T(8,128)S(1)}, f32[256,2560]{1,0:T(8,128)}, u32[]{:S(2)}) copy-start(f32[256,2560]{1,0:T(8,128)} %refs_0_.3) | copy-start | bytes 7864324
  0.6 44.6 %copy-start.1 = (bf16[2,1280,192]{1,2,0:T(8,128)(2,1)S(1)}, bf16[2,1280,192]{1,2,0:T(8,128)(2,1)}, u32[]{:S(2)}) copy-start(bf16[2,1280,192]{1,2,0:T(8,128)(2,1)} %param.18) | copy-start | bytes 2949124
  0.7 44.5 %copy-start.6 = (bf16[2,4,1280]{2,1,0:T(4,128)(2,1)S(1)}, bf16[2,4,1280]{2,1,0:T(4,128)(2,1)}, u32[]{:S(2)}) copy-start(bf16[2,4,1280]{2,1,0:T(4,128)(2,1)} %refs_8_.3) | copy-start | bytes 61444
  0.7 44.5 %copy-start.8 = (bf16[2,2560]{1,0:T(2,128)(2,1)S(1)}, bf16[2,2560]{1,0:T(2,128)(2,1)}, u32[]{:S(2)}) copy-start(bf16[2,2560]{1,0:T(2,128)(2,1)} %refs_6_.1) | copy-start | bytes 30724
  0.7 44.5 %copy-start.9 = (bf16[2,1280]{1,0:T(2,128)(2,1)S(1)}, bf16[2,1280]{1,0:T(2,128)(2,1)}, u32[]{:S(2)}) copy-start(bf16[2,1280]{1,0:T(2,128)(2,1)} %refs_9_.3) | copy-start | bytes 15364
  36.8 7.5 %copy-start.10 = (f32[256,16,1280]{2,1,0:T(8,128)}, f32[256,16,1280]{2,1,0:T(8,128)S(1)}, u32[]{:S(2)}) copy-start(f32[256,16,1280]{2,1,0:T(8,128)S(1)} %get-tuple-element.27.st) | copy-start | bytes 62914564
  44.4 20.8 %copy-start.3 = (bf16[128,1280]{1,0:T(8,128)(2,1)}, bf16[128,1280]{1,0:T(8,128)(2,1)S(1)}, u32[]{:S(2)}) copy-start(bf16[128,1280]{1,0:T(8,128)(2,1)S(1)} %get-tuple-element.34.refs_1_) | copy-start | bytes 983044
  44.4 23.0 %collective-permute-start = (bf16[128,1280]{1,0:T(8,128)(2,1)S(1)}, bf16[128,1280]{1,0:T(8,128)(2,1)S(1)}, u32[]{:S(2)}, u32[]{:S(2)}) collective-permute-start(bf16[128,1280]{1,0:T(8,128)(2,1)S(1)} %get-tuple-element.34.refs_1_), channel_id=1, source_target_pairs={{0,2},{2,0},{1,3},{3,1},{4,6},{6,4},{5,7},{7,5}} | collective-permute-start | bytes 983048 | tf_op jit(solution)/shard_map/ppermute | solution.py:563
  45.2 7.0 %copy-start.11 = (f32[256,16,1280]{2,1,0:T(8,128)S(1)}, f32[256,16,1280]{2,1,0:T(8,128)}, u32[]{:S(2)}) copy-start(f32[256,16,1280]{2,1,0:T(8,128)} %copy-done.10) | copy-start | bytes 62914564
  65.2 0.8 copy-start.4
  66.0 0.7 copy-start.5
  66.7 0.6 copy-start.7
  67.3 0.7 copy-start.12
  97.7 10.0 %collective-permute-start.2 = (bf16[128,1280]{1,0:T(8,128)(2,1)S(1)}, bf16[128,1280]{1,0:T(8,128)(2,1)S(1)}, u32[]{:S(2)}, u32[]{:S(2)}) collective-permute-start(bf16[128,1280]{1,0:T(8,128)(2,1)S(1)} %get-tuple-element.43.refs_4_), channel_id=1, source_target_pairs={{0,2},{2,0},{1,3},{3,1},{4,6},{6,4},{5,7},{7,5}} | collective-permute-start | bytes 983048 | tf_op jit(solution)/shard_map/ppermute | solution.py:567
  99.0 16.6 %collective-permute-start.1 = (bf16[128,1280]{1,0:T(8,128)(2,1)S(1)}, bf16[128,1280]{1,0:T(8,128)(2,1)S(1)}, u32[]{:S(2)}, u32[]{:S(2)}) collective-permute-start(bf16[128,1280]{1,0:T(8,128)(2,1)S(1)} %get-tuple-element.43.refs_4_), channel_id=1, source_target_pairs={{0,1},{1,0},{2,3},{3,2},{4,5},{5,4},{6,7},{7,6}} | collective-permute-start | bytes 983048 | tf_op jit(solution)/shard_map/ppermute | solution.py:568
  107.7 7.9 %collective-permute-start.3 = (bf16[128,1280]{1,0:T(8,128)(2,1)S(1)}, bf16[128,1280]{1,0:T(8,128)(2,1)S(1)}, u32[]{:S(2)}, u32[]{:S(2)}) collective-permute-start(bf16[128,1280]{1,0:T(8,128)(2,1)S(1)} %collective-permute-done.2.refs_6_), channel_id=1, source_target_pairs={{0,1},{1,0},{2,3},{3,2},{4,5},{5,4},{6,7},{7,6}} | collective-permute-start | bytes 983048 | tf_op jit(solution)/shard_map/ppermute | solution.py:570
  107.7 7.9 %copy-start.2 = (f32[128,2560]{1,0:T(8,128)S(1)}, f32[128,2560]{1,0:T(8,128)}, u32[]{:S(2)}) copy-start(f32[128,2560]{1,0:T(8,128)} %get-tuple-element.38.r_b) | copy-start | bytes 3932164

commit v7 on v6

--- a/solution.py
+++ b/solution.py
@@ -386,7 +386,7 @@
     half = feat // 2
     nproj = w_x.shape[1]
     nchunk = chan // NCH
-    flat = [] if first else list(ready)
+    flat = [] if first else [pltpu.with_memory_space_constraint(a, pltpu.VMEM) for a in ready]
     held = rows if first else HALF
     args = [residual] + flat + [norm_w, w_in, conv_w, conv_b, w_x, conv_st, w_dt, b_dt, a_log, d_skip, w_out, state]
     specs = [ANY] + [VMEM] * len(flat) + [VMEM, ANY, VMEM, VMEM, VMEM, ANY, VMEM, VMEM, VMEM, VMEM, ANY, ANY]
@@ -484,8 +484,8 @@
     nchunk = chan // NCH
     vm = pltpu.VMEM
     dma = pltpu.SemaphoreType.DMA
-    args = [pltpu.with_memory_space_constraint(a, pltpu.VMEM) for a in (st, cw)]
-    args += [residual, *pieces, norm_w, w_in, conv_w, conv_b, w_x, conv_st]
+    st, cw, *pieces = [pltpu.with_memory_space_constraint(a, pltpu.VMEM) for a in (st, cw, *pieces)]
+    args = [st, cw, residual, *pieces, norm_w, w_in, conv_w, conv_b, w_x, conv_st]
     return pl.pallas_call(
         functools.partial(mid_kernel, layer),
         out_shape=[jax.ShapeDtypeStruct(shapes[0], F32), jax.ShapeDtypeStruct(shapes[1], BF16),
@@ -496,7 +496,7 @@
         scratch_shapes=[vm((nchunk, 2 * feat, NCH), BF16), vm((2 * HALF, 2 * feat), BF16), vm((HALF, feat), BF16),
                         vm((128, 512), BF16), vm((HALF, feat), F32), vm((HALF, chan), BF16),
                         dma((5,)), dma((nchunk,)), dma((st.shape[0] // SB,))],
-        compiler_params=pltpu.CompilerParams(vmem_limit_bytes=22 * 2 ** 20),
+        compiler_params=pltpu.CompilerParams(vmem_limit_bytes=34 * 2 ** 20),
         cost_estimate=pl.CostEstimate(flops=2 * 10 ** 10, bytes_accessed=42 * 2 ** 20, transcendentals=0),
     )(*args)
 

time: 118 us -> 103 us (0.87)
  local copies, waits for them, and re-layouts: 17.3 us -> 0.01 us
  Pallas kernels: 88.6 us -> 90.9 us
    unnamed x26 -> x4, local copies, waits for them, and re-layouts: 17.3 us -> 0.01 us
    pallas_call x1, Pallas kernels: 13 us -> 15.6 us  [mid_call(): pl.pallas_call(functools.partial(mid_kernel, layer), out_shape=[jax.Shape...]
  transfers between devices with their start and end apart: 4 -> 4, of which waited for: 1 -> 1; matrix products, arithmetic and copies ran while one was open for 0% -> 0% of each run, Pallas kernels for 18% -> 23%
where the time goes in v7:
time: 103 us; the launch traced here: 102 us
  Pallas kernels  90.9 us (88%)
  waiting for transfers between devices  8.68 us (8%)
  starting transfers between devices  2.18 us (2%)
    pallas_call x2, Pallas kernels, layer_call(): pl.pallas_call(functools.partial(layer_kernel, layer, first), out_shape=o...  65.2 us
    pallas_call x1, Pallas kernels, mid_call(): pl.pallas_call(functools.partial(mid_kernel, layer), out_shape=[jax.Shape...  15.6 us
    ppermute x2, waiting for transfers between devices, step(): vb = lax.ppermute(ub, 'tp', CROSS)  8.67 us
    pallas_call x1, Pallas kernels, w_call(): pl.pallas_call(functools.partial(w_kernel, layer), out_shape=[jax.ShapeDt...  8.16 us
    ppermute x2, starting transfers between devices, step(): vb = lax.ppermute(ub, 'tp', CROSS)  2.07 us
  transfers between devices with their start and end apart: 4, of which 1 were waited for; matrix products, arithmetic and copies ran while one was open for 0% of the time, Pallas kernels for 23%

profile of v7, /device:TPU:0, one launch (start us, length us, event | category | flops | bytes accessed | tf_op | source)
XLA Modules:
  0.0 102.5 jit_solution(1267055156208097307)
XLA Ops:
  0.6 36.0 %shard_map.148 = (f32[256,16,1280]{2,1,0:T(8,128)S(1)}, bf16[3,256,1280]{2,1,0:T(8,128)(2,1)S(1)}, bf16[128,1280]{1,0:T(8,128)(2,1)S(1)}, bf16[128,1280]{1,0:T(8...) custom-call(f32[256,2560]{1,0:T(8,128)} %refs_0_.3, ...), custom_call_target="tpu_custom_call" | custom-call | flops 20000000000 | bytes 48234496 | tf_op jit(solution)/shard_map/pallas_call | solution.py:402
  36.6 0.8 collective-permute-start
  37.5 15.6 %shard_map.149 = (f32[2,256,16,1280]{3,2,1,0:T(8,128)}, bf16[2,3,256,1280]{3,2,1,0:T(8,128)(2,1)}, bf16[128,1280]{1,0:T(8,128)(2,1)S(1)}, bf16[128,1280]{1,0:T(8...) custom-call(f32[256,16,1280]{2,1,0:T(8,128)S(1)} %get-tuple-element.27.st, ...), custom_call_target="tpu_custom_call" | custom-call | flops 20000000000 | bytes 44040192 | tf_op jit(solution)/shard_map/pallas_call | solution.py:489
  53.1 0.0 collective-permute-done.refs_2_
  53.1 29.2 %shard_map.150 = (f32[256,16,1280]{2,1,0:T(8,128)S(1)}, bf16[3,128,1280]{2,1,0:T(8,128)(2,1)S(1)}, bf16[128,1280]{1,0:T(8,128)(2,1)S(1)}, bf16[128,1280]{1,0:T(8...) custom-call(f32[256,2560]{1,0:T(8,128)} %refs_0_.3, ...), custom_call_target="tpu_custom_call" | custom-call | flops 20000000000 | bytes 48234496 | tf_op jit(solution)/shard_map/pallas_call | solution.py:402
  82.3 1.2 %collective-permute-start.2 = (bf16[128,1280]{1,0:T(8,128)(2,1)S(1)}, bf16[128,1280]{1,0:T(8,128)(2,1)S(1)}, u32[]{:S(2)}, u32[]{:S(2)}) collective-permute-start(bf16[128,1280]{1,0:T(8,128)(2,1)S(1)} %get-tuple-element.43.refs_4_), channel_id=1, source_target_pairs={{0,2},{2,0},{1,3},{3,1},{4,6},{6,4},{5,7},{7,5}} | collective-permute-start | bytes 983048 | tf_op jit(solution)/shard_map/ppermute | solution.py:567
  83.6 0.1 collective-permute-start.1
  83.7 8.7 %collective-permute-done.2.refs_6_ = bf16[128,1280]{1,0:T(8,128)(2,1)S(1)} collective-permute-done((bf16[128,1280]{1,0:T(8,128)(2,1)S(1)}, bf16[128,1280]{1,0:T(8,128)(2,1)S(1)}, u32[]{:S(2)}, u32[]{:S(2)}) %collective-permute-start.2) | collective-permute-done | bytes 327712 | tf_op jit(solution)/shard_map/ppermute | solution.py:567
  92.4 0.0 collective-permute-start.3
  92.4 0.0 copy-start
  92.4 0.0 copy-start.1
  92.4 8.2 %shard_map.151 = (f32[2,256,16,1280]{3,2,1,0:T(8,128)}, bf16[2,3,256,1280]{3,2,1,0:T(8,128)(2,1)}) custom-call(f32[256,16,1280]{2,1,0:T(8,128)S(1)} %get-tuple-element.44.st, bf16[3,128,1280]{2,1,0:T(8,128)(2,1)S(1)} %get-tuple-element.45.cw_a, bf16[3,128,1280]{2,1,0:T(8,128)(2,1)S(1)} %get-tuple-element.46.cw_b, ...), custom_call_target="tpu_custom_call", output_to_operand_aliasing={{0}: (3, {}), {1}: (4, {})} | custom-call | flops 20000000000 | bytes 44040192 | tf_op jit(solution)/shard_map/pallas_call | solution.py:521
  100.5 0.0 collective-permute-done.1.refs_5_
  100.6 0.0 collective-permute-done.3.refs_7_
  100.6 0.0 copy-done
  100.6 0.0 copy-done.1
  100.6 1.9 %fin.1 = f32[256,2560]{1,0:T(8,128)} custom-call(f32[128,2560]{1,0:T(8,128)S(1)} %copy-done, f32[128,2560]{1,0:T(8,128)S(1)} %copy-done.1, bf16[128,1280]{1,0:T(8,128)(2,1)S(1)} %get-tuple-element.39.refs_0_, bf16[128,1280]{1,0:T(8,128)(2,1)S(1)} %get-tuple-element.40.refs_1_, bf16[128,1280]{1,0:T(8,128)(2,1)S(1)} %get-tuple-element.41.refs_2_, ...), custom_call_target="tpu_custom_call" | custom-call | tf_op jit(solution)/shard_map/fin/pallas_call | solution.py:546
Async XLA Ops:
  36.6 16.4 %collective-permute-start = (bf16[128,1280]{1,0:T(8,128)(2,1)S(1)}, bf16[128,1280]{1,0:T(8,128)(2,1)S(1)}, u32[]{:S(2)}, u32[]{:S(2)}) collective-permute-start(bf16[128,1280]{1,0:T(8,128)(2,1)S(1)} %get-tuple-element.34.refs_1_), channel_id=1, source_target_pairs={{0,2},{2,0},{1,3},{3,1},{4,6},{6,4},{5,7},{7,5}} | collective-permute-start | bytes 983048 | tf_op jit(solution)/shard_map/ppermute | solution.py:563
  82.3 10.0 %collective-permute-start.2 = (bf16[128,1280]{1,0:T(8,128)(2,1)S(1)}, bf16[128,1280]{1,0:T(8,128)(2,1)S(1)}, u32[]{:S(2)}, u32[]{:S(2)}) collective-permute-start(bf16[128,1280]{1,0:T(8,128)(2,1)S(1)} %get-tuple-element.43.refs_4_), channel_id=1, source_target_pairs={{0,2},{2,0},{1,3},{3,1},{4,6},{6,4},{5,7},{7,5}} | collective-permute-start | bytes 983048 | tf_op jit(solution)/shard_map/ppermute | solution.py:567
  83.6 16.9 %collective-permute-start.1 = (bf16[128,1280]{1,0:T(8,128)(2,1)S(1)}, bf16[128,1280]{1,0:T(8,128)(2,1)S(1)}, u32[]{:S(2)}, u32[]{:S(2)}) collective-permute-start(bf16[128,1280]{1,0:T(8,128)(2,1)S(1)} %get-tuple-element.43.refs_4_), channel_id=1, source_target_pairs={{0,1},{1,0},{2,3},{3,2},{4,5},{5,4},{6,7},{7,6}} | collective-permute-start | bytes 983048 | tf_op jit(solution)/shard_map/ppermute | solution.py:568
  92.4 8.2 %collective-permute-start.3 = (bf16[128,1280]{1,0:T(8,128)(2,1)S(1)}, bf16[128,1280]{1,0:T(8,128)(2,1)S(1)}, u32[]{:S(2)}, u32[]{:S(2)}) collective-permute-start(bf16[128,1280]{1,0:T(8,128)(2,1)S(1)} %collective-permute-done.2.refs_6_), channel_id=1, source_target_pairs={{0,1},{1,0},{2,3},{3,2},{4,5},{5,4},{6,7},{7,6}} | collective-permute-start | bytes 983048 | tf_op jit(solution)/shard_map/ppermute | solution.py:570
  92.4 8.2 %copy-start = (f32[128,2560]{1,0:T(8,128)S(1)}, f32[128,2560]{1,0:T(8,128)}, u32[]{:S(2)}) copy-start(f32[128,2560]{1,0:T(8,128)} %get-tuple-element.33.r_a) | copy-start | bytes 3932164
  92.4 8.2 %copy-start.1 = (f32[128,2560]{1,0:T(8,128)S(1)}, f32[128,2560]{1,0:T(8,128)}, u32[]{:S(2)}) copy-start(f32[128,2560]{1,0:T(8,128)} %get-tuple-element.38.r_b) | copy-start | bytes 3932164

commit v8 on v7

--- a/solution.py
+++ b/solution.py
@@ -298,6 +298,8 @@
         dt_s[...] = jnp.maximum(pre, 0.0) + jnp.log1p(jnp.exp(-jnp.abs(pre)))
         bc = jnp.concatenate([rms0(p[rank:rank + nst]), rms0(p[rank + nst:])], axis=0)
         bc_s[:, 0:2 * nst] = jnp.transpose(bc)
+        if k == 1:
+            reduce_a(1)
 
         def block(i, carry, k=k):
             st_copy(i + k * nblk).wait()
@@ -337,13 +339,9 @@
                     red_a(q).start()
                     project(yg, core, mine_a.at[q], F32)
 
-                @pl.when(i == nblk // 2 + 1)
+                @pl.when(i == nblk // 2)
                 def _():
                     reduce_a(0)
-            else:
-                @pl.when(i == 1)
-                def _():
-                    reduce_a(1)
 
             return carry
 
@@ -448,6 +446,7 @@
     ex_s[...] = expand_matrix()
     core = lax.rem(lax.axis_index('tp'), 2)
     r_copy.wait()
+    w_copy(3).start()
     st_copy(nst - 1).start()
     c_copy.start()
     add_pieces(rbuf, 0, halves_of(core, feat // 2), ua, upa, va, vpa)
@@ -460,9 +459,9 @@
     def chunk(c, carry):
         w_copy(c).wait()
 
-        @pl.when(c + 3 < nchunk)
+        @pl.when(c + 4 < nchunk)
         def _():
-            w_copy(c + 3).start()
+            w_copy(c + 4).start()
 
         for t in range(3):
             st_copy(3 * c + t).start()

time: 103 us -> 102 us (level)
  starting transfers between devices: 2.18 us -> 1.13 us
    ppermute x2, starting transfers between devices: 2.07 us -> 1.02 us  [step(): vb = lax.ppermute(ub, 'tp', CROSS)]
where the time goes in v8:
time: 102 us
  Pallas kernels  90.8 us (89%)
  waiting for transfers between devices  9.28 us (9%)
  starting transfers between devices  1.13 us (1%)
    pallas_call x2, Pallas kernels, layer_call(): pl.pallas_call(functools.partial(layer_kernel, layer, first), out_shape=o...  65 us
    pallas_call x1, Pallas kernels, mid_call(): pl.pallas_call(functools.partial(mid_kernel, layer), out_shape=[jax.Shape...  15.8 us
    ppermute x2, waiting for transfers between devices, step(): vb = lax.ppermute(ub, 'tp', CROSS)  9.28 us
    pallas_call x1, Pallas kernels, w_call(): pl.pallas_call(functools.partial(w_kernel, layer), out_shape=[jax.ShapeDt...  8.16 us
  transfers between devices with their start and end apart: 4, of which 1 were waited for; matrix products, arithmetic and copies ran while one was open for 0% of the time, Pallas kernels for 23%

profile of v8, /device:TPU:0, one launch (start us, length us, event | category | flops | bytes accessed | tf_op | source)
XLA Modules:
  0.0 101.9 jit_solution(4083286308885444239)
XLA Ops:
  0.6 36.0 %shard_map.148 = (f32[256,16,1280]{2,1,0:T(8,128)S(1)}, bf16[3,256,1280]{2,1,0:T(8,128)(2,1)S(1)}, bf16[128,1280]{1,0:T(8,128)(2,1)S(1)}, bf16[128,1280]{1,0:T(8...) custom-call(f32[256,2560]{1,0:T(8,128)} %refs_0_.3, ...), custom_call_target="tpu_custom_call" | custom-call | flops 20000000000 | bytes 48234496 | tf_op jit(solution)/shard_map/pallas_call | solution.py:400
  36.6 0.4 collective-permute-start
  37.0 15.8 %shard_map.149 = (f32[2,256,16,1280]{3,2,1,0:T(8,128)}, bf16[2,3,256,1280]{3,2,1,0:T(8,128)(2,1)}, bf16[128,1280]{1,0:T(8,128)(2,1)S(1)}, bf16[128,1280]{1,0:T(8...) custom-call(f32[256,16,1280]{2,1,0:T(8,128)S(1)} %get-tuple-element.27.st, ...), custom_call_target="tpu_custom_call" | custom-call | flops 20000000000 | bytes 44040192 | tf_op jit(solution)/shard_map/pallas_call | solution.py:488
  52.8 0.0 collective-permute-done.refs_2_
  52.8 29.0 %shard_map.150 = (f32[256,16,1280]{2,1,0:T(8,128)S(1)}, bf16[3,128,1280]{2,1,0:T(8,128)(2,1)S(1)}, bf16[128,1280]{1,0:T(8,128)(2,1)S(1)}, bf16[128,1280]{1,0:T(8...) custom-call(f32[256,2560]{1,0:T(8,128)} %refs_0_.3, ...), custom_call_target="tpu_custom_call" | custom-call | flops 20000000000 | bytes 48234496 | tf_op jit(solution)/shard_map/pallas_call | solution.py:400
  81.8 0.6 collective-permute-start.2
  82.4 0.1 collective-permute-start.1
  82.5 9.3 %collective-permute-done.2.refs_6_ = bf16[128,1280]{1,0:T(8,128)(2,1)S(1)} collective-permute-done((bf16[128,1280]{1,0:T(8,128)(2,1)S(1)}, bf16[128,1280]{1,0:T(8,128)(2,1)S(1)}, u32[]{:S(2)}, u32[]{:S(2)}) %collective-permute-start.2) | collective-permute-done | bytes 327712 | tf_op jit(solution)/shard_map/ppermute | solution.py:566
  91.8 0.0 collective-permute-start.3
  91.8 0.0 copy-start
  91.8 0.0 copy-start.1
  91.8 8.2 %shard_map.151 = (f32[2,256,16,1280]{3,2,1,0:T(8,128)}, bf16[2,3,256,1280]{3,2,1,0:T(8,128)(2,1)}) custom-call(f32[256,16,1280]{2,1,0:T(8,128)S(1)} %get-tuple-element.44.st, bf16[3,128,1280]{2,1,0:T(8,128)(2,1)S(1)} %get-tuple-element.45.cw_a, bf16[3,128,1280]{2,1,0:T(8,128)(2,1)S(1)} %get-tuple-element.46.cw_b, ...), custom_call_target="tpu_custom_call", output_to_operand_aliasing={{0}: (3, {}), {1}: (4, {})} | custom-call | flops 20000000000 | bytes 44040192 | tf_op jit(solution)/shard_map/pallas_call | solution.py:520
  100.0 0.0 collective-permute-done.1.refs_5_
  100.0 0.0 collective-permute-done.3.refs_7_
  100.0 0.0 copy-done
  100.0 0.0 copy-done.1
  100.0 1.9 %fin.1 = f32[256,2560]{1,0:T(8,128)} custom-call(f32[128,2560]{1,0:T(8,128)S(1)} %copy-done, f32[128,2560]{1,0:T(8,128)S(1)} %copy-done.1, bf16[128,1280]{1,0:T(8,128)(2,1)S(1)} %get-tuple-element.39.refs_0_, bf16[128,1280]{1,0:T(8,128)(2,1)S(1)} %get-tuple-element.40.refs_1_, bf16[128,1280]{1,0:T(8,128)(2,1)S(1)} %get-tuple-element.41.refs_2_, ...), custom_call_target="tpu_custom_call" | custom-call | tf_op jit(solution)/shard_map/fin/pallas_call | solution.py:545
Async XLA Ops:
  36.6 16.2 %collective-permute-start = (bf16[128,1280]{1,0:T(8,128)(2,1)S(1)}, bf16[128,1280]{1,0:T(8,128)(2,1)S(1)}, u32[]{:S(2)}, u32[]{:S(2)}) collective-permute-start(bf16[128,1280]{1,0:T(8,128)(2,1)S(1)} %get-tuple-element.34.refs_1_), channel_id=1, source_target_pairs={{0,2},{2,0},{1,3},{3,1},{4,6},{6,4},{5,7},{7,5}} | collective-permute-start | bytes 983048 | tf_op jit(solution)/shard_map/ppermute | solution.py:562
  81.8 10.0 %collective-permute-start.2 = (bf16[128,1280]{1,0:T(8,128)(2,1)S(1)}, bf16[128,1280]{1,0:T(8,128)(2,1)S(1)}, u32[]{:S(2)}, u32[]{:S(2)}) collective-permute-start(bf16[128,1280]{1,0:T(8,128)(2,1)S(1)} %get-tuple-element.43.refs_4_), channel_id=1, source_target_pairs={{0,2},{2,0},{1,3},{3,1},{4,6},{6,4},{5,7},{7,5}} | collective-permute-start | bytes 983048 | tf_op jit(solution)/shard_map/ppermute | solution.py:566
  82.4 17.6 %collective-permute-start.1 = (bf16[128,1280]{1,0:T(8,128)(2,1)S(1)}, bf16[128,1280]{1,0:T(8,128)(2,1)S(1)}, u32[]{:S(2)}, u32[]{:S(2)}) collective-permute-start(bf16[128,1280]{1,0:T(8,128)(2,1)S(1)} %get-tuple-element.43.refs_4_), channel_id=1, source_target_pairs={{0,1},{1,0},{2,3},{3,2},{4,5},{5,4},{6,7},{7,6}} | collective-permute-start | bytes 983048 | tf_op jit(solution)/shard_map/ppermute | solution.py:567
  91.8 8.2 %collective-permute-start.3 = (bf16[128,1280]{1,0:T(8,128)(2,1)S(1)}, bf16[128,1280]{1,0:T(8,128)(2,1)S(1)}, u32[]{:S(2)}, u32[]{:S(2)}) collective-permute-start(bf16[128,1280]{1,0:T(8,128)(2,1)S(1)} %collective-permute-done.2.refs_6_), channel_id=1, source_target_pairs={{0,1},{1,0},{2,3},{3,2},{4,5},{5,4},{6,7},{7,6}} | collective-permute-start | bytes 983048 | tf_op jit(solution)/shard_map/ppermute | solution.py:569
  91.8 8.2 %copy-start = (f32[128,2560]{1,0:T(8,128)S(1)}, f32[128,2560]{1,0:T(8,128)}, u32[]{:S(2)}) copy-start(f32[128,2560]{1,0:T(8,128)} %get-tuple-element.33.r_a) | copy-start | bytes 3932164
  91.8 8.2 %copy-start.1 = (f32[128,2560]{1,0:T(8,128)S(1)}, f32[128,2560]{1,0:T(8,128)}, u32[]{:S(2)}) copy-start(f32[128,2560]{1,0:T(8,128)} %get-tuple-element.38.r_b) | copy-start | bytes 3932164

commit v9 on v8

--- a/solution.py
+++ b/solution.py
@@ -16,6 +16,7 @@
 NCH = 256
 SB = 16
 HALF = 128
+SPLIT = 512
 LOG2E = math.log2(math.e)
 MESH = pl.DeviceIdType.MESH
 
@@ -24,11 +25,35 @@
     return v * jax.nn.sigmoid(v)
 
 
-def expand_matrix():
-    row = lax.broadcasted_iota(jnp.int32, (128, 512), 0)
-    col = lax.broadcasted_iota(jnp.int32, (128, 512), 1)
-    target = 2 * row + jnp.where(col < 256, 0, 257)
-    return jnp.where(col == target, 1.0, 0.0).astype(BF16)
+def order_matrix():
+    row = lax.broadcasted_iota(jnp.int32, (128, 128), 0)
+    col = lax.broadcasted_iota(jnp.int32, (128, 128), 1)
+    low = col & 7
+    source = col - low + (low >> 1) + 4 * (low & 1)
+    return jnp.where(row == source, 1.0, 0.0).astype(BF16)
+
+
+def split_rows(wbuf, c):
+    even = (lax.broadcasted_iota(jnp.int32, (SPLIT // 16, 8, NCH), 1) & 1) == 0
+
+    def block(b, carry):
+        start = b * SPLIT
+        v = wbuf[c, pl.ds(start, SPLIT), :].astype(F32).reshape(SPLIT // 16, 2, 8, NCH)
+        first, second = v[:, 0], v[:, 1]
+        x = jnp.where(even, first, pltpu.roll(second, 1, 1))
+        z = jnp.where(even, pltpu.roll(first, 7, 1), second)
+        wbuf[c, pl.ds(start, SPLIT // 2), :] = x.reshape(SPLIT // 2, NCH).astype(BF16)
+        wbuf[c, pl.ds(start + SPLIT // 2, SPLIT // 2), :] = z.reshape(SPLIT // 2, NCH).astype(BF16)
+        return carry
+
+    for b in range(wbuf.shape[1] // SPLIT):
+        block(b, 0)
+
+
+def split_half(wbuf, c, side):
+    half = SPLIT // 2
+    return jnp.concatenate([wbuf[c, b * SPLIT + side * half:b * SPLIT + (side + 1) * half, :]
+                            for b in range(wbuf.shape[1] // SPLIT)], axis=0)
 
 
 def rms0(v):
@@ -76,11 +101,8 @@
 
     def expand(j, carry):
         for t in range(4):
-            src = pl.ds(pl.multiple_of(j * 512 + t * 128, 128), 128)
-            e = jnp.dot(hbuf[:, src], ex_s[...], preferred_element_type=F32).astype(BF16)
-            cols = pl.ds(pl.multiple_of(j * 1024 + t * 256, 256), 256)
-            hx[0:HALF, cols] = e[:, :256]
-            hx[HALF:2 * HALF, cols] = e[:, 256:]
+            cols = pl.ds(pl.multiple_of(j * 512 + t * 128, 128), 128)
+            hx[:, cols] = jnp.dot(hbuf[:, cols], ex_s[...], preferred_element_type=F32).astype(BF16)
         return carry
 
     lax.fori_loop(0, feat // 512, expand, 0)
@@ -93,9 +115,8 @@
 def in_chunk(layer, c, hx, wbuf, conv_w, conv_b, window, z_out, xc_out):
     old0, old1, old2, x_out = window
     sl = cols_of(c)
-    acc = jnp.dot(hx[...], wbuf[c], preferred_element_type=F32)
-    x = acc[:HALF].astype(BF16)
-    z_out[:, sl] = acc[HALF:].astype(BF16)
+    x = jnp.dot(hx[...], split_half(wbuf, c, 0), preferred_element_type=F32).astype(BF16)
+    z_out[:, sl] = jnp.dot(hx[...], split_half(wbuf, c, 1), preferred_element_type=F32).astype(BF16)
     x_out[:, sl] = x
     taps = conv_w[layer, :, sl].astype(F32)
     pre = old0[:, sl].astype(F32) * taps[0:1] + old1[:, sl].astype(F32) * taps[1:2]
@@ -183,7 +204,7 @@
     old_copy.start()
     win_copy.start()
     w_copy(2).start()
-    ex_s[...] = expand_matrix()
+    ex_s[...] = order_matrix()
     a_s[...] = -jnp.exp(a_log[layer]) * LOG2E
     pl.semaphore_wait(barrier, 2)
     relays = []
@@ -228,6 +249,8 @@
                 @pl.when(c + 3 < nchunk)
                 def _():
                     w_copy(c + 3).start()
+
+                split_rows(wbuf, c)
 
             if k == 1:
                 for t in range(3):
@@ -401,7 +424,7 @@
         functools.partial(layer_kernel, layer, first),
         out_shape=outs, in_specs=specs, out_specs=out_specs,
         scratch_shapes=[
-            vm((nchunk, 2 * feat, NCH), BF16), vm((2 * HALF, 2 * feat), BF16), vm((HALF, feat), BF16), vm((128, 512), BF16),
+            vm((nchunk, 2 * feat, NCH), BF16), vm((HALF, feat), BF16), vm((HALF, feat), BF16), vm((128, 128), BF16),
             vm((2, nproj, HALF), BF16), vm((2, nproj, HALF), BF16), vm((2, nproj, HALF), BF16),
             vm((2, nproj, HALF), BF16), vm((held, feat), F32), vm((held, chan), BF16), vm((rows, chan), BF16),
             vm((rows, chan), BF16), vm((HALF, chan), F32), vm((HALF, 128), F32), vm((nst, chan), F32), vm((HALF, chan), F32),
@@ -443,7 +466,7 @@
     win_copy.start()
     w_copy(1).start()
     w_copy(2).start()
-    ex_s[...] = expand_matrix()
+    ex_s[...] = order_matrix()
     core = lax.rem(lax.axis_index('tp'), 2)
     r_copy.wait()
     w_copy(3).start()
@@ -463,6 +486,7 @@
         def _():
             w_copy(c + 4).start()
 
+        split_rows(wbuf, c)
         for t in range(3):
             st_copy(3 * c + t).start()
         in_chunk(nxt, c, hx, wbuf, conv_w, conv_b, window, z_a, xc_a)
@@ -492,8 +516,8 @@
                    vm((3, HALF, chan), BF16), jax.ShapeDtypeStruct((HALF, feat), F32)],
         in_specs=[VMEM, VMEM, ANY] + [VMEM] * 4 + [VMEM, ANY, VMEM, VMEM, VMEM, ANY],
         out_specs=[ANY, ANY, VMEM, VMEM, VMEM, VMEM, ANY],
-        scratch_shapes=[vm((nchunk, 2 * feat, NCH), BF16), vm((2 * HALF, 2 * feat), BF16), vm((HALF, feat), BF16),
-                        vm((128, 512), BF16), vm((HALF, feat), F32), vm((HALF, chan), BF16),
+        scratch_shapes=[vm((nchunk, 2 * feat, NCH), BF16), vm((HALF, feat), BF16), vm((HALF, feat), BF16),
+                        vm((128, 128), BF16), vm((HALF, feat), F32), vm((HALF, chan), BF16),
                         dma((5,)), dma((nchunk,)), dma((st.shape[0] // SB,))],
         compiler_params=pltpu.CompilerParams(vmem_limit_bytes=34 * 2 ** 20),
         cost_estimate=pl.CostEstimate(flops=2 * 10 ** 10, bytes_accessed=42 * 2 ** 20, transcendentals=0),

time: 102 us -> 101 us (level)
  no operation moved by 1% of the time
where the time goes in v9:
time: 101 us
  Pallas kernels  90.1 us (89%)
  waiting for transfers between devices  9.06 us (9%)
  starting transfers between devices  1.36 us (1%)
    pallas_call x2, Pallas kernels, layer_call(): pl.pallas_call(functools.partial(layer_kernel, layer, first), out_shape=o...  64.5 us
    pallas_call x1, Pallas kernels, mid_call(): pl.pallas_call(functools.partial(mid_kernel, layer), out_shape=[jax.Shape...  15.5 us
    ppermute x2, waiting for transfers between devices, step(): vb = lax.ppermute(ub, 'tp', CROSS)  9.06 us
    pallas_call x1, Pallas kernels, w_call(): pl.pallas_call(functools.partial(w_kernel, layer), out_shape=[jax.ShapeDt...  8.16 us
  transfers between devices with their start and end apart: 4, of which 1 were waited for; matrix products, arithmetic and copies ran while one was open for 0% of the time, Pallas kernels for 23%

profile of v9, /device:TPU:0, one launch (start us, length us, event | category | flops | bytes accessed | tf_op | source)
XLA Modules:
  0.0 101.2 jit_solution(9822349459423471135)
XLA Ops:
  0.6 35.6 %shard_map.148 = (f32[256,16,1280]{2,1,0:T(8,128)S(1)}, bf16[3,256,1280]{2,1,0:T(8,128)(2,1)S(1)}, bf16[128,1280]{1,0:T(8,128)(2,1)S(1)}, bf16[128,1280]{1,0:T(8...) custom-call(f32[256,2560]{1,0:T(8,128)} %refs_0_.3, ...), custom_call_target="tpu_custom_call" | custom-call | flops 20000000000 | bytes 48234496 | tf_op jit(solution)/shard_map/pallas_call | solution.py:423
  36.3 0.4 collective-permute-start
  36.7 15.5 %shard_map.149 = (f32[2,256,16,1280]{3,2,1,0:T(8,128)}, bf16[2,3,256,1280]{3,2,1,0:T(8,128)(2,1)}, bf16[128,1280]{1,0:T(8,128)(2,1)S(1)}, bf16[128,1280]{1,0:T(8...) custom-call(f32[256,16,1280]{2,1,0:T(8,128)S(1)} %get-tuple-element.27.st, ...), custom_call_target="tpu_custom_call" | custom-call | flops 20000000000 | bytes 44040192 | tf_op jit(solution)/shard_map/pallas_call | solution.py:512
  52.2 0.0 collective-permute-done.refs_2_
  52.2 28.9 %shard_map.150 = (f32[256,16,1280]{2,1,0:T(8,128)S(1)}, bf16[3,128,1280]{2,1,0:T(8,128)(2,1)S(1)}, bf16[128,1280]{1,0:T(8,128)(2,1)S(1)}, bf16[128,1280]{1,0:T(8...) custom-call(f32[256,2560]{1,0:T(8,128)} %refs_0_.3, ...), custom_call_target="tpu_custom_call" | custom-call | flops 20000000000 | bytes 48234496 | tf_op jit(solution)/shard_map/pallas_call | solution.py:423
  81.1 1.0 collective-permute-start.2
  82.0 0.0 collective-permute-start.1
  82.0 9.1 %collective-permute-done.2.refs_6_ = bf16[128,1280]{1,0:T(8,128)(2,1)S(1)} collective-permute-done((bf16[128,1280]{1,0:T(8,128)(2,1)S(1)}, bf16[128,1280]{1,0:T(8,128)(2,1)S(1)}, u32[]{:S(2)}, u32[]{:S(2)}) %collective-permute-start.2) | collective-permute-done | bytes 327712 | tf_op jit(solution)/shard_map/ppermute | solution.py:590
  91.1 0.0 collective-permute-start.3
  91.1 0.0 copy-start
  91.1 0.0 copy-start.1
  91.1 8.2 %shard_map.151 = (f32[2,256,16,1280]{3,2,1,0:T(8,128)}, bf16[2,3,256,1280]{3,2,1,0:T(8,128)(2,1)}) custom-call(f32[256,16,1280]{2,1,0:T(8,128)S(1)} %get-tuple-element.44.st, bf16[3,128,1280]{2,1,0:T(8,128)(2,1)S(1)} %get-tuple-element.45.cw_a, bf16[3,128,1280]{2,1,0:T(8,128)(2,1)S(1)} %get-tuple-element.46.cw_b, ...), custom_call_target="tpu_custom_call", output_to_operand_aliasing={{0}: (3, {}), {1}: (4, {})} | custom-call | flops 20000000000 | bytes 44040192 | tf_op jit(solution)/shard_map/pallas_call | solution.py:544
  99.3 0.0 collective-permute-done.1.refs_5_
  99.3 0.0 collective-permute-done.3.refs_7_
  99.3 0.0 copy-done
  99.3 0.0 copy-done.1
  99.3 1.9 %fin.1 = f32[256,2560]{1,0:T(8,128)} custom-call(f32[128,2560]{1,0:T(8,128)S(1)} %copy-done, f32[128,2560]{1,0:T(8,128)S(1)} %copy-done.1, bf16[128,1280]{1,0:T(8,128)(2,1)S(1)} %get-tuple-element.39.refs_0_, bf16[128,1280]{1,0:T(8,128)(2,1)S(1)} %get-tuple-element.40.refs_1_, bf16[128,1280]{1,0:T(8,128)(2,1)S(1)} %get-tuple-element.41.refs_2_, ...), custom_call_target="tpu_custom_call" | custom-call | tf_op jit(solution)/shard_map/fin/pallas_call | solution.py:569
Async XLA Ops:
  36.3 15.9 %collective-permute-start = (bf16[128,1280]{1,0:T(8,128)(2,1)S(1)}, bf16[128,1280]{1,0:T(8,128)(2,1)S(1)}, u32[]{:S(2)}, u32[]{:S(2)}) collective-permute-start(bf16[128,1280]{1,0:T(8,128)(2,1)S(1)} %get-tuple-element.34.refs_1_), channel_id=1, source_target_pairs={{0,2},{2,0},{1,3},{3,1},{4,6},{6,4},{5,7},{7,5}} | collective-permute-start | bytes 983048 | tf_op jit(solution)/shard_map/ppermute | solution.py:586
  81.1 10.0 %collective-permute-start.2 = (bf16[128,1280]{1,0:T(8,128)(2,1)S(1)}, bf16[128,1280]{1,0:T(8,128)(2,1)S(1)}, u32[]{:S(2)}, u32[]{:S(2)}) collective-permute-start(bf16[128,1280]{1,0:T(8,128)(2,1)S(1)} %get-tuple-element.43.refs_4_), channel_id=1, source_target_pairs={{0,2},{2,0},{1,3},{3,1},{4,6},{6,4},{5,7},{7,5}} | collective-permute-start | bytes 983048 | tf_op jit(solution)/shard_map/ppermute | solution.py:590
  82.0 17.2 %collective-permute-start.1 = (bf16[128,1280]{1,0:T(8,128)(2,1)S(1)}, bf16[128,1280]{1,0:T(8,128)(2,1)S(1)}, u32[]{:S(2)}, u32[]{:S(2)}) collective-permute-start(bf16[128,1280]{1,0:T(8,128)(2,1)S(1)} %get-tuple-element.43.refs_4_), channel_id=1, source_target_pairs={{0,1},{1,0},{2,3},{3,2},{4,5},{5,4},{6,7},{7,6}} | collective-permute-start | bytes 983048 | tf_op jit(solution)/shard_map/ppermute | solution.py:591
  91.1 8.2 %collective-permute-start.3 = (bf16[128,1280]{1,0:T(8,128)(2,1)S(1)}, bf16[128,1280]{1,0:T(8,128)(2,1)S(1)}, u32[]{:S(2)}, u32[]{:S(2)}) collective-permute-start(bf16[128,1280]{1,0:T(8,128)(2,1)S(1)} %collective-permute-done.2.refs_6_), channel_id=1, source_target_pairs={{0,1},{1,0},{2,3},{3,2},{4,5},{5,4},{6,7},{7,6}} | collective-permute-start | bytes 983048 | tf_op jit(solution)/shard_map/ppermute | solution.py:593
  91.1 8.2 %copy-start = (f32[128,2560]{1,0:T(8,128)S(1)}, f32[128,2560]{1,0:T(8,128)}, u32[]{:S(2)}) copy-start(f32[128,2560]{1,0:T(8,128)} %get-tuple-element.33.r_a) | copy-start | bytes 3932164
  91.1 8.2 %copy-start.1 = (f32[128,2560]{1,0:T(8,128)S(1)}, f32[128,2560]{1,0:T(8,128)}, u32[]{:S(2)}) copy-start(f32[128,2560]{1,0:T(8,128)} %get-tuple-element.38.r_b) | copy-start | bytes 3932164

commit v10 on v9

--- a/solution.py
+++ b/solution.py
@@ -83,7 +83,7 @@
         rbuf[dst, hi] = rbuf[dst, hi] + (up[src, :].astype(F32) + vp[src, :].astype(F32))
         return carry
 
-    lax.fori_loop(0, HALF // 32, add, 0)
+    lax.fori_loop(0, HALF // 32, add, 0, unroll=True)
 
 
 def norm_expand(rbuf, start, norm_row, hbuf, ex_s, hx):
@@ -97,7 +97,7 @@
         hbuf[pl.ds(off, 32), :] = (r * inv * nw).astype(BF16)
         return carry
 
-    lax.fori_loop(0, HALF // 32, norm, 0)
+    lax.fori_loop(0, HALF // 32, norm, 0, unroll=True)
 
     def expand(j, carry):
         for t in range(4):
@@ -105,7 +105,7 @@
             hx[:, cols] = jnp.dot(hbuf[:, cols], ex_s[...], preferred_element_type=F32).astype(BF16)
         return carry
 
-    lax.fori_loop(0, feat // 512, expand, 0)
+    lax.fori_loop(0, feat // 512, expand, 0, unroll=True)
 
 
 def cols_of(c):

time: 101 us -> 99.9 us (0.989)
  Pallas kernels: 90.1 us -> 88.6 us
    pallas_call x2, Pallas kernels: 64.5 us -> 63.1 us  [layer_call(): pl.pallas_call(functools.partial(layer_kernel, layer, first), out_shape=o...]
  transfers between devices with their start and end apart: 4 -> 4, of which waited for: 1 -> 1; matrix products, arithmetic and copies ran while one was open for 0% -> 0% of each run, Pallas kernels for 23% -> 24%
where the time goes in v10:
time: 99.9 us; the launch traced here: 99.7 us
  Pallas kernels  88.6 us (89%)
  waiting for transfers between devices  9.1 us (9%)
  starting transfers between devices  1.32 us (1%)
    pallas_call x2, Pallas kernels, layer_call(): pl.pallas_call(functools.partial(layer_kernel, layer, first), out_shape=o...  63.1 us
    pallas_call x1, Pallas kernels, mid_call(): pl.pallas_call(functools.partial(mid_kernel, layer), out_shape=[jax.Shape...  15.5 us
    ppermute x2, waiting for transfers between devices, step(): vb = lax.ppermute(ub, 'tp', CROSS)  9.09 us
    pallas_call x1, Pallas kernels, w_call(): pl.pallas_call(functools.partial(w_kernel, layer), out_shape=[jax.ShapeDt...  8.16 us
  transfers between devices with their start and end apart: 4, of which 1 were waited for; matrix products, arithmetic and copies ran while one was open for 0% of the time, Pallas kernels for 24%

profile of v10, /device:TPU:0, one launch (start us, length us, event | category | flops | bytes accessed | tf_op | source)
XLA Modules:
  0.0 99.7 jit_solution(15449767692951762729)
XLA Ops:
  0.6 34.9 %shard_map.148 = (f32[256,16,1280]{2,1,0:T(8,128)S(1)}, bf16[3,256,1280]{2,1,0:T(8,128)(2,1)S(1)}, bf16[128,1280]{1,0:T(8,128)(2,1)S(1)}, bf16[128,1280]{1,0:T(8...) custom-call(f32[256,2560]{1,0:T(8,128)} %refs_0_.3, ...), custom_call_target="tpu_custom_call" | custom-call | flops 20000000000 | bytes 48234496 | tf_op jit(solution)/shard_map/pallas_call | solution.py:423
  35.5 0.4 collective-permute-start
  35.9 15.5 %shard_map.149 = (f32[2,256,16,1280]{3,2,1,0:T(8,128)}, bf16[2,3,256,1280]{3,2,1,0:T(8,128)(2,1)}, bf16[128,1280]{1,0:T(8,128)(2,1)S(1)}, bf16[128,1280]{1,0:T(8...) custom-call(f32[256,16,1280]{2,1,0:T(8,128)S(1)} %get-tuple-element.27.st, ...), custom_call_target="tpu_custom_call" | custom-call | flops 20000000000 | bytes 44040192 | tf_op jit(solution)/shard_map/pallas_call | solution.py:512
  51.4 0.0 collective-permute-done.refs_2_
  51.4 28.2 %shard_map.150 = (f32[256,16,1280]{2,1,0:T(8,128)S(1)}, bf16[3,128,1280]{2,1,0:T(8,128)(2,1)S(1)}, bf16[128,1280]{1,0:T(8,128)(2,1)S(1)}, bf16[128,1280]{1,0:T(8...) custom-call(f32[256,2560]{1,0:T(8,128)} %refs_0_.3, ...), custom_call_target="tpu_custom_call" | custom-call | flops 20000000000 | bytes 48234496 | tf_op jit(solution)/shard_map/pallas_call | solution.py:423
  79.6 0.9 collective-permute-start.2
  80.5 0.0 collective-permute-start.1
  80.5 9.1 %collective-permute-done.2.refs_6_ = bf16[128,1280]{1,0:T(8,128)(2,1)S(1)} collective-permute-done((bf16[128,1280]{1,0:T(8,128)(2,1)S(1)}, bf16[128,1280]{1,0:T(8,128)(2,1)S(1)}, u32[]{:S(2)}, u32[]{:S(2)}) %collective-permute-start.2) | collective-permute-done | bytes 327712 | tf_op jit(solution)/shard_map/ppermute | solution.py:590
  89.6 0.0 collective-permute-start.3
  89.6 0.0 copy-start
  89.6 0.0 copy-start.1
  89.6 8.2 %shard_map.151 = (f32[2,256,16,1280]{3,2,1,0:T(8,128)}, bf16[2,3,256,1280]{3,2,1,0:T(8,128)(2,1)}) custom-call(f32[256,16,1280]{2,1,0:T(8,128)S(1)} %get-tuple-element.44.st, bf16[3,128,1280]{2,1,0:T(8,128)(2,1)S(1)} %get-tuple-element.45.cw_a, bf16[3,128,1280]{2,1,0:T(8,128)(2,1)S(1)} %get-tuple-element.46.cw_b, ...), custom_call_target="tpu_custom_call", output_to_operand_aliasing={{0}: (3, {}), {1}: (4, {})} | custom-call | flops 20000000000 | bytes 44040192 | tf_op jit(solution)/shard_map/pallas_call | solution.py:544
  97.8 0.0 collective-permute-done.1.refs_5_
  97.8 0.0 collective-permute-done.3.refs_7_
  97.8 0.0 copy-done
  97.8 0.0 copy-done.1
  97.9 1.9 %fin.1 = f32[256,2560]{1,0:T(8,128)} custom-call(f32[128,2560]{1,0:T(8,128)S(1)} %copy-done, f32[128,2560]{1,0:T(8,128)S(1)} %copy-done.1, bf16[128,1280]{1,0:T(8,128)(2,1)S(1)} %get-tuple-element.39.refs_0_, bf16[128,1280]{1,0:T(8,128)(2,1)S(1)} %get-tuple-element.40.refs_1_, bf16[128,1280]{1,0:T(8,128)(2,1)S(1)} %get-tuple-element.41.refs_2_, ...), custom_call_target="tpu_custom_call" | custom-call | tf_op jit(solution)/shard_map/fin/pallas_call | solution.py:569
Async XLA Ops:
  35.5 15.9 %collective-permute-start = (bf16[128,1280]{1,0:T(8,128)(2,1)S(1)}, bf16[128,1280]{1,0:T(8,128)(2,1)S(1)}, u32[]{:S(2)}, u32[]{:S(2)}) collective-permute-start(bf16[128,1280]{1,0:T(8,128)(2,1)S(1)} %get-tuple-element.34.refs_1_), channel_id=1, source_target_pairs={{0,2},{2,0},{1,3},{3,1},{4,6},{6,4},{5,7},{7,5}} | collective-permute-start | bytes 983048 | tf_op jit(solution)/shard_map/ppermute | solution.py:586
  79.6 10.0 %collective-permute-start.2 = (bf16[128,1280]{1,0:T(8,128)(2,1)S(1)}, bf16[128,1280]{1,0:T(8,128)(2,1)S(1)}, u32[]{:S(2)}, u32[]{:S(2)}) collective-permute-start(bf16[128,1280]{1,0:T(8,128)(2,1)S(1)} %get-tuple-element.43.refs_4_), channel_id=1, source_target_pairs={{0,2},{2,0},{1,3},{3,1},{4,6},{6,4},{5,7},{7,5}} | collective-permute-start | bytes 983048 | tf_op jit(solution)/shard_map/ppermute | solution.py:590
  80.5 17.3 %collective-permute-start.1 = (bf16[128,1280]{1,0:T(8,128)(2,1)S(1)}, bf16[128,1280]{1,0:T(8,128)(2,1)S(1)}, u32[]{:S(2)}, u32[]{:S(2)}) collective-permute-start(bf16[128,1280]{1,0:T(8,128)(2,1)S(1)} %get-tuple-element.43.refs_4_), channel_id=1, source_target_pairs={{0,1},{1,0},{2,3},{3,2},{4,5},{5,4},{6,7},{7,6}} | collective-permute-start | bytes 983048 | tf_op jit(solution)/shard_map/ppermute | solution.py:591
  89.6 8.2 %collective-permute-start.3 = (bf16[128,1280]{1,0:T(8,128)(2,1)S(1)}, bf16[128,1280]{1,0:T(8,128)(2,1)S(1)}, u32[]{:S(2)}, u32[]{:S(2)}) collective-permute-start(bf16[128,1280]{1,0:T(8,128)(2,1)S(1)} %collective-permute-done.2.refs_6_), channel_id=1, source_target_pairs={{0,1},{1,0},{2,3},{3,2},{4,5},{5,4},{6,7},{7,6}} | collective-permute-start | bytes 983048 | tf_op jit(solution)/shard_map/ppermute | solution.py:593
  89.6 8.2 %copy-start = (f32[128,2560]{1,0:T(8,128)S(1)}, f32[128,2560]{1,0:T(8,128)}, u32[]{:S(2)}) copy-start(f32[128,2560]{1,0:T(8,128)} %get-tuple-element.33.r_a) | copy-start | bytes 3932164
  89.6 8.2 %copy-start.1 = (f32[128,2560]{1,0:T(8,128)S(1)}, f32[128,2560]{1,0:T(8,128)}, u32[]{:S(2)}) copy-start(f32[128,2560]{1,0:T(8,128)} %get-tuple-element.38.r_b) | copy-start | bytes 3932164
